TPU v7x, 512 devices: a whole 4x8x8 slice. The times are simulated.
512 devices in a mesh: row: 64 (over y, z_hi, core), col: 8 (over z_lo, x).
Axes of the slice: x: 4, y: 8, z: 8 (z_hi: 4, z_lo: 2; z = z_hi * 2 + z_lo), core: 2. Of those that a mesh axis runs over, the one named last changes fastest.
Arguments:
- stiffness: bfloat16 [512, 768, 768], P(('row', 'col'))
- local_inverse: bfloat16 [512, 768, 768], P(('row', 'col'))
- averaging_basis: bfloat16 [512, 768, 64], P(('row', 'col')), may hold values from -0.4375 to 0.4375
- loads: bfloat16 [512, 768, 128], P(('row', 'col')), may hold values from -6 to 6
- start: float32 [98304, 128], P(('row', 'col')), may hold values from -6 to 6
- coarse_inverse: float32 [64, 8, 24, 12288], P(None, 'col', None, 'row')
- sizes: int32 [512], P(('row', 'col')), may hold values from 384 to 768, as said below
- dof_ids: int32 [512, 768], P(('row', 'col')), may hold values from 0 to 98303, as said below
- coarse_ids: int32 [512, 64], P(('row', 'col')), may hold values from 0 to 12287, as said below
Outputs:
- solution_field: float32 [98304, 128], P(('row', 'col'))
- residual: float32 [98304, 128], P(('row', 'col'))
Inputs may be any that keep to these rules, and one draw needn't show every extreme that they name: `sizes`: the largest interface order, 768, occurs in every draw. `dof_ids`: subdomain s sits at row s // 8 and column s % 8; global interface dof g is owned by subdomain g // 192. The 768 slots of a subdomain hold distinct dofs, each owned by the subdomain itself or a subdomain at most one row and one column away; slots from sizes[s] on are not used. `coarse_ids`: coarse dof k is owned by subdomain k // 24. The 64 coarse dofs of a subdomain are distinct, each owned by the subdomain itself or a subdomain at most one row and one column away.
All inputs are finite; a program needn't handle non-finite values.
Results may differ from a plain program's by a relative error of at most 0.0064.
Values may be sent and summed in bfloat16 or wider, within the bound.
No kernel may reach another device: no remote copies, remote signals or barrier semaphores. Data moves between devices by JAX's collectives and lax.ppermute only.
A program may use at most 64 MiB of HBM per device.

v0:
```python
import jax
import jax.numpy as jnp
from jax import lax
from jax.sharding import PartitionSpec as P

ITERS = 2


HIGHEST_PRECISION = lax.Precision.HIGHEST


def extended(cells, sides, width):
    for axis, dim in sides:
        count = lax.axis_size(axis)
        ends = count - 1
        head = lax.slice_in_dim(cells, 0, width, axis=dim)
        tail = lax.slice_in_dim(cells, cells.shape[dim] - width, cells.shape[dim], axis=dim)
        cells = jnp.concatenate(
            [
                lax.ppermute(tail, axis, [(i, (i + 1) % count) for i in range(ends)]),
                cells,
                lax.ppermute(head, axis, [((i + 1) % count, i) for i in range(ends)]),
            ],
            axis=dim,
        )
    return cells


def from_everyone(array, axis):
    devices = lax.axis_size(axis)
    return lax.all_to_all(
        jnp.broadcast_to(array[None], (devices, *array.shape)), axis, 0, 0, tiled=True
    )


def joined_along(blocks, dim):
    blocks = jnp.moveaxis(blocks, 0, dim)
    lengths = blocks.shape
    return blocks.reshape(*lengths[:dim], lengths[dim] * lengths[dim + 1], *lengths[dim + 2 :])


def gather_directly(array, axis, dim):
    blocks = from_everyone(array, axis)
    return joined_along(blocks, dim)


def over_copies(array, axis):
    return from_everyone(array, axis).sum(axis=0)


def window_positions(wanted, per_owner):
    members = lax.axis_size("col")
    owner = wanted // per_owner
    row_step = owner // members - lax.axis_index("row") + 1
    col_step = owner % members - lax.axis_index("col") + 1
    return (row_step * 3 + col_step) * per_owner + wanted % per_owner


def row_positions(wanted, per_row):
    row_step = wanted // per_row - lax.axis_index("row") + 1
    return row_step * per_row + wanted % per_row


def take_rows(window_rows, positions, active):
    picked = jnp.take(window_rows, positions, axis=0, mode="clip")
    keep = active.reshape(active.shape + (1,) * (picked.ndim - 1))
    return jnp.where(keep, picked, jnp.zeros_like(picked))


def to_owners(blocks):
    across = extended(blocks[:, ::2], (("col", 1),), 1)
    middle = blocks[:, 1] + across[:, 0] + across[:, 3]
    downward = extended(middle[::2], (("row", 0),), 1)
    return middle[1] + downward[0] + downward[3]


def owned_window(owned):
    wide = extended(owned[None, None], (("row", 0), ("col", 1)), 1)
    return wide.reshape((-1,) + owned.shape[1:])


def spread_back(positions, active, values, per_owner):
    window_size = 9 * per_owner
    target = jnp.where(active, positions, window_size)
    summed = jax.ops.segment_sum(values, target, num_segments=window_size + 1)[:window_size]
    return to_owners(summed.reshape((3, 3, per_owner) + values.shape[1:]))


def body(
    stiffness,
    local_inverse,
    averaging_basis,
    loads,
    start,
    coarse_inverse,
    sizes,
    dof_ids,
    coarse_ids,
):
    per_owner = start.shape[0]
    per_coarse = coarse_inverse.shape[2]
    order_local = dof_ids.shape[1]
    active = jnp.arange(order_local, dtype=jnp.int32) < sizes[0]
    active_float = active.astype(jnp.float32)
    positions = window_positions(dof_ids[0], per_owner)
    every_primal = jnp.ones((coarse_ids.shape[1],), dtype=bool)
    coarse_positions = window_positions(coarse_ids[0], per_coarse)
    out_positions = row_positions(coarse_ids[0], per_coarse * lax.axis_size("col"))
    count_owned = spread_back(positions, active, active_float, per_owner)
    count_local = jnp.take(owned_window(count_owned), positions, axis=0, mode="clip")
    weight = active_float / (count_local + 1.0 - active_float)
    panel = coarse_inverse.reshape(-1, coarse_inverse.shape[3])
    solution_field = start
    residual = start
    for repeat in range(ITERS):
        iterate_half = solution_field.astype(jnp.bfloat16)
        nearby = extended(iterate_half[None, None], (("row", 0), ("col", 1)), 1)
        local_iterate = take_rows(nearby.reshape(-1, nearby.shape[3]), positions, active)
        image = jnp.dot(stiffness[0], local_iterate, preferred_element_type=jnp.float32)
        residual = spread_back(positions, active, loads[0].astype(jnp.float32) - image, per_owner)
        scaled = (weight[:, None] * take_rows(owned_window(residual), positions, active)).astype(
            jnp.bfloat16
        )
        local_part = jnp.dot(local_inverse[0], scaled, preferred_element_type=jnp.float32)
        primal = lax.dot_general(
            averaging_basis[0], scaled, (((0,), (0,)), ((), ())), preferred_element_type=jnp.float32
        )
        coarse_owned = spread_back(coarse_positions, every_primal, primal, per_coarse)
        coarse_part = lax.dot_general(
            panel,
            gather_directly(coarse_owned, "row", 0),
            (((0,), (0,)), ((), ())),
            precision=HIGHEST_PRECISION,
            preferred_element_type=jnp.float32,
        )
        totals = over_copies(coarse_part, "col").astype(jnp.bfloat16)
        beside_all = extended(totals[None], (("row", 0),), 1)
        coarse_local = take_rows(
            beside_all.reshape(-1, beside_all.shape[-1]), out_positions, every_primal
        )
        correction = jnp.dot(averaging_basis[0], coarse_local, preferred_element_type=jnp.float32)
        update = weight[:, None] * (local_part + correction)
        solution_field = solution_field + spread_back(positions, active, update, per_owner)
    return (solution_field, residual)


def solution(mesh):
    in_specs = (
        P(("row", "col"), None, None),
        P(("row", "col"), None, None),
        P(("row", "col"), None, None),
        P(("row", "col"), None, None),
        P(("row", "col"), None),
        P(None, "col", None, "row"),
        P(("row", "col")),
        P(("row", "col"), None),
        P(("row", "col"), None),
    )
    out_specs = (P(("row", "col"), None), P(("row", "col"), None))
    return jax.shard_map(body, mesh=mesh, in_specs=in_specs, out_specs=out_specs, check_vma=False)
```

profile of v0, /device:TPU:14, one launch (start us, length us, event | category | flops | bytes accessed | tf_op | source)
XLA Modules:
  0.0 480.4 jit_solution(1548997288690296500)
XLA Ops:
  1.7 10.3 %collective-permute-start.9 = (bf16[1,1,192,128]{3,2,1,0:T(8,128)(2,1)S(1)}, bf16[1,1,192,128]{3,2,1,0:T(8,128)(2,1)S(1)}, u32[]{:S(2)}, u32[]{:S(2)}) collective-permute-start(bf16[1,1,192,128]{3,2,1,0:T(8,128)(2,1)S(1)} %convert_bitcast_fusion.3), channel_id=1, source_target_pairs={{8,0},{16,8},{24,16},{32,24},{40,32},{48,40},{56,48},{64,56},{72,6... | collective-permute-start | bytes 147464 | tf_op jit(solution)/shard_map/ppermute | solution.py:22
  43.0 6.4 %scatter_custom_fusion.1 = f32[1729,128]{1,0:T(8,128)S(1)} fusion(s32[768]{0:T(1024)} %copy-done.11, f32[768,128]{1,0:T(8,128)S(1)} %copy.20, f32[]{:T(128)} %constant.92.clone.1), kind=kCustom, calls=%fused_computation.42 | custom fusion | flops 98304 | bytes 885760 | tf_op jit(solution)/shard_map/scatter-add | solution.py:85
  49.6 6.5 %collective-permute-start.12 = (f32[3,1,192,128]{3,2,1,0:T(8,128)S(1)}, f32[3,1,192,128]{3,2,1,0:T(8,128)S(1)}, u32[]{:S(2)}, u32[]{:S(2)}) collective-permute-start(f32[3,1,192,128]{3,2,1,0:T(8,128)S(1)} %get-tuple-element.12), channel_id=1, source_target_pairs={{0,1},{1,2},{2,3},{3,4},{4,5},{5,6},{6,7},{8,9},{9,10},{10,11},{11... | collective-permute-start | bytes 884744 | tf_op jit(solution)/shard_map/ppermute | solution.py:20
  62.0 6.7 %collective-permute-start.3 = (f32[1,192]{1,0:T(1,128)S(1)}, f32[1,192]{1,0:T(1,128)S(1)}, u32[]{:S(2)}, u32[]{:S(2)}) collective-permute-start(f32[1,192]{1,0:T(1,128)S(1)} %get-tuple-element.35), channel_id=1, source_target_pairs={{8,0},{16,8},{24,16},{32,24},{40,32},{48,40},{56,48},{64,56},{72,6... | collective-permute-start | bytes 2312 | tf_op jit(solution)/shard_map/ppermute | solution.py:22
  71.7 6.7 %collective-permute-start.15 = (f32[1,192,128]{2,1,0:T(8,128)S(1)}, f32[1,192,128]{2,1,0:T(8,128)S(1)}, u32[]{:S(2)}, u32[]{:S(2)}) collective-permute-start(f32[1,192,128]{2,1,0:T(8,128)S(1)} %get-tuple-element.23), channel_id=1, source_target_pairs={{8,0},{16,8},{24,16},{32,24},{40,32},{48,40},{56,48},{64,56},{72,6... | collective-permute-start | bytes 294920 | tf_op jit(solution)/shard_map/ppermute | solution.py:22
  82.8 6.2 %collective-permute-start.17 = (f32[1,1,192,128]{3,2,1,0:T(8,128)S(1)}, f32[1,1,192,128]{3,2,1,0:T(8,128)S(1)}, u32[]{:S(2)}, u32[]{:S(2)}) collective-permute-start(f32[1,1,192,128]{3,2,1,0:T(8,128)S(1)} %fusion.40), channel_id=1, source_target_pairs={{8,0},{16,8},{24,16},{32,24},{40,32},{48,40},{56,48},{64,56},{72,6... | collective-permute-start | bytes 294920 | tf_op jit(solution)/shard_map/ppermute | solution.py:22
  92.9 6.0 %collective-permute-start.6 = (f32[3,1,192]{2,1,0:T(1,128)S(1)}, f32[3,1,192]{2,1,0:T(1,128)S(1)}, u32[]{:S(2)}, u32[]{:S(2)}) collective-permute-start(f32[3,1,192]{2,1,0:T(1,128)S(1)} %pad_maximum_fusion.11), channel_id=1, source_target_pairs={{0,1},{1,2},{2,3},{3,4},{4,5},{5,6},{6,7},{8,9},{9,10},{10,11},{11... | collective-permute-start | bytes 6920 | tf_op jit(solution)/shard_map/ppermute | solution.py:20
  100.9 6.0 %collective-permute-start.18 = (f32[3,1,192,128]{3,2,1,0:T(8,128)S(1)}, f32[3,1,192,128]{3,2,1,0:T(8,128)}, u32[]{:S(2)}, u32[]{:S(2)}) collective-permute-start(f32[3,1,192,128]{3,2,1,0:T(8,128)S(1)} %pad_maximum_fusion.4), channel_id=1, source_target_pairs={{0,1},{1,2},{2,3},{3,4},{4,5},{5,6},{6,7},{8,9},{9,10},{10,11},{11... | collective-permute-start | bytes 884744 | tf_op jit(solution)/shard_map/ppermute | solution.py:20
  115.6 6.2 %collective-permute-start.20 = (f32[3,1,24,128]{3,2,1,0:T(8,128)S(1)}, f32[3,1,24,128]{3,2,1,0:T(8,128)S(1)}, u32[]{:S(2)}, u32[]{:S(2)}) collective-permute-start(f32[3,1,24,128]{3,2,1,0:T(8,128)S(1)} %get-tuple-element.26), channel_id=1, source_target_pairs={{0,1},{1,2},{2,3},{3,4},{4,5},{5,6},{6,7},{8,9},{9,10},{10,11},{11... | collective-permute-start | bytes 110600 | tf_op jit(solution)/shard_map/ppermute | solution.py:20
  131.7 6.7 %collective-permute-start.23 = (f32[1,24,128]{2,1,0:T(8,128)S(1)}, f32[1,24,128]{2,1,0:T(8,128)S(1)}, u32[]{:S(2)}, u32[]{:S(2)}) collective-permute-start(f32[1,24,128]{2,1,0:T(8,128)S(1)} %get-tuple-element.31), channel_id=1, source_target_pairs={{8,0},{16,8},{24,16},{32,24},{40,32},{48,40},{56,48},{64,56},{72,6... | collective-permute-start | bytes 36872 | tf_op jit(solution)/shard_map/ppermute | solution.py:22
  139.8 40.6 %all_to_all.20 = f32[64,24,128]{2,1,0:T(8,128)S(1)} all-to-all(f32[64,24,128]{2,1,0:T(8,128)S(1)} %broadcast_in_dim.110), channel_id=1, replica_groups=mesh['row'=64,'col'=8] {'row'}, dimensions={0} | all-to-all | bytes 1572864 | tf_op jit(solution)/shard_map/all_to_all | solution.py:31
  188.7 9.9 %all-to-all-done.1 = f32[8,192,128]{2,1,0:T(8,128)} async-done(((f32[8,192,128]{2,1,0:T(8,128)}), f32[8,192,128]{2,1,0:T(8,128)}, u32[]{:S(2)}, u32[]{:S(2)}) %all-to-all-start.1) | async-done | bytes 786464 | tf_op jit(solution)/shard_map/all_to_all | solution.py:31
  213.6 6.4 %scatter_custom_fusion.3 = f32[1729,128]{1,0:T(8,128)S(1)} fusion(s32[768]{0:T(1024)} %copy-done.11, f32[768,128]{1,0:T(8,128)S(1)} %copy.21, f32[]{:T(128)} %constant.92.clone.1), kind=kCustom, calls=%fused_computation.40 | custom fusion | flops 98304 | bytes 885760 | tf_op jit(solution)/shard_map/scatter-add | solution.py:85
  230.1 6.5 %collective-permute-done.27 = f32[3,1,192,128]{3,2,1,0:T(8,128)S(1)} collective-permute-done((f32[3,1,192,128]{3,2,1,0:T(8,128)S(1)}, f32[3,1,192,128]{3,2,1,0:T(8,128)S(1)}, u32[]{:S(2)}, u32[]{:S(2)}) %collective-permute-start.27) | collective-permute-done | bytes 294944 | tf_op jit(solution)/shard_map/ppermute | solution.py:22
  238.6 6.7 %collective-permute-start.29 = (f32[1,192,128]{2,1,0:T(8,128)S(1)}, f32[1,192,128]{2,1,0:T(8,128)S(1)}, u32[]{:S(2)}, u32[]{:S(2)}) collective-permute-start(f32[1,192,128]{2,1,0:T(8,128)S(1)} %get-tuple-element.21), channel_id=1, source_target_pairs={{8,0},{16,8},{24,16},{32,24},{40,32},{48,40},{56,48},{64,56},{72,6... | collective-permute-start | bytes 294920 | tf_op jit(solution)/shard_map/ppermute | solution.py:22
  248.1 6.7 %collective-permute-start.31 = (bf16[1,1,192,128]{3,2,1,0:T(8,128)(2,1)S(1)}, bf16[1,1,192,128]{3,2,1,0:T(8,128)(2,1)S(1)}, u32[]{:S(2)}, u32[]{:S(2)}) collective-permute-start(bf16[1,1,192,128]{3,2,1,0:T(8,128)(2,1)S(1)} %get-tuple-element.4), channel_id=1, source_target_pairs={{8,0},{16,8},{24,16},{32,24},{40,32},{48,40},{56,48},{64,56},{72,6... | collective-permute-start | bytes 147464 | tf_op jit(solution)/shard_map/ppermute | solution.py:22
  256.8 6.5 %collective-permute-done.30 = bf16[1,1,192,128]{3,2,1,0:T(8,128)(2,1)S(1)} collective-permute-done((bf16[1,1,192,128]{3,2,1,0:T(8,128)(2,1)S(1)}, bf16[1,1,192,128]{3,2,1,0:T(8,128)(2,1)S(1)}, u32[]{:S(2)}, u32[]{:S(2)}) %collective-permute-start.30) | collective-permute-done | bytes 49184 | tf_op jit(solution)/shard_map/ppermute | solution.py:20
  265.4 6.0 %collective-permute-start.32 = (bf16[3,1,192,128]{3,2,1,0:T(8,128)(2,1)S(1)}, bf16[3,1,192,128]{3,2,1,0:T(8,128)(2,1)S(1)}, u32[]{:S(2)}, u32[]{:S(2)}) collective-permute-start(bf16[3,1,192,128]{3,2,1,0:T(8,128)(2,1)S(1)} %pad_maximum_fusion.8), channel_id=1, source_target_pairs={{0,1},{1,2},{2,3},{3,4},{4,5},{5,6},{6,7},{8,9},{9,10},{10,11},{11... | collective-permute-start | bytes 442376 | tf_op jit(solution)/shard_map/ppermute | solution.py:20
  279.1 6.7 %scatter_custom_fusion.4 = f32[1729,128]{1,0:T(8,128)S(1)} fusion(s32[768]{0:T(1024)} %copy-done.11, f32[768,128]{1,0:T(8,128)} %copy.22, f32[]{:T(128)} %constant.92.clone.1), kind=kCustom, calls=%fused_computation.38 | custom fusion | flops 98304 | bytes 885760 | tf_op jit(solution)/shard_map/scatter-add | solution.py:85
  286.0 6.8 %collective-permute-start.34 = (f32[3,1,192,128]{3,2,1,0:T(8,128)S(1)}, f32[3,1,192,128]{3,2,1,0:T(8,128)S(1)}, u32[]{:S(2)}, u32[]{:S(2)}) collective-permute-start(f32[3,1,192,128]{3,2,1,0:T(8,128)S(1)} %get-tuple-element.8), channel_id=1, source_target_pairs={{0,1},{1,2},{2,3},{3,4},{4,5},{5,6},{6,7},{8,9},{9,10},{10,11},{11... | collective-permute-start | bytes 884744 | tf_op jit(solution)/shard_map/ppermute | solution.py:20
  297.0 7.6 %collective-permute-done.35 = f32[3,1,192,128]{3,2,1,0:T(8,128)S(1)} collective-permute-done((f32[3,1,192,128]{3,2,1,0:T(8,128)S(1)}, f32[3,1,192,128]{3,2,1,0:T(8,128)S(1)}, u32[]{:S(2)}, u32[]{:S(2)}) %collective-permute-start.35) | collective-permute-done | bytes 294944 | tf_op jit(solution)/shard_map/ppermute | solution.py:22
  306.6 6.7 %collective-permute-start.37 = (f32[1,192,128]{2,1,0:T(8,128)S(1)}, f32[1,192,128]{2,1,0:T(8,128)S(1)}, u32[]{:S(2)}, u32[]{:S(2)}) collective-permute-start(f32[1,192,128]{2,1,0:T(8,128)S(1)} %get-tuple-element.19), channel_id=1, source_target_pairs={{8,0},{16,8},{24,16},{32,24},{40,32},{48,40},{56,48},{64,56},{72,6... | collective-permute-start | bytes 294920 | tf_op jit(solution)/shard_map/ppermute | solution.py:22
  316.1 6.8 %collective-permute-start.39 = (f32[1,1,192,128]{3,2,1,0:T(8,128)S(1)}, f32[1,1,192,128]{3,2,1,0:T(8,128)S(1)}, u32[]{:S(2)}, u32[]{:S(2)}) collective-permute-start(f32[1,1,192,128]{3,2,1,0:T(8,128)S(1)} %get-tuple-element.15), channel_id=1, source_target_pairs={{8,0},{16,8},{24,16},{32,24},{40,32},{48,40},{56,48},{64,56},{72,6... | collective-permute-start | bytes 294920 | tf_op jit(solution)/shard_map/ppermute | solution.py:22
  325.1 6.8 %collective-permute-done.38 = f32[1,1,192,128]{3,2,1,0:T(8,128)S(1)} collective-permute-done((f32[1,1,192,128]{3,2,1,0:T(8,128)S(1)}, f32[1,1,192,128]{3,2,1,0:T(8,128)S(1)}, u32[]{:S(2)}, u32[]{:S(2)}) %collective-permute-start.38) | collective-permute-done | bytes 98336 | tf_op jit(solution)/shard_map/ppermute | solution.py:20
  347.1 6.5 %collective-permute-start.42 = (f32[3,1,24,128]{3,2,1,0:T(8,128)S(1)}, f32[3,1,24,128]{3,2,1,0:T(8,128)S(1)}, u32[]{:S(2)}, u32[]{:S(2)}) collective-permute-start(f32[3,1,24,128]{3,2,1,0:T(8,128)S(1)} %get-tuple-element.24), channel_id=1, source_target_pairs={{0,1},{1,2},{2,3},{3,4},{4,5},{5,6},{6,7},{8,9},{9,10},{10,11},{11... | collective-permute-start | bytes 110600 | tf_op jit(solution)/shard_map/ppermute | solution.py:20
  363.6 6.7 %collective-permute-start.45 = (f32[1,24,128]{2,1,0:T(8,128)S(1)}, f32[1,24,128]{2,1,0:T(8,128)S(1)}, u32[]{:S(2)}, u32[]{:S(2)}) collective-permute-start(f32[1,24,128]{2,1,0:T(8,128)S(1)} %get-tuple-element.29), channel_id=1, source_target_pairs={{8,0},{16,8},{24,16},{32,24},{40,32},{48,40},{56,48},{64,56},{72,6... | collective-permute-start | bytes 36872 | tf_op jit(solution)/shard_map/ppermute | solution.py:22
  371.7 42.4 %all_to_all.21 = f32[64,24,128]{2,1,0:T(8,128)S(1)} all-to-all(f32[64,24,128]{2,1,0:T(8,128)S(1)} %broadcast_in_dim.114), channel_id=1, replica_groups=mesh['row'=64,'col'=8] {'row'}, dimensions={0} | all-to-all | bytes 1572864 | tf_op jit(solution)/shard_map/all_to_all | solution.py:31
  416.8 14.6 %all_to_all.22 = f32[8,192,128]{2,1,0:T(8,128)} all-to-all(f32[8,192,128]{2,1,0:T(8,128)S(1)} %broadcast_in_dim.115), channel_id=1, replica_groups=mesh['row'=64,'col'=8] {'col'}, dimensions={0} | all-to-all | bytes 1572864 | tf_op jit(solution)/shard_map/all_to_all | solution.py:31
  438.4 6.1 %collective-permute-done.46 = bf16[1,192,128]{2,1,0:T(8,128)(2,1)S(1)} collective-permute-done((bf16[1,192,128]{2,1,0:T(8,128)(2,1)}, bf16[1,192,128]{2,1,0:T(8,128)(2,1)S(1)}, u32[]{:S(2)}, u32[]{:S(2)}) %collective-permute-start.46) | collective-permute-done | bytes 49184 | tf_op jit(solution)/shard_map/ppermute | solution.py:20
  447.4 6.4 %scatter_custom_fusion.6 = f32[1729,128]{1,0:T(8,128)S(1)} fusion(s32[768]{0:T(1024)} %copy-done.11, f32[768,128]{1,0:T(8,128)S(1)} %copy.23, f32[]{:T(128)} %constant.92.clone.1), kind=kCustom, calls=%fused_computation.36 | custom fusion | flops 98304 | bytes 885760 | tf_op jit(solution)/shard_map/scatter-add | solution.py:85
  462.7 6.1 %collective-permute-done.49 = f32[3,1,192,128]{3,2,1,0:T(8,128)S(1)} collective-permute-done((f32[3,1,192,128]{3,2,1,0:T(8,128)S(1)}, f32[3,1,192,128]{3,2,1,0:T(8,128)S(1)}, u32[]{:S(2)}, u32[]{:S(2)}) %collective-permute-start.49) | collective-permute-done | bytes 294944 | tf_op jit(solution)/shard_map/ppermute | solution.py:22
  470.8 6.7 %collective-permute-start.51 = (f32[1,192,128]{2,1,0:T(8,128)S(1)}, f32[1,192,128]{2,1,0:T(8,128)S(1)}, u32[]{:S(2)}, u32[]{:S(2)}) collective-permute-start(f32[1,192,128]{2,1,0:T(8,128)S(1)} %get-tuple-element.17), channel_id=1, source_target_pairs={{8,0},{16,8},{24,16},{32,24},{40,32},{48,40},{56,48},{64,56},{72,6... | collective-permute-start | bytes 294920 | tf_op jit(solution)/shard_map/ppermute | solution.py:22
  (208 shorter events, 184.2 us)
Async XLA Ops:
  1.7 25.0 %collective-permute-start.9 = (bf16[1,1,192,128]{3,2,1,0:T(8,128)(2,1)S(1)}, bf16[1,1,192,128]{3,2,1,0:T(8,128)(2,1)S(1)}, u32[]{:S(2)}, u32[]{:S(2)}) collective-permute-start(bf16[1,1,192,128]{3,2,1,0:T(8,128)(2,1)S(1)} %convert_bitcast_fusion.3), channel_id=1, source_target_pairs={{8,0},{16,8},{24,16},{32,24},{40,32},{48,40},{56,48},{64,56},{72,6... | collective-permute-start | bytes 147464 | tf_op jit(solution)/shard_map/ppermute | solution.py:22
  11.9 14.7 %collective-permute-start.8 = (bf16[1,1,192,128]{3,2,1,0:T(8,128)(2,1)S(1)}, bf16[1,1,192,128]{3,2,1,0:T(8,128)(2,1)S(1)}, u32[]{:S(2)}, u32[]{:S(2)}) collective-permute-start(bf16[1,1,192,128]{3,2,1,0:T(8,128)(2,1)S(1)} %convert_bitcast_fusion.3), channel_id=1, source_target_pairs={{0,8},{8,16},{16,24},{24,32},{32,40},{40,48},{48,56},{56,64},{64,7... | collective-permute-start | bytes 147464 | tf_op jit(solution)/shard_map/ppermute | solution.py:20
  20.8 37.2 %collective-permute-start = (f32[3,1,192]{2,1,0:T(1,128)}, f32[3,1,192]{2,1,0:T(1,128)}, u32[]{:S(2)}, u32[]{:S(2)}) collective-permute-start(f32[3,1,192]{2,1,0:T(1,128)} %get-tuple-element.32), channel_id=1, source_target_pairs={{0,1},{1,2},{2,3},{3,4},{4,5},{5,6},{6,7},{8,9},{9,10},{10,11},{11... | collective-permute-start | bytes 6920 | tf_op jit(solution)/shard_map/ppermute | solution.py:20
  24.3 33.7 %collective-permute-start.1 = (f32[3,1,192]{2,1,0:T(1,128)}, f32[3,1,192]{2,1,0:T(1,128)}, u32[]{:S(2)}, u32[]{:S(2)}) collective-permute-start(f32[3,1,192]{2,1,0:T(1,128)} %get-tuple-element.33), channel_id=1, source_target_pairs={{1,0},{2,1},{3,2},{4,3},{5,4},{6,5},{7,6},{9,8},{10,9},{11,10},{12... | collective-permute-start | bytes 6920 | tf_op jit(solution)/shard_map/ppermute | solution.py:22
  26.7 10.4 %collective-permute-start.11 = (bf16[3,1,192,128]{3,2,1,0:T(8,128)(2,1)S(1)}, bf16[3,1,192,128]{3,2,1,0:T(8,128)(2,1)S(1)}, u32[]{:S(2)}, u32[]{:S(2)}) collective-permute-start(bf16[3,1,192,128]{3,2,1,0:T(8,128)(2,1)S(1)} %pad_maximum_fusion.6), channel_id=1, source_target_pairs={{1,0},{2,1},{3,2},{4,3},{5,4},{6,5},{7,6},{9,8},{10,9},{11,10},{12... | collective-permute-start | bytes 442376 | tf_op jit(solution)/shard_map/ppermute | solution.py:22
  49.6 19.1 %collective-permute-start.12 = (f32[3,1,192,128]{3,2,1,0:T(8,128)S(1)}, f32[3,1,192,128]{3,2,1,0:T(8,128)S(1)}, u32[]{:S(2)}, u32[]{:S(2)}) collective-permute-start(f32[3,1,192,128]{3,2,1,0:T(8,128)S(1)} %get-tuple-element.12), channel_id=1, source_target_pairs={{0,1},{1,2},{2,3},{3,4},{4,5},{5,6},{6,7},{8,9},{9,10},{10,11},{11... | collective-permute-start | bytes 884744 | tf_op jit(solution)/shard_map/ppermute | solution.py:20
  56.1 12.6 %collective-permute-start.13 = (f32[3,1,192,128]{3,2,1,0:T(8,128)S(1)}, f32[3,1,192,128]{3,2,1,0:T(8,128)}, u32[]{:S(2)}, u32[]{:S(2)}) collective-permute-start(f32[3,1,192,128]{3,2,1,0:T(8,128)S(1)} %get-tuple-element.13), channel_id=1, source_target_pairs={{1,0},{2,1},{3,2},{4,3},{5,4},{6,5},{7,6},{9,8},{10,9},{11,10},{12... | collective-permute-start | bytes 884744 | tf_op jit(solution)/shard_map/ppermute | solution.py:22
  60.1 18.2 %collective-permute-start.2 = (f32[1,192]{1,0:T(1,128)S(1)}, f32[1,192]{1,0:T(1,128)S(1)}, u32[]{:S(2)}, u32[]{:S(2)}) collective-permute-start(f32[1,192]{1,0:T(1,128)S(1)} %get-tuple-element.34), channel_id=1, source_target_pairs={{0,8},{8,16},{16,24},{24,32},{32,40},{40,48},{48,56},{56,64},{64,7... | collective-permute-start | bytes 2312 | tf_op jit(solution)/shard_map/ppermute | solution.py:20
  62.0 16.3 %collective-permute-start.3 = (f32[1,192]{1,0:T(1,128)S(1)}, f32[1,192]{1,0:T(1,128)S(1)}, u32[]{:S(2)}, u32[]{:S(2)}) collective-permute-start(f32[1,192]{1,0:T(1,128)S(1)} %get-tuple-element.35), channel_id=1, source_target_pairs={{8,0},{16,8},{24,16},{32,24},{40,32},{48,40},{56,48},{64,56},{72,6... | collective-permute-start | bytes 2312 | tf_op jit(solution)/shard_map/ppermute | solution.py:22
  69.8 13.0 %collective-permute-start.14 = (f32[1,192,128]{2,1,0:T(8,128)S(1)}, f32[1,192,128]{2,1,0:T(8,128)S(1)}, u32[]{:S(2)}, u32[]{:S(2)}) collective-permute-start(f32[1,192,128]{2,1,0:T(8,128)S(1)} %get-tuple-element.22), channel_id=1, source_target_pairs={{0,8},{8,16},{16,24},{24,32},{32,40},{40,48},{48,56},{56,64},{64,7... | collective-permute-start | bytes 294920 | tf_op jit(solution)/shard_map/ppermute | solution.py:20
  71.7 11.0 %collective-permute-start.15 = (f32[1,192,128]{2,1,0:T(8,128)S(1)}, f32[1,192,128]{2,1,0:T(8,128)S(1)}, u32[]{:S(2)}, u32[]{:S(2)}) collective-permute-start(f32[1,192,128]{2,1,0:T(8,128)S(1)} %get-tuple-element.23), channel_id=1, source_target_pairs={{8,0},{16,8},{24,16},{32,24},{40,32},{48,40},{56,48},{64,56},{72,6... | collective-permute-start | bytes 294920 | tf_op jit(solution)/shard_map/ppermute | solution.py:22
  78.4 12.5 %collective-permute-start.5 = (f32[1,1,192]{2,1,0:T(1,128)S(1)}, f32[1,1,192]{2,1,0:T(1,128)S(1)}, u32[]{:S(2)}, u32[]{:S(2)}) collective-permute-start(f32[1,1,192]{2,1,0:T(1,128)S(1)} %fusion.72), channel_id=1, source_target_pairs={{8,0},{16,8},{24,16},{32,24},{40,32},{48,40},{56,48},{64,56},{72,6... | collective-permute-start | bytes 2312 | tf_op jit(solution)/shard_map/ppermute | solution.py:22
  80.3 10.6 %collective-permute-start.4 = (f32[1,1,192]{2,1,0:T(1,128)S(1)}, f32[1,1,192]{2,1,0:T(1,128)S(1)}, u32[]{:S(2)}, u32[]{:S(2)}) collective-permute-start(f32[1,1,192]{2,1,0:T(1,128)S(1)} %fusion.72), channel_id=1, source_target_pairs={{0,8},{8,16},{16,24},{24,32},{32,40},{40,48},{48,56},{56,64},{64,7... | collective-permute-start | bytes 2312 | tf_op jit(solution)/shard_map/ppermute | solution.py:20
  82.8 16.1 %collective-permute-start.17 = (f32[1,1,192,128]{3,2,1,0:T(8,128)S(1)}, f32[1,1,192,128]{3,2,1,0:T(8,128)S(1)}, u32[]{:S(2)}, u32[]{:S(2)}) collective-permute-start(f32[1,1,192,128]{3,2,1,0:T(8,128)S(1)} %fusion.40), channel_id=1, source_target_pairs={{8,0},{16,8},{24,16},{32,24},{40,32},{48,40},{56,48},{64,56},{72,6... | collective-permute-start | bytes 294920 | tf_op jit(solution)/shard_map/ppermute | solution.py:22
  89.0 9.9 %collective-permute-start.16 = (f32[1,1,192,128]{3,2,1,0:T(8,128)S(1)}, f32[1,1,192,128]{3,2,1,0:T(8,128)S(1)}, u32[]{:S(2)}, u32[]{:S(2)}) collective-permute-start(f32[1,1,192,128]{3,2,1,0:T(8,128)S(1)} %fusion.40), channel_id=1, source_target_pairs={{0,8},{8,16},{16,24},{24,32},{32,40},{40,48},{48,56},{56,64},{64,7... | collective-permute-start | bytes 294920 | tf_op jit(solution)/shard_map/ppermute | solution.py:20
  90.9 16.0 %collective-permute-start.7 = (f32[3,1,192]{2,1,0:T(1,128)S(1)}, f32[3,1,192]{2,1,0:T(1,128)S(1)}, u32[]{:S(2)}, u32[]{:S(2)}) collective-permute-start(f32[3,1,192]{2,1,0:T(1,128)S(1)} %pad_maximum_fusion.11), channel_id=1, source_target_pairs={{1,0},{2,1},{3,2},{4,3},{5,4},{6,5},{7,6},{9,8},{10,9},{11,10},{12... | collective-permute-start | bytes 6920 | tf_op jit(solution)/shard_map/ppermute | solution.py:22
  92.9 14.1 %collective-permute-start.6 = (f32[3,1,192]{2,1,0:T(1,128)S(1)}, f32[3,1,192]{2,1,0:T(1,128)S(1)}, u32[]{:S(2)}, u32[]{:S(2)}) collective-permute-start(f32[3,1,192]{2,1,0:T(1,128)S(1)} %pad_maximum_fusion.11), channel_id=1, source_target_pairs={{0,1},{1,2},{2,3},{3,4},{4,5},{5,6},{6,7},{8,9},{9,10},{10,11},{11... | collective-permute-start | bytes 6920 | tf_op jit(solution)/shard_map/ppermute | solution.py:20
  98.9 12.6 %collective-permute-start.19 = (f32[3,1,192,128]{3,2,1,0:T(8,128)S(1)}, f32[3,1,192,128]{3,2,1,0:T(8,128)S(1)}, u32[]{:S(2)}, u32[]{:S(2)}) collective-permute-start(f32[3,1,192,128]{3,2,1,0:T(8,128)S(1)} %pad_maximum_fusion.4), channel_id=1, source_target_pairs={{1,0},{2,1},{3,2},{4,3},{5,4},{6,5},{7,6},{9,8},{10,9},{11,10},{12... | collective-permute-start | bytes 884744 | tf_op jit(solution)/shard_map/ppermute | solution.py:22
  100.9 10.7 %collective-permute-start.18 = (f32[3,1,192,128]{3,2,1,0:T(8,128)S(1)}, f32[3,1,192,128]{3,2,1,0:T(8,128)}, u32[]{:S(2)}, u32[]{:S(2)}) collective-permute-start(f32[3,1,192,128]{3,2,1,0:T(8,128)S(1)} %pad_maximum_fusion.4), channel_id=1, source_target_pairs={{0,1},{1,2},{2,3},{3,4},{4,5},{5,6},{6,7},{8,9},{9,10},{10,11},{11... | collective-permute-start | bytes 884744 | tf_op jit(solution)/shard_map/ppermute | solution.py:20
  184.1 14.6 %all-to-all-start.1 = ((f32[8,192,128]{2,1,0:T(8,128)}), f32[8,192,128]{2,1,0:T(8,128)}, u32[]{:S(2)}, u32[]{:S(2)}) async-start(f32[8,192,128]{2,1,0:T(8,128)} %broadcast_in_dim.111), calls=%async_computation.1 | async-start | bytes 1572864 | tf_op jit(solution)/shard_map/all_to_all | solution.py:31
  220.2 9.8 %collective-permute-start.26 = (f32[3,1,192,128]{3,2,1,0:T(8,128)S(1)}, f32[3,1,192,128]{3,2,1,0:T(8,128)S(1)}, u32[]{:S(2)}, u32[]{:S(2)}) collective-permute-start(f32[3,1,192,128]{3,2,1,0:T(8,128)S(1)} %get-tuple-element.10), channel_id=1, source_target_pairs={{0,1},{1,2},{2,3},{3,4},{4,5},{5,6},{6,7},{8,9},{9,10},{10,11},{11... | collective-permute-start | bytes 884744 | tf_op jit(solution)/shard_map/ppermute | solution.py:20
  225.8 10.7 %collective-permute-start.27 = (f32[3,1,192,128]{3,2,1,0:T(8,128)S(1)}, f32[3,1,192,128]{3,2,1,0:T(8,128)S(1)}, u32[]{:S(2)}, u32[]{:S(2)}) collective-permute-start(f32[3,1,192,128]{3,2,1,0:T(8,128)S(1)} %get-tuple-element.11), channel_id=1, source_target_pairs={{1,0},{2,1},{3,2},{4,3},{5,4},{6,5},{7,6},{9,8},{10,9},{11,10},{12... | collective-permute-start | bytes 884744 | tf_op jit(solution)/shard_map/ppermute | solution.py:22
  236.7 8.9 %collective-permute-start.28 = (f32[1,192,128]{2,1,0:T(8,128)S(1)}, f32[1,192,128]{2,1,0:T(8,128)S(1)}, u32[]{:S(2)}, u32[]{:S(2)}) collective-permute-start(f32[1,192,128]{2,1,0:T(8,128)S(1)} %get-tuple-element.20), channel_id=1, source_target_pairs={{0,8},{8,16},{16,24},{24,32},{32,40},{40,48},{48,56},{56,64},{64,7... | collective-permute-start | bytes 294920 | tf_op jit(solution)/shard_map/ppermute | solution.py:20
  263.3 9.3 %collective-permute-start.33 = (bf16[3,1,192,128]{3,2,1,0:T(8,128)(2,1)S(1)}, bf16[3,1,192,128]{3,2,1,0:T(8,128)(2,1)S(1)}, u32[]{:S(2)}, u32[]{:S(2)}) collective-permute-start(bf16[3,1,192,128]{3,2,1,0:T(8,128)(2,1)S(1)} %pad_maximum_fusion.8), channel_id=1, source_target_pairs={{1,0},{2,1},{3,2},{4,3},{5,4},{6,5},{7,6},{9,8},{10,9},{11,10},{12... | collective-permute-start | bytes 442376 | tf_op jit(solution)/shard_map/ppermute | solution.py:22
  286.0 11.0 %collective-permute-start.34 = (f32[3,1,192,128]{3,2,1,0:T(8,128)S(1)}, f32[3,1,192,128]{3,2,1,0:T(8,128)S(1)}, u32[]{:S(2)}, u32[]{:S(2)}) collective-permute-start(f32[3,1,192,128]{3,2,1,0:T(8,128)S(1)} %get-tuple-element.8), channel_id=1, source_target_pairs={{0,1},{1,2},{2,3},{3,4},{4,5},{5,6},{6,7},{8,9},{9,10},{10,11},{11... | collective-permute-start | bytes 884744 | tf_op jit(solution)/shard_map/ppermute | solution.py:20
  292.8 11.8 %collective-permute-start.35 = (f32[3,1,192,128]{3,2,1,0:T(8,128)S(1)}, f32[3,1,192,128]{3,2,1,0:T(8,128)S(1)}, u32[]{:S(2)}, u32[]{:S(2)}) collective-permute-start(f32[3,1,192,128]{3,2,1,0:T(8,128)S(1)} %get-tuple-element.9), channel_id=1, source_target_pairs={{1,0},{2,1},{3,2},{4,3},{5,4},{6,5},{7,6},{9,8},{10,9},{11,10},{12... | collective-permute-start | bytes 884744 | tf_op jit(solution)/shard_map/ppermute | solution.py:22
  316.1 9.0 %collective-permute-start.39 = (f32[1,1,192,128]{3,2,1,0:T(8,128)S(1)}, f32[1,1,192,128]{3,2,1,0:T(8,128)S(1)}, u32[]{:S(2)}, u32[]{:S(2)}) collective-permute-start(f32[1,1,192,128]{3,2,1,0:T(8,128)S(1)} %get-tuple-element.15), channel_id=1, source_target_pairs={{8,0},{16,8},{24,16},{32,24},{40,32},{48,40},{56,48},{64,56},{72,6... | collective-permute-start | bytes 294920 | tf_op jit(solution)/shard_map/ppermute | solution.py:22
  331.9 10.7 %collective-permute-start.41 = (f32[3,1,192,128]{3,2,1,0:T(8,128)S(1)}, f32[3,1,192,128]{3,2,1,0:T(8,128)S(1)}, u32[]{:S(2)}, u32[]{:S(2)}) collective-permute-start(f32[3,1,192,128]{3,2,1,0:T(8,128)S(1)} %pad_maximum_fusion.5), channel_id=1, source_target_pairs={{1,0},{2,1},{3,2},{4,3},{5,4},{6,5},{7,6},{9,8},{10,9},{11,10},{12... | collective-permute-start | bytes 884744 | tf_op jit(solution)/shard_map/ppermute | solution.py:22
  333.8 10.3 %collective-permute-start.40 = (f32[3,1,192,128]{3,2,1,0:T(8,128)S(1)}, f32[3,1,192,128]{3,2,1,0:T(8,128)S(1)}, u32[]{:S(2)}, u32[]{:S(2)}) collective-permute-start(f32[3,1,192,128]{3,2,1,0:T(8,128)S(1)} %pad_maximum_fusion.5), channel_id=1, source_target_pairs={{0,1},{1,2},{2,3},{3,4},{4,5},{5,6},{6,7},{8,9},{9,10},{10,11},{11... | collective-permute-start | bytes 884744 | tf_op jit(solution)/shard_map/ppermute | solution.py:20
  435.4 9.1 %collective-permute-start.46 = (bf16[1,192,128]{2,1,0:T(8,128)(2,1)}, bf16[1,192,128]{2,1,0:T(8,128)(2,1)S(1)}, u32[]{:S(2)}, u32[]{:S(2)}) collective-permute-start(bf16[1,192,128]{2,1,0:T(8,128)(2,1)} %bitcast.217), channel_id=1, source_target_pairs={{0,8},{8,16},{16,24},{24,32},{32,40},{40,48},{48,56},{56,64},{64,7... | collective-permute-start | bytes 147464 | tf_op jit(solution)/shard_map/ppermute | solution.py:20
  458.1 10.7 %collective-permute-start.49 = (f32[3,1,192,128]{3,2,1,0:T(8,128)S(1)}, f32[3,1,192,128]{3,2,1,0:T(8,128)S(1)}, u32[]{:S(2)}, u32[]{:S(2)}) collective-permute-start(f32[3,1,192,128]{3,2,1,0:T(8,128)S(1)} %get-tuple-element.7), channel_id=1, source_target_pairs={{1,0},{2,1},{3,2},{4,3},{5,4},{6,5},{7,6},{9,8},{10,9},{11,10},{12... | collective-permute-start | bytes 884744 | tf_op jit(solution)/shard_map/ppermute | solution.py:22
  468.9 8.9 %collective-permute-start.50 = (f32[1,192,128]{2,1,0:T(8,128)S(1)}, f32[1,192,128]{2,1,0:T(8,128)S(1)}, u32[]{:S(2)}, u32[]{:S(2)}) collective-permute-start(f32[1,192,128]{2,1,0:T(8,128)S(1)} %get-tuple-element.16), channel_id=1, source_target_pairs={{0,8},{8,16},{16,24},{24,32},{32,40},{40,48},{48,56},{56,64},{64,7... | collective-permute-start | bytes 294920 | tf_op jit(solution)/shard_map/ppermute | solution.py:20
  (34 other events, 531.7 us)
where the time goes:
time: 484 us; the launch traced here: 480 us
  starting transfers between devices  209 us (43%)
  blocking collectives  97.6 us (20%)
  waiting for transfers between devices  90.4 us (19%)
  other arithmetic  45.8 us (9%)
  local copies, waits for them, and re-layouts  21.2 us (4%)
  matrix products  14 us (3%)
    ppermute x26, starting transfers between devices, extended(): lax.ppermute(head, axis, [((i + 1) % count, i) for i in range(ends)])  108 us
    all_to_all x3, blocking collectives, from_everyone(): lax.all_to_all(jnp.broadcast_to(array[None], (devices, *array.shape)), ax...  97.6 us
    ppermute x26, starting transfers between devices, extended(): lax.ppermute(tail, axis, [(i, (i + 1) % count) for i in range(ends)])  95.7 us
    ppermute x26, waiting for transfers between devices, extended(): lax.ppermute(head, axis, [((i + 1) % count, i) for i in range(ends)])  44.7 us
    ppermute x26, waiting for transfers between devices, extended(): lax.ppermute(tail, axis, [(i, (i + 1) % count) for i in range(ends)])  35.8 us
    scatter-add x7, other arithmetic, spread_back(): jax.ops.segment_sum(values, target, num_segments=window_size + 1)  32.7 us
    all_to_all x1, waiting for transfers between devices, from_everyone(): lax.all_to_all(jnp.broadcast_to(array[None], (devices, *array.shape)), ax...  9.94 us
  transfers between devices with their start and end apart: 53, of which 26 were waited for; matrix products, arithmetic and copies ran while one was open for 6% of the time, Pallas kernels for 0%

commit v1 on v0

v1 whole, which is shorter than its diff:
```python
import jax
import jax.numpy as jnp
from jax import lax
from jax.experimental import pallas as pl
from jax.experimental.pallas import tpu as pltpu
from jax.sharding import PartitionSpec as P

ITERS = 2
LANES = 128
F32 = jnp.float32
BF16 = jnp.bfloat16
RES_A, RES_M, RES_B, RES_H = BF16, F32, F32, F32
COARSE_A, COARSE_M = BF16, F32
UPD_A, UPD_M, UPD_B = BF16, F32, F32
RHS_1, RHS_2, PART = BF16, BF16, F32


def dot(a, b):
    return jnp.dot(a, b, preferred_element_type=F32)


def call(kernel, outs, *args):
    return pl.pallas_call(
        kernel,
        out_shape=tuple(jax.ShapeDtypeStruct(s, d) for s, d in outs),
        compiler_params=pltpu.CompilerParams(vmem_limit_bytes=48 * 1024 * 1024),
    )(*args)


def window_positions(wanted, per_owner):
    members = lax.axis_size("col")
    owner = wanted // per_owner
    row_step = owner // members - lax.axis_index("row") + 1
    col_step = owner % members - lax.axis_index("col") + 1
    return row_step, col_step, wanted % per_owner


def pair(to_next, to_previous, axis):
    count = lax.axis_size(axis)
    from_previous = lax.ppermute(to_next, axis, [(i, i + 1) for i in range(count - 1)])
    from_next = lax.ppermute(to_previous, axis, [(i + 1, i) for i in range(count - 1)])
    return from_previous, from_next


def from_everyone(block, groups):
    copies = jnp.broadcast_to(block[None], (len(groups[0]), *block.shape))
    return lax.all_to_all(copies, "row", 0, 0, axis_index_groups=groups, tiled=True)


def wide(a):
    return a.astype(F32)


def sum_cols(left, middle, right):
    from_previous, from_next = pair(right, left, "col")
    return wide(middle) + wide(from_previous) + wide(from_next)


def sum_rows(summed, kind):
    third = summed.shape[0] // 3
    up, own, down = summed[:third], summed[third : 2 * third], summed[2 * third :]
    from_previous, from_next = pair(down.astype(kind), up.astype(kind), "row")
    return own + wide(from_previous) + wide(from_next)


def spread(owned):
    from_previous, from_next = pair(owned, owned, "row")
    column = jnp.concatenate([from_previous, owned, from_next], axis=0)
    left, right = pair(column, column, "col")
    return left, column, right


def prepare_kernel(pos_col, pos_row, coarse_col, coarse_row, out_col, basis, g, gt, cs, og, basis_t, counts):
    slots, window = g.shape
    own = window // 9
    g[...] = (pos_col[...] == lax.broadcasted_iota(jnp.int32, (slots, window), 1)).astype(F32).astype(BF16)
    gt[...] = (pos_row[...] == lax.broadcasted_iota(jnp.int32, (window, slots), 0)).astype(F32).astype(BF16)
    cs[...] = (coarse_row[...] == lax.broadcasted_iota(jnp.int32, cs.shape, 0)).astype(F32).astype(BF16)
    og[...] = (out_col[...] == lax.broadcasted_iota(jnp.int32, og.shape, 1)).astype(F32).astype(BF16)
    basis_t[...] = wide(basis[...]).T.astype(BF16)
    lane = lax.broadcasted_iota(jnp.int32, (slots, LANES), 1)
    counts[...] = jnp.zeros_like(counts)
    pos = jnp.broadcast_to(pos_col[...], (slots, LANES))
    for block in range(9):
        for half in range(-(-own // LANES)):
            hit = pos == lane + (block * own + half * LANES)
            row = block * 8 + half
            counts[row : row + 1, :] = jnp.sum(hit.astype(F32), axis=0, keepdims=True)


def panel_kernel(panel, high, low):
    turned = panel[...].T
    top = turned.astype(BF16)
    high[...] = top
    low[...] = (turned - top.astype(F32)).astype(BF16)


def picked(g, values):
    if values.dtype == BF16:
        return dot(g, values)
    high = values.astype(BF16)
    return dot(g, high) + dot(g, (values - wide(high)).astype(BF16))


def gathered(g, left, middle, right):
    third = left.shape[0]
    return (
        picked(g[:, :third], left) + picked(g[:, third : 2 * third], middle) + picked(g[:, 2 * third :], right)
    )


def scattered(gt, values, left, middle, right):
    third = left.shape[0]
    high = values.astype(BF16)
    low = (values - wide(high)).astype(BF16)
    for k, out in enumerate((left, middle, right)):
        rows = gt[k * third : (k + 1) * third]
        placed = dot(rows, high)
        if out.dtype == F32:
            placed = placed + dot(rows, low)
        out[...] = placed.astype(out.dtype)


def residual_kernel(win_l, win_m, win_r, g, gt, stiffness, loads, out_l, out_m, out_r):
    iterate = gathered(g, win_l[...], win_m[...], win_r[...]).astype(BF16)
    terms = wide(loads[...]) - dot(stiffness[...], iterate)
    scattered(gt, terms, out_l, out_m, out_r)


def weight_kernel(counts, pos_col, weight):
    slots = pos_col.shape[0]
    own = weight_own(counts)
    lane = lax.broadcasted_iota(jnp.int32, (slots, LANES), 1)
    pos = jnp.broadcast_to(pos_col[...], (slots, LANES))
    total = jnp.zeros((slots, LANES), F32)
    for block in range(9):
        for half in range(-(-own // LANES)):
            left = own - half * LANES
            hit = pos == lane + (block * own + half * LANES)
            if left < LANES:
                hit = hit & (lane < left)
            row = block * 8 + half
            total = total + jnp.where(hit, counts[row : row + 1, :], 0.0)
    shared = jnp.sum(total, axis=1, keepdims=True)
    live = (pos_col[...] >= 0).astype(F32)
    weight[...] = jnp.broadcast_to(live / (shared + 1.0 - live), weight.shape)


def weight_own(counts):
    return OWN_OF[counts.shape[0]]


OWN_OF = {}


def primal_kernel(win_l, win_m, win_r, g, weight, basis_t, cs, scaled, out_l, out_m, out_r):
    rows = gathered(g, win_l[...], win_m[...], win_r[...])
    values = (weight[...] * rows).astype(BF16)
    scaled[...] = values
    primal = dot(basis_t[...], values)
    scattered(cs, primal, out_l, out_m, out_r)


def local_kernel(local_inverse, scaled, out):
    out[...] = dot(local_inverse[...], scaled[...])


def fold_kernel(blocks, out):
    count = blocks.shape[0]
    third = blocks.shape[1] // 3
    for row in range(-1, count + 1):
        total = None
        for k in range(max(row - 1, 0), min(row + 1, count - 1) + 1):
            part = wide(blocks[k, (row - k + 1) * third : (row - k + 2) * third, :])
            total = part if total is None else total + part
        out[(row + 1) * third : (row + 2) * third, :] = total.astype(out.dtype)


def coarse_kernel(blocks, high, low, out, rhs):
    groups = blocks.shape[0]
    third = blocks.shape[1] // 10
    for y in range(groups):
        base = y * 8 * third
        rhs[base : base + 8 * third, :] = blocks[y, third : 9 * third, :]
        if y > 0:
            first = wide(blocks[y, third : 2 * third, :]) + wide(blocks[y - 1, 9 * third :, :])
            rhs[base : base + third, :] = first.astype(rhs.dtype)
        if y + 1 < groups:
            last = wide(blocks[y, 8 * third : 9 * third, :]) + wide(blocks[y + 1, :third, :])
            rhs[base + 7 * third : base + 8 * third, :] = last.astype(rhs.dtype)
    values = rhs[...]
    top = values.astype(BF16)
    part = dot(high[...], top) + dot(low[...], top)
    if rhs.dtype == F32:
        part = part + dot(high[...], (values - wide(top)).astype(BF16))
    part = part.astype(out.dtype)
    members = out.shape[0]
    for c in range(members):
        for step in range(3):
            owner = c + step - 1
            rows = slice(step * third, (step + 1) * third)
            if 0 <= owner < members:
                out[c, rows, :] = part[owner * third : (owner + 1) * third]
            else:
                out[c, rows, :] = jnp.zeros((third, LANES), out.dtype)


def update_kernel(sol_u, sol_m, sol_d, og, basis, weight, local_part, gt, out_l, out_m, out_r):
    third = sol_u.shape[0]
    coarse = (
        dot(og[:, :third], sol_u[...])
        + dot(og[:, third : 2 * third], sol_m[...])
        + dot(og[:, 2 * third :], sol_d[...])
    ).astype(BF16)
    update = weight[...] * (local_part[...] + dot(basis[...], coarse))
    scattered(gt, update, out_l, out_m, out_r)


def body(stiffness, local_inverse, averaging_basis, loads, start, coarse_inverse, sizes, dof_ids, coarse_ids):
    own = start.shape[0]
    per_coarse = coarse_inverse.shape[2]
    slots = dof_ids.shape[1]
    primals = coarse_ids.shape[1]
    rows = lax.axis_size("row")
    members = lax.axis_size("col")
    window, coarse_window = 9 * own, 9 * per_coarse
    inner = [[8 * y + k for k in range(8)] for y in range(rows // 8)]
    outer = [[8 * y + k for y in range(rows // 8)] for k in range(8)]
    halves = -(-own // LANES)
    OWN_OF[72] = own

    active = jnp.arange(slots, dtype=jnp.int32) < sizes[0]
    row_step, col_step, inside = window_positions(dof_ids[0], own)
    positions = jnp.where(active, (col_step * 3 + row_step) * own + inside, -1)
    row_step, col_step, inside = window_positions(coarse_ids[0], per_coarse)
    coarse_in = (col_step * 3 + row_step) * per_coarse + inside
    coarse_out = (row_step * 3 + col_step) * per_coarse + inside
    basis = averaging_basis[0]

    near = spread(start.astype(BF16))

    g, gt, cs, og, basis_t, counts = call(
        prepare_kernel,
        [
            ((slots, window), BF16),
            ((window, slots), BF16),
            ((coarse_window, primals), BF16),
            ((primals, coarse_window), BF16),
            ((primals, slots), BF16),
            ((72, LANES), F32),
        ],
        positions[:, None],
        positions[None, :],
        coarse_in[:, None],
        coarse_in[None, :],
        coarse_out[:, None],
        basis,
    )
    panel = coarse_inverse.reshape(-1, coarse_inverse.shape[3])
    high, low = call(panel_kernel, [(panel.shape[::-1], BF16)] * 2, panel)

    weight = None
    field = start
    residual = start
    for sweep in range(ITERS):
        third = 3 * own
        left, middle, right = call(
            residual_kernel,
            [((third, LANES), d) for d in (RES_A, RES_M, RES_A)],
            *near,
            g,
            gt,
            stiffness[0],
            loads[0],
        )
        if weight is None:
            def ride(part, column):
                parts = []
                for k in range(3):
                    parts.append(part[k * own : (k + 1) * own])
                    at = (3 * column + k) * 8
                    parts.append(counts[at : at + 8].astype(part.dtype))
                return jnp.concatenate(parts, axis=0)

            left, middle, right = ride(left, 0), ride(middle, 1), ride(right, 2)
        owned = sum_rows(sum_cols(left, middle, right), RES_B)
        residual = owned[:own]
        near = spread(owned.astype(RES_H))
        if weight is None:
            step = own + 8
            blocks = [n[k * step + own : (k + 1) * step] for n in near for k in range(3)]
            shared = jnp.concatenate([wide(b) for b in blocks], axis=0)
            near = tuple(
                jnp.concatenate([n[k * step : k * step + own] for k in range(3)], axis=0) for n in near
            )
            (weight,) = call(weight_kernel, [((slots, LANES), F32)], shared, positions[:, None])
        third = 3 * per_coarse
        scaled, left, middle, right = call(
            primal_kernel,
            [((slots, LANES), BF16)] + [((third, LANES), d) for d in (COARSE_A, COARSE_M, COARSE_A)],
            *near,
            g,
            weight,
            basis_t,
            cs,
        )
        (local_part,) = call(local_kernel, [((slots, LANES), F32)], local_inverse[0], scaled)
        mine = sum_cols(left, middle, right).astype(RHS_1)
        first = from_everyone(mine, inner)
        (folded,) = call(fold_kernel, [((10 * per_coarse, LANES), RHS_2)], first)
        second = from_everyone(folded, outer)
        parts, _ = call(
            coarse_kernel,
            [((members, third, LANES), PART), ((rows * per_coarse, LANES), RHS_2)],
            second,
            high,
            low,
        )
        parts = lax.all_to_all(parts, "col", 0, 0, tiled=True)
        totals = wide(parts).sum(axis=0).astype(BF16)
        above, below = pair(totals, totals, "row")
        third = 3 * own
        left, middle, right = call(
            update_kernel,
            [((third, LANES), d) for d in (UPD_A, UPD_M, UPD_A)],
            above,
            totals,
            below,
            og,
            basis,
            weight,
            local_part,
            gt,
        )
        field = field + sum_rows(sum_cols(left, middle, right), UPD_B)
        if sweep + 1 < ITERS:
            near = spread(field.astype(BF16))
    return field, residual


def solution(mesh):
    in_specs = (
        P(("row", "col"), None, None),
        P(("row", "col"), None, None),
        P(("row", "col"), None, None),
        P(("row", "col"), None, None),
        P(("row", "col"), None),
        P(None, "col", None, "row"),
        P(("row", "col")),
        P(("row", "col"), None),
        P(("row", "col"), None),
    )
    out_specs = (P(("row", "col"), None), P(("row", "col"), None))
    return jax.shard_map(body, mesh=mesh, in_specs=in_specs, out_specs=out_specs, check_vma=False)
```

time: 484 us -> 357 us (0.74)
  starting transfers between devices: 209 us -> 156 us
  other arithmetic: 45.8 us -> 7.51 us
  blocking collectives: 97.6 us -> 70.8 us
  Pallas kernels: 0 us -> 23.3 us
  matrix products: 14 us -> 0 us
  local copies, waits for them, and re-layouts: 21.2 us -> 8.63 us
    ppermute x52 -> x40, starting transfers between devices: 204 us -> 149 us  [the longest x20 103 us: pair(): lax.ppermute(to_previous, axis, [(i + 1, i) for i in range(count - 1)])]
    scatter-add x7 -> x0, other arithmetic: 32.7 us -> none  [spread_back(): jax.ops.segment_sum(values, target, num_segments=window_size + 1)]
    all_to_all x3 -> x5, blocking collectives: 97.6 us -> 70.8 us  [the longest x3 50.5 us: from_everyone(): lax.all_to_all(copies, 'row', 0, 0, axis_index_groups=groups, tiled=True)]
    pallas_call x0 -> x15, Pallas kernels: none -> 23.3 us  [call(): pl.pallas_call(kernel, out_shape=tuple((jax.ShapeDtypeStruct(s, d) for s,...]
    gather x7 -> x0, local copies, waits for them, and re-layouts: 14 us -> none  [the longest x6 9.57 us: take_rows(): picked = jnp.take(window_rows, positions, axis=0, mode='clip')]
    dot_general x10 -> x0, matrix products: 14 us -> none  [the longest x2 5.32 us: body(): lax.dot_general(panel, gather_directly(coarse_owned, 'row', 0), (((0,), (...]
    ppermute x52 -> x40, waiting for transfers between devices: 80.5 us -> 73.2 us  [the longest x20 57 us: pair(): lax.ppermute(to_previous, axis, [(i + 1, i) for i in range(count - 1)])]
  transfers between devices with their start and end apart: 53 -> 41, of which waited for: 26 -> 31; matrix products, arithmetic and copies ran while one was open for 6% -> 1% of each run, Pallas kernels for 0% -> 1%
where the time goes in v1:
time: 357 us; the launch traced here: 355 us
  starting transfers between devices  156 us (44%)
  waiting for transfers between devices  86.1 us (24%)
  blocking collectives  70.8 us (20%)
  Pallas kernels  23.3 us (7%)
  local copies, waits for them, and re-layouts  8.63 us (2%)
  other arithmetic  7.51 us (2%)
    ppermute x20, starting transfers between devices, pair(): lax.ppermute(to_previous, axis, [(i + 1, i) for i in range(count - 1)])  103 us
    ppermute x20, waiting for transfers between devices, pair(): lax.ppermute(to_previous, axis, [(i + 1, i) for i in range(count - 1)])  57 us
    all_to_all x3, blocking collectives, from_everyone(): lax.all_to_all(copies, 'row', 0, 0, axis_index_groups=groups, tiled=True)  50.5 us
    ppermute x20, starting transfers between devices, pair(): lax.ppermute(to_next, axis, [(i, i + 1) for i in range(count - 1)])  45.2 us
    pallas_call x15, Pallas kernels, call(): pl.pallas_call(kernel, out_shape=tuple((jax.ShapeDtypeStruct(s, d) for s,...  23.3 us
    all_to_all x2, blocking collectives, body(): parts = lax.all_to_all(parts, 'col', 0, 0, tiled=True)  20.3 us
    ppermute x20, waiting for transfers between devices, pair(): lax.ppermute(to_next, axis, [(i, i + 1) for i in range(count - 1)])  16.2 us
    all_to_all x1, waiting for transfers between devices, from_everyone(): lax.all_to_all(copies, 'row', 0, 0, axis_index_groups=groups, tiled=True)  12.8 us
  transfers between devices with their start and end apart: 41, of which 31 were waited for; matrix products, arithmetic and copies ran while one was open for 1% of the time, Pallas kernels for 1%

profile of v1, /device:TPU:14, one launch (start us, length us, event | category | flops | bytes accessed | tf_op | source)
XLA Modules:
  0.0 354.8 jit_solution(8065503171681353617)
XLA Ops:
  3.5 10.3 %collective-permute-start.1 = (bf16[192,128]{1,0:T(8,128)(2,1)S(1)}, bf16[192,128]{1,0:T(8,128)(2,1)S(1)}, u32[]{:S(2)}, u32[]{:S(2)}) collective-permute-start(bf16[192,128]{1,0:T(8,128)(2,1)S(1)} %convert_element_type.60), channel_id=1, source_target_pairs={{8,0},{16,8},{24,16},{32,24},{40,32},{48,40},{56,48},{64,56},{72,6... | collective-permute-start | bytes 147464 | tf_op jit(solution)/shard_map/ppermute | solution.py:41
  30.9 4.3 %shard_map.105 = (bf16[576,128]{1,0:T(8,128)(2,1)S(1)}, f32[576,128]{1,0:T(8,128)S(1)}, bf16[576,128]{1,0:T(8,128)(2,1)S(1)}) custom-call(bf16[576,128]{1,0:T(8,128)(2,1)S(1)} %collective-permute-done.2.win_l, bf16[576,128]{1,0:T(8,128)(2,1)S(1)} %pad_maximum_fusion.5.win_m, bf16[576,128]{1,0:T(8,128)(2,1)S(1)} %collective-permute-done.3.win_r, ...), custom_call_target="tpu_custom_call" | custom-call | tf_op jit(solution)/shard_map/pallas_call | solution.py:23
  42.5 4.9 %collective-permute-done.5 = bf16[600,128]{1,0:T(8,128)(2,1)S(1)} collective-permute-done((bf16[600,128]{1,0:T(8,128)(2,1)S(1)}, bf16[600,128]{1,0:T(8,128)(2,1)S(1)}, u32[]{:S(2)}, u32[]{:S(2)}) %collective-permute-start.5) | collective-permute-done | bytes 153632 | tf_op jit(solution)/shard_map/ppermute | solution.py:41
  49.4 6.7 %collective-permute-start.7 = (f32[200,128]{1,0:T(8,128)S(1)}, f32[200,128]{1,0:T(8,128)S(1)}, u32[]{:S(2)}, u32[]{:S(2)}) collective-permute-start(f32[200,128]{1,0:T(8,128)S(1)} %get-tuple-element.75), channel_id=1, source_target_pairs={{8,0},{16,8},{24,16},{32,24},{40,32},{48,40},{56,48},{64,56},{72,6... | collective-permute-start | bytes 307208 | tf_op jit(solution)/shard_map/ppermute | solution.py:41
  60.3 6.8 %collective-permute-start.9 = (f32[200,128]{1,0:T(8,128)S(1)}, f32[200,128]{1,0:T(8,128)S(1)}, u32[]{:S(2)}, u32[]{:S(2)}) collective-permute-start(f32[200,128]{1,0:T(8,128)S(1)} %fusion.13), channel_id=1, source_target_pairs={{8,0},{16,8},{24,16},{32,24},{40,32},{48,40},{56,48},{64,56},{72,6... | collective-permute-start | bytes 307208 | tf_op jit(solution)/shard_map/ppermute | solution.py:41
  71.2 3.9 %collective-permute-start.11 = (f32[600,128]{1,0:T(8,128)S(1)}, f32[600,128]{1,0:T(8,128)S(1)}, u32[]{:S(2)}, u32[]{:S(2)}) collective-permute-start(f32[600,128]{1,0:T(8,128)S(1)} %pad_maximum_fusion), channel_id=1, source_target_pairs={{1,0},{2,1},{3,2},{4,3},{5,4},{6,5},{7,6},{9,8},{10,9},{11,10},{12... | collective-permute-start | bytes 921608 | tf_op jit(solution)/shard_map/ppermute | solution.py:41
  75.2 4.9 %collective-permute-done.10 = f32[600,128]{1,0:T(8,128)S(1)} collective-permute-done((f32[600,128]{1,0:T(8,128)S(1)}, f32[600,128]{1,0:T(8,128)S(1)}, u32[]{:S(2)}, u32[]{:S(2)}) %collective-permute-start.10) | collective-permute-done | bytes 307232 | tf_op jit(solution)/shard_map/ppermute | solution.py:40
  80.1 4.4 %collective-permute-done.11 = f32[600,128]{1,0:T(8,128)S(1)} collective-permute-done((f32[600,128]{1,0:T(8,128)S(1)}, f32[600,128]{1,0:T(8,128)S(1)}, u32[]{:S(2)}, u32[]{:S(2)}) %collective-permute-start.11) | collective-permute-done | bytes 307232 | tf_op jit(solution)/shard_map/ppermute | solution.py:41
  98.1 13.5 %all_to_all.30.blocks = bf16[8,72,128]{2,1,0:T(8,128)(2,1)S(1)} all-to-all(bf16[8,72,128]{2,1,0:T(8,128)(2,1)S(1)} %broadcast_in_dim.10), channel_id=1, replica_groups={{0,8,16,24,32,40,48,56},{64,72,80,88,96,104,112,120},{128,136,144,152,1..., dimensions={0} | all-to-all | bytes 294912 | tf_op jit(solution)/shard_map/all_to_all | solution.py:47
  112.5 7.5 %all-to-all-start.1 = ((bf16[8,240,128]{2,1,0:T(8,128)(2,1)}), bf16[8,240,128]{2,1,0:T(8,128)(2,1)S(1)}, u32[]{:S(2)}, u32[]{:S(2)}) async-start(bf16[8,240,128]{2,1,0:T(8,128)(2,1)} %broadcast_in_dim.11), calls=%async_computation.1 | async-start | bytes 983040 | tf_op jit(solution)/shard_map/all_to_all | solution.py:47
  121.9 12.8 %all-to-all-done.1.blocks = bf16[8,240,128]{2,1,0:T(8,128)(2,1)S(1)} async-done(((bf16[8,240,128]{2,1,0:T(8,128)(2,1)}), bf16[8,240,128]{2,1,0:T(8,128)(2,1)S(1)}, u32[]{:S(2)}, u32[]{:S(2)}) %all-to-all-start.1) | async-done | bytes 491552 | tf_op jit(solution)/shard_map/all_to_all | solution.py:47
  137.6 10.3 %all_to_all.31 = f32[8,72,128]{2,1,0:T(8,128)} all-to-all(f32[8,72,128]{2,1,0:T(8,128)S(1)} %get-tuple-element.45), channel_id=1, replica_groups=mesh['row'=64,'col'=8] {'col'}, dimensions={0} | all-to-all | bytes 589824 | tf_op jit(solution)/shard_map/all_to_all | solution.py:319
  150.7 6.7 %collective-permute-start.15 = (bf16[72,128]{1,0:T(8,128)(2,1)S(1)}, bf16[72,128]{1,0:T(8,128)(2,1)S(1)}, u32[]{:S(2)}, u32[]{:S(2)}) collective-permute-start(bf16[72,128]{1,0:T(8,128)(2,1)S(1)} %reduce_sum.18.sol_m), channel_id=1, source_target_pairs={{8,0},{16,8},{24,16},{32,24},{40,32},{48,40},{56,48},{64,56},{72,6... | collective-permute-start | bytes 55304 | tf_op jit(solution)/shard_map/ppermute | solution.py:41
  160.7 4.1 %collective-permute-start.16 = (bf16[576,128]{1,0:T(8,128)(2,1)S(1)}, bf16[576,128]{1,0:T(8,128)(2,1)S(1)}, u32[]{:S(2)}, u32[]{:S(2)}) collective-permute-start(bf16[576,128]{1,0:T(8,128)(2,1)S(1)} %get-tuple-element.49), channel_id=1, source_target_pairs={{0,1},{1,2},{2,3},{3,4},{4,5},{5,6},{6,7},{8,9},{9,10},{10,11},{11... | collective-permute-start | bytes 442376 | tf_op jit(solution)/shard_map/ppermute | solution.py:40
  167.9 6.1 %collective-permute-done.17 = bf16[576,128]{1,0:T(8,128)(2,1)S(1)} collective-permute-done((bf16[576,128]{1,0:T(8,128)(2,1)S(1)}, bf16[576,128]{1,0:T(8,128)(2,1)S(1)}, u32[]{:S(2)}, u32[]{:S(2)}) %collective-permute-start.17) | collective-permute-done | bytes 147488 | tf_op jit(solution)/shard_map/ppermute | solution.py:41
  175.9 6.7 %collective-permute-start.19 = (f32[192,128]{1,0:T(8,128)S(1)}, f32[192,128]{1,0:T(8,128)S(1)}, u32[]{:S(2)}, u32[]{:S(2)}) collective-permute-start(f32[192,128]{1,0:T(8,128)S(1)} %get-tuple-element.81), channel_id=1, source_target_pairs={{8,0},{16,8},{24,16},{32,24},{40,32},{48,40},{56,48},{64,56},{72,6... | collective-permute-start | bytes 294920 | tf_op jit(solution)/shard_map/ppermute | solution.py:41
  187.4 6.7 %collective-permute-start.21 = (bf16[192,128]{1,0:T(8,128)(2,1)S(1)}, bf16[192,128]{1,0:T(8,128)(2,1)S(1)}, u32[]{:S(2)}, u32[]{:S(2)}) collective-permute-start(bf16[192,128]{1,0:T(8,128)(2,1)S(1)} %get-tuple-element.62), channel_id=1, source_target_pairs={{8,0},{16,8},{24,16},{32,24},{40,32},{48,40},{56,48},{64,56},{72,6... | collective-permute-start | bytes 147464 | tf_op jit(solution)/shard_map/ppermute | solution.py:41
  202.9 4.0 %collective-permute-done.23.win_r = bf16[576,128]{1,0:T(8,128)(2,1)S(1)} collective-permute-done((bf16[576,128]{1,0:T(8,128)(2,1)S(1)}, bf16[576,128]{1,0:T(8,128)(2,1)S(1)}, u32[]{:S(2)}, u32[]{:S(2)}) %collective-permute-start.23) | collective-permute-done | bytes 147488 | tf_op jit(solution)/shard_map/ppermute | solution.py:41
  207.0 4.4 %shard_map.113 = (bf16[576,128]{1,0:T(8,128)(2,1)S(1)}, f32[576,128]{1,0:T(8,128)S(1)}, bf16[576,128]{1,0:T(8,128)(2,1)S(1)}) custom-call(bf16[576,128]{1,0:T(8,128)(2,1)S(1)} %collective-permute-done.22.win_l, bf16[576,128]{1,0:T(8,128)(2,1)S(1)} %pad_maximum_fusion.6.win_m, bf16[576,128]{1,0:T(8,128)(2,1)S(1)} %collective-permute-done.23.win_r, ...), custom_call_target="tpu_custom_call" | custom-call | tf_op jit(solution)/shard_map/pallas_call | solution.py:23
  218.6 4.0 %collective-permute-done.25 = bf16[576,128]{1,0:T(8,128)(2,1)S(1)} collective-permute-done((bf16[576,128]{1,0:T(8,128)(2,1)S(1)}, bf16[576,128]{1,0:T(8,128)(2,1)S(1)}, u32[]{:S(2)}, u32[]{:S(2)}) %collective-permute-start.25) | collective-permute-done | bytes 147488 | tf_op jit(solution)/shard_map/ppermute | solution.py:41
  224.6 6.7 %collective-permute-start.27 = (f32[192,128]{1,0:T(8,128)S(1)}, f32[192,128]{1,0:T(8,128)S(1)}, u32[]{:S(2)}, u32[]{:S(2)}) collective-permute-start(f32[192,128]{1,0:T(8,128)S(1)} %get-tuple-element.79), channel_id=1, source_target_pairs={{8,0},{16,8},{24,16},{32,24},{40,32},{48,40},{56,48},{64,56},{72,6... | collective-permute-start | bytes 294920 | tf_op jit(solution)/shard_map/ppermute | solution.py:41
  235.4 6.8 %collective-permute-start.29 = (f32[192,128]{1,0:T(8,128)S(1)}, f32[192,128]{1,0:T(8,128)S(1)}, u32[]{:S(2)}, u32[]{:S(2)}) collective-permute-start(f32[192,128]{1,0:T(8,128)S(1)} %fusion.16), channel_id=1, source_target_pairs={{8,0},{16,8},{24,16},{32,24},{40,32},{48,40},{56,48},{64,56},{72,6... | collective-permute-start | bytes 294920 | tf_op jit(solution)/shard_map/ppermute | solution.py:41
  246.4 3.9 %collective-permute-start.31 = (f32[576,128]{1,0:T(8,128)S(1)}, f32[576,128]{1,0:T(8,128)S(1)}, u32[]{:S(2)}, u32[]{:S(2)}) collective-permute-start(f32[576,128]{1,0:T(8,128)S(1)} %pad_maximum_fusion.4.win_m), channel_id=1, source_target_pairs={{1,0},{2,1},{3,2},{4,3},{5,4},{6,5},{7,6},{9,8},{10,9},{11,10},{12... | collective-permute-start | bytes 884744 | tf_op jit(solution)/shard_map/ppermute | solution.py:41
  253.1 4.0 %collective-permute-done.31.win_r = f32[576,128]{1,0:T(8,128)S(1)} collective-permute-done((f32[576,128]{1,0:T(8,128)S(1)}, f32[576,128]{1,0:T(8,128)S(1)}, u32[]{:S(2)}, u32[]{:S(2)}) %collective-permute-start.31) | collective-permute-done | bytes 294944 | tf_op jit(solution)/shard_map/ppermute | solution.py:41
  261.3 3.9 %collective-permute-start.33 = (bf16[72,128]{1,0:T(8,128)(2,1)S(1)}, bf16[72,128]{1,0:T(8,128)(2,1)S(1)}, u32[]{:S(2)}, u32[]{:S(2)}) collective-permute-start(bf16[72,128]{1,0:T(8,128)(2,1)S(1)} %get-tuple-element.56), channel_id=1, source_target_pairs={{1,0},{2,1},{3,2},{4,3},{5,4},{6,5},{7,6},{9,8},{10,9},{11,10},{12... | collective-permute-start | bytes 55304 | tf_op jit(solution)/shard_map/ppermute | solution.py:41
  269.1 12.8 %all_to_all.32.blocks = bf16[8,72,128]{2,1,0:T(8,128)(2,1)S(1)} all-to-all(bf16[8,72,128]{2,1,0:T(8,128)(2,1)S(1)} %broadcast_in_dim.12), channel_id=1, replica_groups={{0,8,16,24,32,40,48,56},{64,72,80,88,96,104,112,120},{128,136,144,152,1..., dimensions={0} | all-to-all | bytes 294912 | tf_op jit(solution)/shard_map/all_to_all | solution.py:47
  281.9 24.3 %all_to_all.33.blocks = bf16[8,240,128]{2,1,0:T(8,128)(2,1)S(1)} all-to-all(bf16[8,240,128]{2,1,0:T(8,128)(2,1)S(1)} %broadcast_in_dim.13), channel_id=1, replica_groups={{0,64,128,192,256,320,384,448},{8,72,136,200,264,328,392,456},{16,80,14..., dimensions={0} | all-to-all | bytes 983040 | tf_op jit(solution)/shard_map/all_to_all | solution.py:47
  307.3 10.0 %all_to_all.34 = f32[8,72,128]{2,1,0:T(8,128)} all-to-all(f32[8,72,128]{2,1,0:T(8,128)S(1)} %get-tuple-element.57), channel_id=1, replica_groups=mesh['row'=64,'col'=8] {'col'}, dimensions={0} | all-to-all | bytes 589824 | tf_op jit(solution)/shard_map/all_to_all | solution.py:319
  320.2 6.7 %collective-permute-start.35 = (bf16[72,128]{1,0:T(8,128)(2,1)S(1)}, bf16[72,128]{1,0:T(8,128)(2,1)S(1)}, u32[]{:S(2)}, u32[]{:S(2)}) collective-permute-start(bf16[72,128]{1,0:T(8,128)(2,1)S(1)} %reduce_sum.19.sol_m), channel_id=1, source_target_pairs={{8,0},{16,8},{24,16},{32,24},{40,32},{48,40},{56,48},{64,56},{72,6... | collective-permute-start | bytes 55304 | tf_op jit(solution)/shard_map/ppermute | solution.py:41
  330.1 4.0 %collective-permute-start.36 = (bf16[576,128]{1,0:T(8,128)(2,1)S(1)}, bf16[576,128]{1,0:T(8,128)(2,1)S(1)}, u32[]{:S(2)}, u32[]{:S(2)}) collective-permute-start(bf16[576,128]{1,0:T(8,128)(2,1)S(1)} %get-tuple-element.60), channel_id=1, source_target_pairs={{0,1},{1,2},{2,3},{3,4},{4,5},{5,6},{6,7},{8,9},{9,10},{10,11},{11... | collective-permute-start | bytes 442376 | tf_op jit(solution)/shard_map/ppermute | solution.py:40
  337.2 6.1 %collective-permute-done.37 = bf16[576,128]{1,0:T(8,128)(2,1)S(1)} collective-permute-done((bf16[576,128]{1,0:T(8,128)(2,1)S(1)}, bf16[576,128]{1,0:T(8,128)(2,1)S(1)}, u32[]{:S(2)}, u32[]{:S(2)}) %collective-permute-start.37) | collective-permute-done | bytes 147488 | tf_op jit(solution)/shard_map/ppermute | solution.py:41
  345.3 6.7 %collective-permute-start.39 = (f32[192,128]{1,0:T(8,128)S(1)}, f32[192,128]{1,0:T(8,128)S(1)}, u32[]{:S(2)}, u32[]{:S(2)}) collective-permute-start(f32[192,128]{1,0:T(8,128)S(1)} %get-tuple-element.77), channel_id=1, source_target_pairs={{8,0},{16,8},{24,16},{32,24},{40,32},{48,40},{56,48},{64,56},{72,6... | collective-permute-start | bytes 294920 | tf_op jit(solution)/shard_map/ppermute | solution.py:41
  (196 shorter events, 123.8 us)
Async XLA Ops:
  1.6 16.8 %collective-permute-start = (bf16[192,128]{1,0:T(8,128)(2,1)S(1)}, bf16[192,128]{1,0:T(8,128)(2,1)S(1)}, u32[]{:S(2)}, u32[]{:S(2)}) collective-permute-start(bf16[192,128]{1,0:T(8,128)(2,1)S(1)} %convert_element_type.60), channel_id=1, source_target_pairs={{0,8},{8,16},{16,24},{24,32},{32,40},{40,48},{48,56},{56,64},{64,7... | collective-permute-start | bytes 147464 | tf_op jit(solution)/shard_map/ppermute | solution.py:40
  3.5 14.9 %collective-permute-start.1 = (bf16[192,128]{1,0:T(8,128)(2,1)S(1)}, bf16[192,128]{1,0:T(8,128)(2,1)S(1)}, u32[]{:S(2)}, u32[]{:S(2)}) collective-permute-start(bf16[192,128]{1,0:T(8,128)(2,1)S(1)} %convert_element_type.60), channel_id=1, source_target_pairs={{8,0},{16,8},{24,16},{32,24},{40,32},{48,40},{56,48},{64,56},{72,6... | collective-permute-start | bytes 147464 | tf_op jit(solution)/shard_map/ppermute | solution.py:41
  18.4 8.9 %collective-permute-start.2 = (bf16[576,128]{1,0:T(8,128)(2,1)S(1)}, bf16[576,128]{1,0:T(8,128)(2,1)S(1)}, u32[]{:S(2)}, u32[]{:S(2)}) collective-permute-start(bf16[576,128]{1,0:T(8,128)(2,1)S(1)} %pad_maximum_fusion.5.win_m), channel_id=1, source_target_pairs={{0,1},{1,2},{2,3},{3,4},{4,5},{5,6},{6,7},{8,9},{9,10},{10,11},{11... | collective-permute-start | bytes 442376 | tf_op jit(solution)/shard_map/ppermute | solution.py:40
  21.7 9.1 %collective-permute-start.3 = (bf16[576,128]{1,0:T(8,128)(2,1)S(1)}, bf16[576,128]{1,0:T(8,128)(2,1)S(1)}, u32[]{:S(2)}, u32[]{:S(2)}) collective-permute-start(bf16[576,128]{1,0:T(8,128)(2,1)S(1)} %pad_maximum_fusion.5.win_m), channel_id=1, source_target_pairs={{1,0},{2,1},{3,2},{4,3},{5,4},{6,5},{7,6},{9,8},{10,9},{11,10},{12... | collective-permute-start | bytes 442376 | tf_op jit(solution)/shard_map/ppermute | solution.py:41
  38.2 9.2 %collective-permute-start.5 = (bf16[600,128]{1,0:T(8,128)(2,1)S(1)}, bf16[600,128]{1,0:T(8,128)(2,1)S(1)}, u32[]{:S(2)}, u32[]{:S(2)}) collective-permute-start(bf16[600,128]{1,0:T(8,128)(2,1)S(1)} %get-tuple-element.85), channel_id=1, source_target_pairs={{1,0},{2,1},{3,2},{4,3},{5,4},{6,5},{7,6},{9,8},{10,9},{11,10},{12... | collective-permute-start | bytes 460808 | tf_op jit(solution)/shard_map/ppermute | solution.py:41
  47.5 9.0 %collective-permute-start.6 = (f32[200,128]{1,0:T(8,128)S(1)}, f32[200,128]{1,0:T(8,128)S(1)}, u32[]{:S(2)}, u32[]{:S(2)}) collective-permute-start(f32[200,128]{1,0:T(8,128)S(1)} %get-tuple-element.74), channel_id=1, source_target_pairs={{0,8},{8,16},{16,24},{24,32},{32,40},{40,48},{48,56},{56,64},{64,7... | collective-permute-start | bytes 307208 | tf_op jit(solution)/shard_map/ppermute | solution.py:40
  49.4 8.9 %collective-permute-start.7 = (f32[200,128]{1,0:T(8,128)S(1)}, f32[200,128]{1,0:T(8,128)S(1)}, u32[]{:S(2)}, u32[]{:S(2)}) collective-permute-start(f32[200,128]{1,0:T(8,128)S(1)} %get-tuple-element.75), channel_id=1, source_target_pairs={{8,0},{16,8},{24,16},{32,24},{40,32},{48,40},{56,48},{64,56},{72,6... | collective-permute-start | bytes 307208 | tf_op jit(solution)/shard_map/ppermute | solution.py:41
  58.3 9.1 %collective-permute-start.8 = (f32[200,128]{1,0:T(8,128)S(1)}, f32[200,128]{1,0:T(8,128)S(1)}, u32[]{:S(2)}, u32[]{:S(2)}) collective-permute-start(f32[200,128]{1,0:T(8,128)S(1)} %fusion.13), channel_id=1, source_target_pairs={{0,8},{8,16},{16,24},{24,32},{32,40},{40,48},{48,56},{56,64},{64,7... | collective-permute-start | bytes 307208 | tf_op jit(solution)/shard_map/ppermute | solution.py:40
  60.3 9.0 %collective-permute-start.9 = (f32[200,128]{1,0:T(8,128)S(1)}, f32[200,128]{1,0:T(8,128)S(1)}, u32[]{:S(2)}, u32[]{:S(2)}) collective-permute-start(f32[200,128]{1,0:T(8,128)S(1)} %fusion.13), channel_id=1, source_target_pairs={{8,0},{16,8},{24,16},{32,24},{40,32},{48,40},{56,48},{64,56},{72,6... | collective-permute-start | bytes 307208 | tf_op jit(solution)/shard_map/ppermute | solution.py:41
  69.3 10.8 %collective-permute-start.10 = (f32[600,128]{1,0:T(8,128)S(1)}, f32[600,128]{1,0:T(8,128)S(1)}, u32[]{:S(2)}, u32[]{:S(2)}) collective-permute-start(f32[600,128]{1,0:T(8,128)S(1)} %pad_maximum_fusion), channel_id=1, source_target_pairs={{0,1},{1,2},{2,3},{3,4},{4,5},{5,6},{6,7},{8,9},{9,10},{10,11},{11... | collective-permute-start | bytes 921608 | tf_op jit(solution)/shard_map/ppermute | solution.py:40
  71.2 13.3 %collective-permute-start.11 = (f32[600,128]{1,0:T(8,128)S(1)}, f32[600,128]{1,0:T(8,128)S(1)}, u32[]{:S(2)}, u32[]{:S(2)}) collective-permute-start(f32[600,128]{1,0:T(8,128)S(1)} %pad_maximum_fusion), channel_id=1, source_target_pairs={{1,0},{2,1},{3,2},{4,3},{5,4},{6,5},{7,6},{9,8},{10,9},{11,10},{12... | collective-permute-start | bytes 921608 | tf_op jit(solution)/shard_map/ppermute | solution.py:41
  112.5 22.3 %all-to-all-start.1 = ((bf16[8,240,128]{2,1,0:T(8,128)(2,1)}), bf16[8,240,128]{2,1,0:T(8,128)(2,1)S(1)}, u32[]{:S(2)}, u32[]{:S(2)}) async-start(bf16[8,240,128]{2,1,0:T(8,128)(2,1)} %broadcast_in_dim.11), calls=%async_computation.1 | async-start | bytes 983040 | tf_op jit(solution)/shard_map/all_to_all | solution.py:47
  148.8 10.3 %collective-permute-start.14 = (bf16[72,128]{1,0:T(8,128)(2,1)S(1)}, bf16[72,128]{1,0:T(8,128)(2,1)S(1)}, u32[]{:S(2)}, u32[]{:S(2)}) collective-permute-start(bf16[72,128]{1,0:T(8,128)(2,1)S(1)} %reduce_sum.18.sol_m), channel_id=1, source_target_pairs={{0,8},{8,16},{16,24},{24,32},{32,40},{40,48},{48,56},{56,64},{64,7... | collective-permute-start | bytes 55304 | tf_op jit(solution)/shard_map/ppermute | solution.py:40
  150.7 8.4 %collective-permute-start.15 = (bf16[72,128]{1,0:T(8,128)(2,1)S(1)}, bf16[72,128]{1,0:T(8,128)(2,1)S(1)}, u32[]{:S(2)}, u32[]{:S(2)}) collective-permute-start(bf16[72,128]{1,0:T(8,128)(2,1)S(1)} %reduce_sum.18.sol_m), channel_id=1, source_target_pairs={{8,0},{16,8},{24,16},{32,24},{40,32},{48,40},{56,48},{64,56},{72,6... | collective-permute-start | bytes 55304 | tf_op jit(solution)/shard_map/ppermute | solution.py:41
  164.8 9.1 %collective-permute-start.17 = (bf16[576,128]{1,0:T(8,128)(2,1)S(1)}, bf16[576,128]{1,0:T(8,128)(2,1)S(1)}, u32[]{:S(2)}, u32[]{:S(2)}) collective-permute-start(bf16[576,128]{1,0:T(8,128)(2,1)S(1)} %get-tuple-element.50), channel_id=1, source_target_pairs={{1,0},{2,1},{3,2},{4,3},{5,4},{6,5},{7,6},{9,8},{10,9},{11,10},{12... | collective-permute-start | bytes 442376 | tf_op jit(solution)/shard_map/ppermute | solution.py:41
  174.0 9.4 %collective-permute-start.18 = (f32[192,128]{1,0:T(8,128)S(1)}, f32[192,128]{1,0:T(8,128)S(1)}, u32[]{:S(2)}, u32[]{:S(2)}) collective-permute-start(f32[192,128]{1,0:T(8,128)S(1)} %get-tuple-element.80), channel_id=1, source_target_pairs={{0,8},{8,16},{16,24},{24,32},{32,40},{40,48},{48,56},{56,64},{64,7... | collective-permute-start | bytes 294920 | tf_op jit(solution)/shard_map/ppermute | solution.py:40
  175.9 8.8 %collective-permute-start.19 = (f32[192,128]{1,0:T(8,128)S(1)}, f32[192,128]{1,0:T(8,128)S(1)}, u32[]{:S(2)}, u32[]{:S(2)}) collective-permute-start(f32[192,128]{1,0:T(8,128)S(1)} %get-tuple-element.81), channel_id=1, source_target_pairs={{8,0},{16,8},{24,16},{32,24},{40,32},{48,40},{56,48},{64,56},{72,6... | collective-permute-start | bytes 294920 | tf_op jit(solution)/shard_map/ppermute | solution.py:41
  185.5 8.7 %collective-permute-start.20 = (bf16[192,128]{1,0:T(8,128)(2,1)S(1)}, bf16[192,128]{1,0:T(8,128)(2,1)S(1)}, u32[]{:S(2)}, u32[]{:S(2)}) collective-permute-start(bf16[192,128]{1,0:T(8,128)(2,1)S(1)} %get-tuple-element.62), channel_id=1, source_target_pairs={{0,8},{8,16},{16,24},{24,32},{32,40},{40,48},{48,56},{56,64},{64,7... | collective-permute-start | bytes 147464 | tf_op jit(solution)/shard_map/ppermute | solution.py:40
  187.4 8.5 %collective-permute-start.21 = (bf16[192,128]{1,0:T(8,128)(2,1)S(1)}, bf16[192,128]{1,0:T(8,128)(2,1)S(1)}, u32[]{:S(2)}, u32[]{:S(2)}) collective-permute-start(bf16[192,128]{1,0:T(8,128)(2,1)S(1)} %get-tuple-element.62), channel_id=1, source_target_pairs={{8,0},{16,8},{24,16},{32,24},{40,32},{48,40},{56,48},{64,56},{72,6... | collective-permute-start | bytes 147464 | tf_op jit(solution)/shard_map/ppermute | solution.py:41
  197.8 9.1 %collective-permute-start.23 = (bf16[576,128]{1,0:T(8,128)(2,1)S(1)}, bf16[576,128]{1,0:T(8,128)(2,1)S(1)}, u32[]{:S(2)}, u32[]{:S(2)}) collective-permute-start(bf16[576,128]{1,0:T(8,128)(2,1)S(1)} %pad_maximum_fusion.6.win_m), channel_id=1, source_target_pairs={{1,0},{2,1},{3,2},{4,3},{5,4},{6,5},{7,6},{9,8},{10,9},{11,10},{12... | collective-permute-start | bytes 442376 | tf_op jit(solution)/shard_map/ppermute | solution.py:41
  213.5 9.1 %collective-permute-start.25 = (bf16[576,128]{1,0:T(8,128)(2,1)S(1)}, bf16[576,128]{1,0:T(8,128)(2,1)S(1)}, u32[]{:S(2)}, u32[]{:S(2)}) collective-permute-start(bf16[576,128]{1,0:T(8,128)(2,1)S(1)} %get-tuple-element.53), channel_id=1, source_target_pairs={{1,0},{2,1},{3,2},{4,3},{5,4},{6,5},{7,6},{9,8},{10,9},{11,10},{12... | collective-permute-start | bytes 442376 | tf_op jit(solution)/shard_map/ppermute | solution.py:41
  222.7 8.9 %collective-permute-start.26 = (f32[192,128]{1,0:T(8,128)S(1)}, f32[192,128]{1,0:T(8,128)S(1)}, u32[]{:S(2)}, u32[]{:S(2)}) collective-permute-start(f32[192,128]{1,0:T(8,128)S(1)} %get-tuple-element.78), channel_id=1, source_target_pairs={{0,8},{8,16},{16,24},{24,32},{32,40},{40,48},{48,56},{56,64},{64,7... | collective-permute-start | bytes 294920 | tf_op jit(solution)/shard_map/ppermute | solution.py:40
  224.6 8.8 %collective-permute-start.27 = (f32[192,128]{1,0:T(8,128)S(1)}, f32[192,128]{1,0:T(8,128)S(1)}, u32[]{:S(2)}, u32[]{:S(2)}) collective-permute-start(f32[192,128]{1,0:T(8,128)S(1)} %get-tuple-element.79), channel_id=1, source_target_pairs={{8,0},{16,8},{24,16},{32,24},{40,32},{48,40},{56,48},{64,56},{72,6... | collective-permute-start | bytes 294920 | tf_op jit(solution)/shard_map/ppermute | solution.py:41
  233.5 9.1 %collective-permute-start.28 = (f32[192,128]{1,0:T(8,128)S(1)}, f32[192,128]{1,0:T(8,128)S(1)}, u32[]{:S(2)}, u32[]{:S(2)}) collective-permute-start(f32[192,128]{1,0:T(8,128)S(1)} %fusion.16), channel_id=1, source_target_pairs={{0,8},{8,16},{16,24},{24,32},{32,40},{40,48},{48,56},{56,64},{64,7... | collective-permute-start | bytes 294920 | tf_op jit(solution)/shard_map/ppermute | solution.py:40
  235.4 9.0 %collective-permute-start.29 = (f32[192,128]{1,0:T(8,128)S(1)}, f32[192,128]{1,0:T(8,128)S(1)}, u32[]{:S(2)}, u32[]{:S(2)}) collective-permute-start(f32[192,128]{1,0:T(8,128)S(1)} %fusion.16), channel_id=1, source_target_pairs={{8,0},{16,8},{24,16},{32,24},{40,32},{48,40},{56,48},{64,56},{72,6... | collective-permute-start | bytes 294920 | tf_op jit(solution)/shard_map/ppermute | solution.py:41
  244.5 8.6 %collective-permute-start.30 = (f32[576,128]{1,0:T(8,128)S(1)}, f32[576,128]{1,0:T(8,128)S(1)}, u32[]{:S(2)}, u32[]{:S(2)}) collective-permute-start(f32[576,128]{1,0:T(8,128)S(1)} %pad_maximum_fusion.4.win_m), channel_id=1, source_target_pairs={{0,1},{1,2},{2,3},{3,4},{4,5},{5,6},{6,7},{8,9},{9,10},{10,11},{11... | collective-permute-start | bytes 884744 | tf_op jit(solution)/shard_map/ppermute | solution.py:40
  246.4 10.7 %collective-permute-start.31 = (f32[576,128]{1,0:T(8,128)S(1)}, f32[576,128]{1,0:T(8,128)S(1)}, u32[]{:S(2)}, u32[]{:S(2)}) collective-permute-start(f32[576,128]{1,0:T(8,128)S(1)} %pad_maximum_fusion.4.win_m), channel_id=1, source_target_pairs={{1,0},{2,1},{3,2},{4,3},{5,4},{6,5},{7,6},{9,8},{10,9},{11,10},{12... | collective-permute-start | bytes 884744 | tf_op jit(solution)/shard_map/ppermute | solution.py:41
  318.3 10.4 %collective-permute-start.34 = (bf16[72,128]{1,0:T(8,128)(2,1)S(1)}, bf16[72,128]{1,0:T(8,128)(2,1)S(1)}, u32[]{:S(2)}, u32[]{:S(2)}) collective-permute-start(bf16[72,128]{1,0:T(8,128)(2,1)S(1)} %reduce_sum.19.sol_m), channel_id=1, source_target_pairs={{0,8},{8,16},{16,24},{24,32},{32,40},{40,48},{48,56},{56,64},{64,7... | collective-permute-start | bytes 55304 | tf_op jit(solution)/shard_map/ppermute | solution.py:40
  320.2 8.4 %collective-permute-start.35 = (bf16[72,128]{1,0:T(8,128)(2,1)S(1)}, bf16[72,128]{1,0:T(8,128)(2,1)S(1)}, u32[]{:S(2)}, u32[]{:S(2)}) collective-permute-start(bf16[72,128]{1,0:T(8,128)(2,1)S(1)} %reduce_sum.19.sol_m), channel_id=1, source_target_pairs={{8,0},{16,8},{24,16},{32,24},{40,32},{48,40},{56,48},{64,56},{72,6... | collective-permute-start | bytes 55304 | tf_op jit(solution)/shard_map/ppermute | solution.py:41
  334.1 9.1 %collective-permute-start.37 = (bf16[576,128]{1,0:T(8,128)(2,1)S(1)}, bf16[576,128]{1,0:T(8,128)(2,1)S(1)}, u32[]{:S(2)}, u32[]{:S(2)}) collective-permute-start(bf16[576,128]{1,0:T(8,128)(2,1)S(1)} %get-tuple-element.61), channel_id=1, source_target_pairs={{1,0},{2,1},{3,2},{4,3},{5,4},{6,5},{7,6},{9,8},{10,9},{11,10},{12... | collective-permute-start | bytes 442376 | tf_op jit(solution)/shard_map/ppermute | solution.py:41
  343.3 8.9 %collective-permute-start.38 = (f32[192,128]{1,0:T(8,128)S(1)}, f32[192,128]{1,0:T(8,128)S(1)}, u32[]{:S(2)}, u32[]{:S(2)}) collective-permute-start(f32[192,128]{1,0:T(8,128)S(1)} %get-tuple-element.76), channel_id=1, source_target_pairs={{0,8},{8,16},{16,24},{24,32},{32,40},{40,48},{48,56},{56,64},{64,7... | collective-permute-start | bytes 294920 | tf_op jit(solution)/shard_map/ppermute | solution.py:40
  345.3 8.8 %collective-permute-start.39 = (f32[192,128]{1,0:T(8,128)S(1)}, f32[192,128]{1,0:T(8,128)S(1)}, u32[]{:S(2)}, u32[]{:S(2)}) collective-permute-start(f32[192,128]{1,0:T(8,128)S(1)} %get-tuple-element.77), channel_id=1, source_target_pairs={{8,0},{16,8},{24,16},{32,24},{40,32},{48,40},{56,48},{64,56},{72,6... | collective-permute-start | bytes 294920 | tf_op jit(solution)/shard_map/ppermute | solution.py:41
  (37 other events, 744.8 us)

commit v2 on v1

--- a/solution.py
+++ b/solution.py
@@ -19,10 +19,15 @@
     return jnp.dot(a, b, preferred_element_type=F32)
 
 
-def call(kernel, outs, *args):
+def call(kernel, outs, *args, scalar=None):
+    specs = [pl.BlockSpec(memory_space=pltpu.VMEM)] * len(args)
+    if scalar is not None:
+        specs = [pl.BlockSpec(memory_space=pltpu.SMEM)] + specs
+        args = (scalar, *args)
     return pl.pallas_call(
         kernel,
         out_shape=tuple(jax.ShapeDtypeStruct(s, d) for s, d in outs),
+        in_specs=specs,
         compiler_params=pltpu.CompilerParams(vmem_limit_bytes=48 * 1024 * 1024),
     )(*args)
 
@@ -42,8 +47,7 @@
     return from_previous, from_next
 
 
-def from_everyone(block, groups):
-    copies = jnp.broadcast_to(block[None], (len(groups[0]), *block.shape))
+def from_everyone(copies, groups):
     return lax.all_to_all(copies, "row", 0, 0, axis_index_groups=groups, tiled=True)
 
 
@@ -51,23 +55,81 @@
     return a.astype(F32)
 
 
-def sum_cols(left, middle, right):
-    from_previous, from_next = pair(right, left, "col")
-    return wide(middle) + wide(from_previous) + wide(from_next)
-
-
-def sum_rows(summed, kind):
+def spread(column):
+    from_previous, from_next = pair(column, column, "row")
+    return from_previous, column, from_next
+
+
+def shared_by_columns(column, up, middle, down):
+    from_previous, from_next = pair(down, up, "row")
+    members = lax.axis_size("col")
+    third = middle.shape[0] // 3
+    summed, sent = call(
+        send_kernel,
+        [(middle.shape, F32), ((members, 2 * third, LANES), BF16)],
+        from_previous,
+        middle,
+        from_next,
+        scalar=column,
+    )
+    got = lax.all_to_all(sent, "col", 0, 0, tiled=True)
+    (assembled,) = call(receive_kernel, [(middle.shape, F32)], got, summed, scalar=column)
+    return assembled
+
+
+def owned_sum(up, middle, down):
+    from_previous, from_next = pair(down, up, "row")
+    summed = wide(middle) + wide(from_previous) + wide(from_next)
     third = summed.shape[0] // 3
-    up, own, down = summed[:third], summed[third : 2 * third], summed[2 * third :]
-    from_previous, from_next = pair(down.astype(kind), up.astype(kind), "row")
+    left, own, right = summed[:third], summed[third : 2 * third], summed[2 * third :]
+    from_previous, from_next = pair(right.astype(UPD_B), left.astype(UPD_B), "col")
     return own + wide(from_previous) + wide(from_next)
 
 
-def spread(owned):
-    from_previous, from_next = pair(owned, owned, "row")
-    column = jnp.concatenate([from_previous, owned, from_next], axis=0)
-    left, right = pair(column, column, "col")
-    return left, column, right
+def nth(c, step, members):
+    return lax.rem(c + step + members, members)
+
+
+def send_kernel(column, from_previous, middle, from_next, summed, sent):
+    third = middle.shape[0] // 3
+    members = sent.shape[0]
+    c = column[0]
+    total = wide(from_previous[...]) + wide(middle[...]) + wide(from_next[...])
+    summed[...] = total
+    left, own, right = (total[k * third : (k + 1) * third].astype(BF16) for k in range(3))
+    sent[nth(c, 1, members), :third, :] = own
+    sent[nth(c, 1, members), third:, :] = right
+    sent[nth(c, 2, members), :third, :] = right
+    sent[nth(c, -1, members), :third, :] = own
+    sent[nth(c, -1, members), third:, :] = left
+    sent[nth(c, -2, members), :third, :] = left
+
+
+def receive_kernel(column, got, summed, out):
+    third = summed.shape[0] // 3
+    members = got.shape[0]
+    c = column[0]
+
+    def part(step, rows):
+        there = (c + step >= 0) & (c + step < members)
+        return jnp.where(there, wide(got[nth(c, step, members), rows, :]), 0.0)
+
+    first, second = slice(0, third), slice(third, 2 * third)
+    out[:third] = summed[:third] + part(-1, first) + part(-2, first)
+    out[third : 2 * third] = summed[third : 2 * third] + part(-1, second) + part(1, second)
+    out[2 * third :] = summed[2 * third :] + part(1, first) + part(2, first)
+
+
+def coarse_receive_kernel(column, got, middle, out):
+    members = got.shape[0]
+    c = column[0]
+    total = wide(middle[...])
+    for step in (-1, 1):
+        there = (c + step >= 0) & (c + step < members)
+        total = total + jnp.where(there, wide(got[nth(c, step, members)]), 0.0)
+    total = total.astype(out.dtype)
+    for k in range(out.shape[0]):
+        out[k] = total
 
 
 def prepare_kernel(pos_col, pos_row, coarse_col, coarse_row, out_col, basis, g, gt, cs, og, basis_t, counts):
@@ -153,12 +215,20 @@
 OWN_OF = {}
 
 
-def primal_kernel(win_l, win_m, win_r, g, weight, basis_t, cs, scaled, out_l, out_m, out_r):
-    rows = gathered(g, win_l[...], win_m[...], win_r[...])
+def primal_kernel(column, up, middle, down, g, weight, basis_t, cs, scaled, sent, kept):
+    rows = gathered(g, up[...], middle[...], down[...])
     values = (weight[...] * rows).astype(BF16)
     scaled[...] = values
     primal = dot(basis_t[...], values)
-    scattered(cs, primal, out_l, out_m, out_r)
+    third = kept.shape[0]
+    members = sent.shape[0]
+    c = column[0]
+    high = primal.astype(BF16)
+    low = (primal - wide(high)).astype(BF16)
+    sent[nth(c, -1, members)] = dot(cs[:third], high).astype(sent.dtype)
+    sent[nth(c, 1, members)] = dot(cs[2 * third :], high).astype(sent.dtype)
+    rows = cs[third : 2 * third]
+    kept[...] = dot(rows, high) + dot(rows, low)
 
 
 def local_kernel(local_inverse, scaled, out):
@@ -173,7 +243,9 @@
         for k in range(max(row - 1, 0), min(row + 1, count - 1) + 1):
             part = wide(blocks[k, (row - k + 1) * third : (row - k + 2) * third, :])
             total = part if total is None else total + part
-        out[(row + 1) * third : (row + 2) * third, :] = total.astype(out.dtype)
+        total = total.astype(out.dtype)
+        for copy in range(out.shape[0]):
+            out[copy, (row + 1) * third : (row + 2) * third, :] = total
 
 
 def coarse_kernel(blocks, high, low, out, rhs):
@@ -229,15 +301,19 @@
     halves = -(-own // LANES)
     OWN_OF[72] = own
 
+    column = lax.axis_index("col").astype(jnp.int32).reshape(1)
+
     active = jnp.arange(slots, dtype=jnp.int32) < sizes[0]
     row_step, col_step, inside = window_positions(dof_ids[0], own)
-    positions = jnp.where(active, (col_step * 3 + row_step) * own + inside, -1)
+    positions = jnp.where(active, (row_step * 3 + col_step) * own + inside, -1)
     row_step, col_step, inside = window_positions(coarse_ids[0], per_coarse)
     coarse_in = (col_step * 3 + row_step) * per_coarse + inside
     coarse_out = (row_step * 3 + col_step) * per_coarse + inside
     basis = averaging_basis[0]
 
-    near = spread(start.astype(BF16))
+    left, right = pair(start, start, "col")
+    across = jnp.concatenate([left, start, right], axis=0)
+    near = spread(across.astype(BF16))
 
     g, gt, cs, og, basis_t, counts = call(
         prepare_kernel,
@@ -260,11 +336,9 @@
     high, low = call(panel_kernel, [(panel.shape[::-1], BF16)] * 2, panel)
 
     weight = None
-    field = start
-    residual = start
     for sweep in range(ITERS):
         third = 3 * own
-        left, middle, right = call(
+        parts = call(
             residual_kernel,
             [((third, LANES), d) for d in (RES_A, RES_M, RES_A)],
             *near,
@@ -274,20 +348,20 @@
             loads[0],
         )
         if weight is None:
-            def ride(part, column):
-                parts = []
-                for k in range(3):
-                    parts.append(part[k * own : (k + 1) * own])
-                    at = (3 * column + k) * 8
-                    parts.append(counts[at : at + 8].astype(part.dtype))
-                return jnp.concatenate(parts, axis=0)
-
-            left, middle, right = ride(left, 0), ride(middle, 1), ride(right, 2)
-        owned = sum_rows(sum_cols(left, middle, right), RES_B)
-        residual = owned[:own]
+            def ride(part, k):
+                pieces = []
+                for j in range(3):
+                    pieces.append(part[j * own : (j + 1) * own])
+                    at = (3 * k + j) * 8
+                    pieces.append(counts[at : at + 8].astype(part.dtype))
+                return jnp.concatenate(pieces, axis=0)
+
+            parts = [ride(part, k) for k, part in enumerate(parts)]
+        owned = shared_by_columns(column, *parts)
+        step = owned.shape[0] // 3
+        residual = owned[step : step + own]
         near = spread(owned.astype(RES_H))
         if weight is None:
-            step = own + 8
             blocks = [n[k * step + own : (k + 1) * step] for n in near for k in range(3)]
             shared = jnp.concatenate([wide(b) for b in blocks], axis=0)
             near = tuple(
@@ -295,20 +369,21 @@
             )
             (weight,) = call(weight_kernel, [((slots, LANES), F32)], shared, positions[:, None])
         third = 3 * per_coarse
-        scaled, left, middle, right = call(
+        scaled, sent, kept = call(
             primal_kernel,
-            [((slots, LANES), BF16)] + [((third, LANES), d) for d in (COARSE_A, COARSE_M, COARSE_A)],
+            [((slots, LANES), BF16), ((members, third, LANES), COARSE_A), ((third, LANES), F32)],
             *near,
             g,
             weight,
             basis_t,
             cs,
+            scalar=column,
         )
-        (local_part,) = call(local_kernel, [((slots, LANES), F32)], local_inverse[0], scaled)
-        mine = sum_cols(left, middle, right).astype(RHS_1)
-        first = from_everyone(mine, inner)
-        (folded,) = call(fold_kernel, [((10 * per_coarse, LANES), RHS_2)], first)
-        second = from_everyone(folded, outer)
+        got = lax.all_to_all(sent, "col", 0, 0, tiled=True)
+        (first,) = call(coarse_receive_kernel, [((8, third, LANES), RHS_1)], got, kept, scalar=column)
+        first = from_everyone(first, inner)
+        (second,) = call(fold_kernel, [((rows // 8, 10 * per_coarse, LANES), RHS_2)], first)
+        second = from_everyone(second, outer)
         parts, _ = call(
             coarse_kernel,
             [((members, third, LANES), PART), ((rows * per_coarse, LANES), RHS_2)],
@@ -316,11 +391,12 @@
             high,
             low,
         )
+        (local_part,) = call(local_kernel, [((slots, LANES), F32)], local_inverse[0], scaled)
         parts = lax.all_to_all(parts, "col", 0, 0, tiled=True)
         totals = wide(parts).sum(axis=0).astype(BF16)
         above, below = pair(totals, totals, "row")
         third = 3 * own
-        left, middle, right = call(
+        parts = call(
             update_kernel,
             [((third, LANES), d) for d in (UPD_A, UPD_M, UPD_A)],
             above,
@@ -332,9 +408,11 @@
             local_part,
             gt,
         )
-        field = field + sum_rows(sum_cols(left, middle, right), UPD_B)
         if sweep + 1 < ITERS:
-            near = spread(field.astype(BF16))
+            across = across + shared_by_columns(column, *parts)
+            near = spread(across.astype(BF16))
+        else:
+            field = across[own : 2 * own] + owned_sum(*parts)
     return field, residual
 
 

time: 357 us -> 339 us (0.950)
  blocking collectives: 70.8 us -> 139 us
  starting transfers between devices: 156 us -> 108 us
  waiting for transfers between devices: 86.1 us -> 46 us
    all_to_all x0 -> x5, blocking collectives: none -> 66.1 us  [the longest x3 46.5 us: shared_by_columns(): got = lax.all_to_all(sent, 'col', 0, 0, tiled=True)]
    ppermute x20 -> x12, waiting for transfers between devices: 57 us -> 13 us  [pair(): lax.ppermute(to_previous, axis, [(i + 1, i) for i in range(count - 1)])]
    ppermute x20 -> x12, starting transfers between devices: 103 us -> 69.4 us  [pair(): lax.ppermute(to_previous, axis, [(i + 1, i) for i in range(count - 1)])]
    ppermute x20 -> x12, starting transfers between devices: 45.2 us -> 30.8 us  [pair(): lax.ppermute(to_next, axis, [(i, i + 1) for i in range(count - 1)])]
    ppermute x20 -> x12, waiting for transfers between devices: 16.2 us -> 20.6 us  [pair(): lax.ppermute(to_next, axis, [(i, i + 1) for i in range(count - 1)])]
    pallas_call x15 -> x23, Pallas kernels: 23.3 us -> 25.3 us  [call(): pl.pallas_call(kernel, out_shape=tuple((jax.ShapeDtypeStruct(s, d) for s,...]
    unnamed x77 -> x81, local copies, waits for them, and re-layouts: 6.6 us -> 7.32 us
  transfers between devices with their start and end apart: 41 -> 25, of which waited for: 31 -> 17; matrix products, arithmetic and copies ran while one was open for 1% -> 2% of each run, Pallas kernels for 1% -> 1%
where the time goes in v2:
time: 339 us; the launch traced here: 337 us
  blocking collectives  139 us (41%)
  starting transfers between devices  108 us (32%)
  waiting for transfers between devices  46 us (14%)
  Pallas kernels  25.3 us (7%)
  local copies, waits for them, and re-layouts  9.89 us (3%)
  other arithmetic  7.26 us (2%)
    ppermute x12, starting transfers between devices, pair(): lax.ppermute(to_previous, axis, [(i + 1, i) for i in range(count - 1)])  69.4 us
    all_to_all x3, blocking collectives, from_everyone(): lax.all_to_all(copies, 'row', 0, 0, axis_index_groups=groups, tiled=True)  50.3 us
    all_to_all x3, blocking collectives, shared_by_columns(): got = lax.all_to_all(sent, 'col', 0, 0, tiled=True)  46.5 us
    ppermute x12, starting transfers between devices, pair(): lax.ppermute(to_next, axis, [(i, i + 1) for i in range(count - 1)])  30.8 us
    pallas_call x23, Pallas kernels, call(): pl.pallas_call(kernel, out_shape=tuple((jax.ShapeDtypeStruct(s, d) for s,...  25.3 us
    all_to_all x2, blocking collectives, body(): parts = lax.all_to_all(parts, 'col', 0, 0, tiled=True)  22.2 us
    ppermute x12, waiting for transfers between devices, pair(): lax.ppermute(to_next, axis, [(i, i + 1) for i in range(count - 1)])  20.6 us
    all_to_all x2, blocking collectives, body(): got = lax.all_to_all(sent, 'col', 0, 0, tiled=True)  19.6 us
  transfers between devices with their start and end apart: 25, of which 17 were waited for; matrix products, arithmetic and copies ran while one was open for 2% of the time, Pallas kernels for 1%

profile of v2, /device:TPU:14, one launch (start us, length us, event | category | flops | bytes accessed | tf_op | source)
XLA Modules:
  0.0 337.0 jit_solution(6351287612353440703)
XLA Ops:
  0.7 4.3 %collective-permute-start = (f32[192,128]{1,0:T(8,128)}, f32[192,128]{1,0:T(8,128)S(1)}, u32[]{:S(2)}, u32[]{:S(2)}) collective-permute-start(f32[192,128]{1,0:T(8,128)} %param.13), channel_id=1, source_target_pairs={{0,1},{1,2},{2,3},{3,4},{4,5},{5,6},{6,7},{8,9},{9,10},{10,11},{11... | collective-permute-start | bytes 294920 | tf_op jit(solution)/shard_map/ppermute | solution.py:45
  15.8 7.9 %collective-permute-start.3 = (bf16[576,128]{1,0:T(8,128)(2,1)S(1)}, bf16[576,128]{1,0:T(8,128)(2,1)S(1)}, u32[]{:S(2)}, u32[]{:S(2)}) collective-permute-start(bf16[576,128]{1,0:T(8,128)(2,1)S(1)} %convert_element_type.24.win_m), channel_id=1, source_target_pairs={{8,0},{16,8},{24,16},{32,24},{40,32},{48,40},{56,48},{64,56},{72,6... | collective-permute-start | bytes 442376 | tf_op jit(solution)/shard_map/ppermute | solution.py:46
  23.8 2.9 shard_map.104
  26.8 5.2 %shard_map.105 = (bf16[576,128]{1,0:T(8,128)(2,1)S(1)}, f32[576,128]{1,0:T(8,128)S(1)}, bf16[576,128]{1,0:T(8,128)(2,1)S(1)}) custom-call(bf16[576,128]{1,0:T(8,128)(2,1)S(1)} %collective-permute-done.2.win_l, bf16[576,128]{1,0:T(8,128)(2,1)S(1)} %convert_element_type.24.win_m, bf16[576,128]{1,0:T(8,128)(2,1)S(1)} %collective-permute-done.3.win_r, ...), custom_call_target="tpu_custom_call" | custom-call | tf_op jit(solution)/shard_map/pallas_call | solution.py:27
  32.3 4.0 %collective-permute-start.4 = (bf16[600,128]{1,0:T(8,128)(2,1)S(1)}, bf16[600,128]{1,0:T(8,128)(2,1)S(1)}, u32[]{:S(2)}, u32[]{:S(2)}) collective-permute-start(bf16[600,128]{1,0:T(8,128)(2,1)S(1)} %get-tuple-element.90), channel_id=1, source_target_pairs={{0,8},{8,16},{16,24},{24,32},{32,40},{40,48},{48,56},{56,64},{64,7... | collective-permute-start | bytes 460808 | tf_op jit(solution)/shard_map/ppermute | solution.py:45
  36.3 4.6 %collective-permute-start.5 = (bf16[600,128]{1,0:T(8,128)(2,1)S(1)}, bf16[600,128]{1,0:T(8,128)(2,1)S(1)}, u32[]{:S(2)}, u32[]{:S(2)}) collective-permute-start(bf16[600,128]{1,0:T(8,128)(2,1)S(1)} %get-tuple-element.89), channel_id=1, source_target_pairs={{8,0},{16,8},{24,16},{32,24},{40,32},{48,40},{56,48},{64,56},{72,6... | collective-permute-start | bytes 460808 | tf_op jit(solution)/shard_map/ppermute | solution.py:46
  43.8 15.9 %all_to_all.55.got = bf16[8,400,128]{2,1,0:T(8,128)(2,1)S(1)} all-to-all(bf16[8,400,128]{2,1,0:T(8,128)(2,1)S(1)} %get-tuple-element.42), channel_id=1, replica_groups=mesh['row'=64,'col'=8] {'col'}, dimensions={0} | all-to-all | bytes 1638400 | tf_op jit(solution)/shard_map/all_to_all | solution.py:75
  59.7 3.6 %collective-permute-start.6 = (f32[600,128]{1,0:T(8,128)S(1)}, f32[600,128]{1,0:T(8,128)S(1)}, u32[]{:S(2)}, u32[]{:S(2)}) collective-permute-start(f32[600,128]{1,0:T(8,128)S(1)} %shard_map.107), channel_id=1, source_target_pairs={{0,8},{8,16},{16,24},{24,32},{32,40},{40,48},{48,56},{56,64},{64,7... | collective-permute-start | bytes 921608 | tf_op jit(solution)/shard_map/ppermute | solution.py:45
  63.4 4.9 %collective-permute-start.7 = (f32[600,128]{1,0:T(8,128)S(1)}, f32[600,128]{1,0:T(8,128)S(1)}, u32[]{:S(2)}, u32[]{:S(2)}) collective-permute-start(f32[600,128]{1,0:T(8,128)S(1)} %shard_map.107), channel_id=1, source_target_pairs={{8,0},{16,8},{24,16},{32,24},{40,32},{48,40},{56,48},{64,56},{72,6... | collective-permute-start | bytes 921608 | tf_op jit(solution)/shard_map/ppermute | solution.py:46
  68.4 5.4 %collective-permute-done.6 = f32[600,128]{1,0:T(8,128)S(1)} collective-permute-done((f32[600,128]{1,0:T(8,128)S(1)}, f32[600,128]{1,0:T(8,128)S(1)}, u32[]{:S(2)}, u32[]{:S(2)}) %collective-permute-start.6) | collective-permute-done | bytes 307232 | tf_op jit(solution)/shard_map/ppermute | solution.py:45
  78.6 9.4 %all_to_all.56.got = bf16[8,72,128]{2,1,0:T(8,128)(2,1)S(1)} all-to-all(bf16[8,72,128]{2,1,0:T(8,128)(2,1)S(1)} %get-tuple-element.46), channel_id=1, replica_groups=mesh['row'=64,'col'=8] {'col'}, dimensions={0} | all-to-all | bytes 294912 | tf_op jit(solution)/shard_map/all_to_all | solution.py:382
  88.0 17.2 %all_to_all.57.blocks = bf16[8,72,128]{2,1,0:T(8,128)(2,1)S(1)} all-to-all(bf16[8,72,128]{2,1,0:T(8,128)(2,1)S(1)} %shard_map.110), channel_id=1, replica_groups={{0,8,16,24,32,40,48,56},{64,72,80,88,96,104,112,120},{128,136,144,152,1..., dimensions={0} | all-to-all | bytes 294912 | tf_op jit(solution)/shard_map/all_to_all | solution.py:51
  106.1 7.5 %all-to-all-start.3 = ((bf16[8,240,128]{2,1,0:T(8,128)(2,1)}), bf16[8,240,128]{2,1,0:T(8,128)(2,1)S(1)}, u32[]{:S(2)}, u32[]{:S(2)}) async-start(bf16[8,240,128]{2,1,0:T(8,128)(2,1)} %shard_map.111), calls=%async_computation.3 | async-start | bytes 983040 | tf_op jit(solution)/shard_map/all_to_all | solution.py:51
  115.5 12.4 %all-to-all-done.3.blocks = bf16[8,240,128]{2,1,0:T(8,128)(2,1)S(1)} async-done(((bf16[8,240,128]{2,1,0:T(8,128)(2,1)}), bf16[8,240,128]{2,1,0:T(8,128)(2,1)S(1)}, u32[]{:S(2)}, u32[]{:S(2)}) %all-to-all-start.3) | async-done | bytes 491552 | tf_op jit(solution)/shard_map/all_to_all | solution.py:51
  130.7 11.2 %all_to_all.58 = f32[8,72,128]{2,1,0:T(8,128)} all-to-all(f32[8,72,128]{2,1,0:T(8,128)S(1)} %get-tuple-element.50), channel_id=1, replica_groups=mesh['row'=64,'col'=8] {'col'}, dimensions={0} | all-to-all | bytes 589824 | tf_op jit(solution)/shard_map/all_to_all | solution.py:395
  144.8 6.7 %collective-permute-start.9 = (bf16[72,128]{1,0:T(8,128)(2,1)S(1)}, bf16[72,128]{1,0:T(8,128)(2,1)S(1)}, u32[]{:S(2)}, u32[]{:S(2)}) collective-permute-start(bf16[72,128]{1,0:T(8,128)(2,1)S(1)} %reduce_sum.18.sol_m), channel_id=1, source_target_pairs={{8,0},{16,8},{24,16},{32,24},{40,32},{48,40},{56,48},{64,56},{72,6... | collective-permute-start | bytes 55304 | tf_op jit(solution)/shard_map/ppermute | solution.py:46
  156.7 6.7 %collective-permute-start.11 = (bf16[576,128]{1,0:T(8,128)(2,1)S(1)}, bf16[576,128]{1,0:T(8,128)(2,1)S(1)}, u32[]{:S(2)}, u32[]{:S(2)}) collective-permute-start(bf16[576,128]{1,0:T(8,128)(2,1)S(1)} %get-tuple-element.55), channel_id=1, source_target_pairs={{8,0},{16,8},{24,16},{32,24},{40,32},{48,40},{56,48},{64,56},{72,6... | collective-permute-start | bytes 442376 | tf_op jit(solution)/shard_map/ppermute | solution.py:46
  166.5 14.9 %all_to_all.59.got = bf16[8,384,128]{2,1,0:T(8,128)(2,1)S(1)} all-to-all(bf16[8,384,128]{2,1,0:T(8,128)(2,1)S(1)} %get-tuple-element.56), channel_id=1, replica_groups=mesh['row'=64,'col'=8] {'col'}, dimensions={0} | all-to-all | bytes 1572864 | tf_op jit(solution)/shard_map/all_to_all | solution.py:75
  184.2 6.7 %collective-permute-start.13 = (bf16[576,128]{1,0:T(8,128)(2,1)S(1)}, bf16[576,128]{1,0:T(8,128)(2,1)S(1)}, u32[]{:S(2)}, u32[]{:S(2)}) collective-permute-start(bf16[576,128]{1,0:T(8,128)(2,1)S(1)} %get-tuple-element.70.win_m), channel_id=1, source_target_pairs={{8,0},{16,8},{24,16},{32,24},{40,32},{48,40},{56,48},{64,56},{72,6... | collective-permute-start | bytes 442376 | tf_op jit(solution)/shard_map/ppermute | solution.py:46
  193.5 4.3 %shard_map.118 = (bf16[576,128]{1,0:T(8,128)(2,1)S(1)}, f32[576,128]{1,0:T(8,128)S(1)}, bf16[576,128]{1,0:T(8,128)(2,1)S(1)}) custom-call(bf16[576,128]{1,0:T(8,128)(2,1)S(1)} %collective-permute-done.12.win_l, bf16[576,128]{1,0:T(8,128)(2,1)S(1)} %get-tuple-element.70.win_m, bf16[576,128]{1,0:T(8,128)(2,1)S(1)} %collective-permute-done.13.win_r, ...), custom_call_target="tpu_custom_call" | custom-call | tf_op jit(solution)/shard_map/pallas_call | solution.py:27
  199.7 7.8 %collective-permute-start.15 = (bf16[576,128]{1,0:T(8,128)(2,1)S(1)}, bf16[576,128]{1,0:T(8,128)(2,1)S(1)}, u32[]{:S(2)}, u32[]{:S(2)}) collective-permute-start(bf16[576,128]{1,0:T(8,128)(2,1)S(1)} %get-tuple-element.60), channel_id=1, source_target_pairs={{8,0},{16,8},{24,16},{32,24},{40,32},{48,40},{56,48},{64,56},{72,6... | collective-permute-start | bytes 442376 | tf_op jit(solution)/shard_map/ppermute | solution.py:46
  210.2 15.7 %all_to_all.60.got = bf16[8,384,128]{2,1,0:T(8,128)(2,1)S(1)} all-to-all(bf16[8,384,128]{2,1,0:T(8,128)(2,1)S(1)} %get-tuple-element.61), channel_id=1, replica_groups=mesh['row'=64,'col'=8] {'col'}, dimensions={0} | all-to-all | bytes 1572864 | tf_op jit(solution)/shard_map/all_to_all | solution.py:75
  228.0 6.7 %collective-permute-start.17 = (f32[576,128]{1,0:T(8,128)S(1)}, f32[576,128]{1,0:T(8,128)S(1)}, u32[]{:S(2)}, u32[]{:S(2)}) collective-permute-start(f32[576,128]{1,0:T(8,128)S(1)} %shard_map.120.middle), channel_id=1, source_target_pairs={{8,0},{16,8},{24,16},{32,24},{40,32},{48,40},{56,48},{64,56},{72,6... | collective-permute-start | bytes 884744 | tf_op jit(solution)/shard_map/ppermute | solution.py:46
  234.6 5.4 %collective-permute-done.16.up = f32[576,128]{1,0:T(8,128)S(1)} collective-permute-done((f32[576,128]{1,0:T(8,128)S(1)}, f32[576,128]{1,0:T(8,128)S(1)}, u32[]{:S(2)}, u32[]{:S(2)}) %collective-permute-start.16) | collective-permute-done | bytes 294944 | tf_op jit(solution)/shard_map/ppermute | solution.py:45
  243.2 10.2 %all_to_all.61.got = bf16[8,72,128]{2,1,0:T(8,128)(2,1)S(1)} all-to-all(bf16[8,72,128]{2,1,0:T(8,128)(2,1)S(1)} %get-tuple-element.63), channel_id=1, replica_groups=mesh['row'=64,'col'=8] {'col'}, dimensions={0} | all-to-all | bytes 294912 | tf_op jit(solution)/shard_map/all_to_all | solution.py:382
  253.4 13.0 %all_to_all.62.blocks = bf16[8,72,128]{2,1,0:T(8,128)(2,1)S(1)} all-to-all(bf16[8,72,128]{2,1,0:T(8,128)(2,1)S(1)} %shard_map.122), channel_id=1, replica_groups={{0,8,16,24,32,40,48,56},{64,72,80,88,96,104,112,120},{128,136,144,152,1..., dimensions={0} | all-to-all | bytes 294912 | tf_op jit(solution)/shard_map/all_to_all | solution.py:51
  266.5 20.1 %all_to_all.63.blocks = bf16[8,240,128]{2,1,0:T(8,128)(2,1)S(1)} all-to-all(bf16[8,240,128]{2,1,0:T(8,128)(2,1)S(1)} %shard_map.123), channel_id=1, replica_groups={{0,64,128,192,256,320,384,448},{8,72,136,200,264,328,392,456},{16,80,14..., dimensions={0} | all-to-all | bytes 983040 | tf_op jit(solution)/shard_map/all_to_all | solution.py:51
  287.7 11.0 %all_to_all.64 = f32[8,72,128]{2,1,0:T(8,128)} all-to-all(f32[8,72,128]{2,1,0:T(8,128)S(1)} %get-tuple-element.65), channel_id=1, replica_groups=mesh['row'=64,'col'=8] {'col'}, dimensions={0} | all-to-all | bytes 589824 | tf_op jit(solution)/shard_map/all_to_all | solution.py:395
  301.6 6.7 %collective-permute-start.19 = (bf16[72,128]{1,0:T(8,128)(2,1)S(1)}, bf16[72,128]{1,0:T(8,128)(2,1)S(1)}, u32[]{:S(2)}, u32[]{:S(2)}) collective-permute-start(bf16[72,128]{1,0:T(8,128)(2,1)S(1)} %reduce_sum.19.sol_m), channel_id=1, source_target_pairs={{8,0},{16,8},{24,16},{32,24},{40,32},{48,40},{56,48},{64,56},{72,6... | collective-permute-start | bytes 55304 | tf_op jit(solution)/shard_map/ppermute | solution.py:46
  313.4 6.7 %collective-permute-start.21 = (bf16[576,128]{1,0:T(8,128)(2,1)S(1)}, bf16[576,128]{1,0:T(8,128)(2,1)S(1)}, u32[]{:S(2)}, u32[]{:S(2)}) collective-permute-start(bf16[576,128]{1,0:T(8,128)(2,1)S(1)} %get-tuple-element.69), channel_id=1, source_target_pairs={{8,0},{16,8},{24,16},{32,24},{40,32},{48,40},{56,48},{64,56},{72,6... | collective-permute-start | bytes 442376 | tf_op jit(solution)/shard_map/ppermute | solution.py:46
  323.2 3.5 %collective-permute-start.22 = (f32[192,128]{1,0:T(8,128)S(1)}, f32[192,128]{1,0:T(8,128)S(1)}, u32[]{:S(2)}, u32[]{:S(2)}) collective-permute-start(f32[192,128]{1,0:T(8,128)S(1)} %get-tuple-element.85), channel_id=1, source_target_pairs={{0,1},{1,2},{2,3},{3,4},{4,5},{5,6},{6,7},{8,9},{9,10},{10,11},{11... | collective-permute-start | bytes 294920 | tf_op jit(solution)/shard_map/ppermute | solution.py:45
  330.6 4.8 %collective-permute-done.23 = f32[192,128]{1,0:T(8,128)S(1)} collective-permute-done((f32[192,128]{1,0:T(8,128)S(1)}, f32[192,128]{1,0:T(8,128)S(1)}, u32[]{:S(2)}, u32[]{:S(2)}) %collective-permute-start.23) | collective-permute-done | bytes 98336 | tf_op jit(solution)/shard_map/ppermute | solution.py:46
  (163 shorter events, 67.7 us)
Async XLA Ops:
  0.7 10.9 %collective-permute-start = (f32[192,128]{1,0:T(8,128)}, f32[192,128]{1,0:T(8,128)S(1)}, u32[]{:S(2)}, u32[]{:S(2)}) collective-permute-start(f32[192,128]{1,0:T(8,128)} %param.13), channel_id=1, source_target_pairs={{0,1},{1,2},{2,3},{3,4},{4,5},{5,6},{6,7},{8,9},{9,10},{10,11},{11... | collective-permute-start | bytes 294920 | tf_op jit(solution)/shard_map/ppermute | solution.py:45
  5.0 8.8 %collective-permute-start.1 = (f32[192,128]{1,0:T(8,128)}, f32[192,128]{1,0:T(8,128)S(1)}, u32[]{:S(2)}, u32[]{:S(2)}) collective-permute-start(f32[192,128]{1,0:T(8,128)} %param.13), channel_id=1, source_target_pairs={{1,0},{2,1},{3,2},{4,3},{5,4},{6,5},{7,6},{9,8},{10,9},{11,10},{12... | collective-permute-start | bytes 294920 | tf_op jit(solution)/shard_map/ppermute | solution.py:46
  13.9 12.9 %collective-permute-start.2 = (bf16[576,128]{1,0:T(8,128)(2,1)S(1)}, bf16[576,128]{1,0:T(8,128)(2,1)S(1)}, u32[]{:S(2)}, u32[]{:S(2)}) collective-permute-start(bf16[576,128]{1,0:T(8,128)(2,1)S(1)} %convert_element_type.24.win_m), channel_id=1, source_target_pairs={{0,8},{8,16},{16,24},{24,32},{32,40},{40,48},{48,56},{56,64},{64,7... | collective-permute-start | bytes 442376 | tf_op jit(solution)/shard_map/ppermute | solution.py:45
  15.8 11.0 %collective-permute-start.3 = (bf16[576,128]{1,0:T(8,128)(2,1)S(1)}, bf16[576,128]{1,0:T(8,128)(2,1)S(1)}, u32[]{:S(2)}, u32[]{:S(2)}) collective-permute-start(bf16[576,128]{1,0:T(8,128)(2,1)S(1)} %convert_element_type.24.win_m), channel_id=1, source_target_pairs={{8,0},{16,8},{24,16},{32,24},{40,32},{48,40},{56,48},{64,56},{72,6... | collective-permute-start | bytes 442376 | tf_op jit(solution)/shard_map/ppermute | solution.py:46
  26.7 49.1 %copy-start.18 = (bf16[64,768]{1,0:T(8,128)(2,1)}, bf16[64,768]{1,0:T(8,128)(2,1)S(1)}, u32[]{:S(2)}) copy-start(bf16[64,768]{1,0:T(8,128)(2,1)S(1)} %get-tuple-element.44.basis_t) | copy-start | bytes 294916
  26.8 49.1 %copy-start.20 = (bf16[216,64]{1,0:T(8,128)(2,1)}, bf16[216,64]{1,0:T(8,128)(2,1)S(1)}, u32[]{:S(2)}) copy-start(bf16[216,64]{1,0:T(8,128)(2,1)S(1)} %get-tuple-element.45.cs) | copy-start | bytes 82948
  32.3 10.8 %collective-permute-start.4 = (bf16[600,128]{1,0:T(8,128)(2,1)S(1)}, bf16[600,128]{1,0:T(8,128)(2,1)S(1)}, u32[]{:S(2)}, u32[]{:S(2)}) collective-permute-start(bf16[600,128]{1,0:T(8,128)(2,1)S(1)} %get-tuple-element.90), channel_id=1, source_target_pairs={{0,8},{8,16},{16,24},{24,32},{32,40},{40,48},{48,56},{56,64},{64,7... | collective-permute-start | bytes 460808 | tf_op jit(solution)/shard_map/ppermute | solution.py:45
  36.3 7.5 %collective-permute-start.5 = (bf16[600,128]{1,0:T(8,128)(2,1)S(1)}, bf16[600,128]{1,0:T(8,128)(2,1)S(1)}, u32[]{:S(2)}, u32[]{:S(2)}) collective-permute-start(bf16[600,128]{1,0:T(8,128)(2,1)S(1)} %get-tuple-element.89), channel_id=1, source_target_pairs={{8,0},{16,8},{24,16},{32,24},{40,32},{48,40},{56,48},{64,56},{72,6... | collective-permute-start | bytes 460808 | tf_op jit(solution)/shard_map/ppermute | solution.py:46
  59.7 14.0 %collective-permute-start.6 = (f32[600,128]{1,0:T(8,128)S(1)}, f32[600,128]{1,0:T(8,128)S(1)}, u32[]{:S(2)}, u32[]{:S(2)}) collective-permute-start(f32[600,128]{1,0:T(8,128)S(1)} %shard_map.107), channel_id=1, source_target_pairs={{0,8},{8,16},{16,24},{24,32},{32,40},{40,48},{48,56},{56,64},{64,7... | collective-permute-start | bytes 921608 | tf_op jit(solution)/shard_map/ppermute | solution.py:45
  63.4 11.4 %collective-permute-start.7 = (f32[600,128]{1,0:T(8,128)S(1)}, f32[600,128]{1,0:T(8,128)S(1)}, u32[]{:S(2)}, u32[]{:S(2)}) collective-permute-start(f32[600,128]{1,0:T(8,128)S(1)} %shard_map.107), channel_id=1, source_target_pairs={{8,0},{16,8},{24,16},{32,24},{40,32},{48,40},{56,48},{64,56},{72,6... | collective-permute-start | bytes 921608 | tf_op jit(solution)/shard_map/ppermute | solution.py:46
  106.1 21.9 %all-to-all-start.3 = ((bf16[8,240,128]{2,1,0:T(8,128)(2,1)}), bf16[8,240,128]{2,1,0:T(8,128)(2,1)S(1)}, u32[]{:S(2)}, u32[]{:S(2)}) async-start(bf16[8,240,128]{2,1,0:T(8,128)(2,1)} %shard_map.111), calls=%async_computation.3 | async-start | bytes 983040 | tf_op jit(solution)/shard_map/all_to_all | solution.py:51
  142.9 10.3 %collective-permute-start.8 = (bf16[72,128]{1,0:T(8,128)(2,1)S(1)}, bf16[72,128]{1,0:T(8,128)(2,1)S(1)}, u32[]{:S(2)}, u32[]{:S(2)}) collective-permute-start(bf16[72,128]{1,0:T(8,128)(2,1)S(1)} %reduce_sum.18.sol_m), channel_id=1, source_target_pairs={{0,8},{8,16},{16,24},{24,32},{32,40},{40,48},{48,56},{56,64},{64,7... | collective-permute-start | bytes 55304 | tf_op jit(solution)/shard_map/ppermute | solution.py:45
  144.8 8.4 %collective-permute-start.9 = (bf16[72,128]{1,0:T(8,128)(2,1)S(1)}, bf16[72,128]{1,0:T(8,128)(2,1)S(1)}, u32[]{:S(2)}, u32[]{:S(2)}) collective-permute-start(bf16[72,128]{1,0:T(8,128)(2,1)S(1)} %reduce_sum.18.sol_m), channel_id=1, source_target_pairs={{8,0},{16,8},{24,16},{32,24},{40,32},{48,40},{56,48},{64,56},{72,6... | collective-permute-start | bytes 55304 | tf_op jit(solution)/shard_map/ppermute | solution.py:46
  154.7 10.2 %collective-permute-start.10 = (bf16[576,128]{1,0:T(8,128)(2,1)S(1)}, bf16[576,128]{1,0:T(8,128)(2,1)S(1)}, u32[]{:S(2)}, u32[]{:S(2)}) collective-permute-start(bf16[576,128]{1,0:T(8,128)(2,1)S(1)} %get-tuple-element.53), channel_id=1, source_target_pairs={{0,8},{8,16},{16,24},{24,32},{32,40},{40,48},{48,56},{56,64},{64,7... | collective-permute-start | bytes 442376 | tf_op jit(solution)/shard_map/ppermute | solution.py:45
  156.7 9.8 %collective-permute-start.11 = (bf16[576,128]{1,0:T(8,128)(2,1)S(1)}, bf16[576,128]{1,0:T(8,128)(2,1)S(1)}, u32[]{:S(2)}, u32[]{:S(2)}) collective-permute-start(bf16[576,128]{1,0:T(8,128)(2,1)S(1)} %get-tuple-element.55), channel_id=1, source_target_pairs={{8,0},{16,8},{24,16},{32,24},{40,32},{48,40},{56,48},{64,56},{72,6... | collective-permute-start | bytes 442376 | tf_op jit(solution)/shard_map/ppermute | solution.py:46
  182.3 10.7 %collective-permute-start.12 = (bf16[576,128]{1,0:T(8,128)(2,1)S(1)}, bf16[576,128]{1,0:T(8,128)(2,1)S(1)}, u32[]{:S(2)}, u32[]{:S(2)}) collective-permute-start(bf16[576,128]{1,0:T(8,128)(2,1)S(1)} %get-tuple-element.70.win_m), channel_id=1, source_target_pairs={{0,8},{8,16},{16,24},{24,32},{32,40},{40,48},{48,56},{56,64},{64,7... | collective-permute-start | bytes 442376 | tf_op jit(solution)/shard_map/ppermute | solution.py:45
  184.2 9.3 %collective-permute-start.13 = (bf16[576,128]{1,0:T(8,128)(2,1)S(1)}, bf16[576,128]{1,0:T(8,128)(2,1)S(1)}, u32[]{:S(2)}, u32[]{:S(2)}) collective-permute-start(bf16[576,128]{1,0:T(8,128)(2,1)S(1)} %get-tuple-element.70.win_m), channel_id=1, source_target_pairs={{8,0},{16,8},{24,16},{32,24},{40,32},{48,40},{56,48},{64,56},{72,6... | collective-permute-start | bytes 442376 | tf_op jit(solution)/shard_map/ppermute | solution.py:46
  197.8 11.9 %collective-permute-start.14 = (bf16[576,128]{1,0:T(8,128)(2,1)S(1)}, bf16[576,128]{1,0:T(8,128)(2,1)S(1)}, u32[]{:S(2)}, u32[]{:S(2)}) collective-permute-start(bf16[576,128]{1,0:T(8,128)(2,1)S(1)} %get-tuple-element.58), channel_id=1, source_target_pairs={{0,8},{8,16},{16,24},{24,32},{32,40},{40,48},{48,56},{56,64},{64,7... | collective-permute-start | bytes 442376 | tf_op jit(solution)/shard_map/ppermute | solution.py:45
  199.7 10.4 %collective-permute-start.15 = (bf16[576,128]{1,0:T(8,128)(2,1)S(1)}, bf16[576,128]{1,0:T(8,128)(2,1)S(1)}, u32[]{:S(2)}, u32[]{:S(2)}) collective-permute-start(bf16[576,128]{1,0:T(8,128)(2,1)S(1)} %get-tuple-element.60), channel_id=1, source_target_pairs={{8,0},{16,8},{24,16},{32,24},{40,32},{48,40},{56,48},{64,56},{72,6... | collective-permute-start | bytes 442376 | tf_op jit(solution)/shard_map/ppermute | solution.py:46
  210.2 30.2 %copy-start.1 = (bf16[768,1728]{1,0:T(8,128)(2,1)S(1)}, bf16[768,1728]{1,0:T(8,128)(2,1)}, u32[]{:S(2)}) copy-start(bf16[768,1728]{1,0:T(8,128)(2,1)} %get-tuple-element.36.g) | copy-start | bytes 7962628
  210.2 30.2 %copy-start.19 = (bf16[64,768]{1,0:T(8,128)(2,1)S(1)}, bf16[64,768]{1,0:T(8,128)(2,1)}, u32[]{:S(2)}) copy-start(bf16[64,768]{1,0:T(8,128)(2,1)} %copy-done.18) | copy-start | bytes 294916
  210.2 30.2 %copy-start.21 = (bf16[216,64]{1,0:T(8,128)(2,1)S(1)}, bf16[216,64]{1,0:T(8,128)(2,1)}, u32[]{:S(2)}) copy-start(bf16[216,64]{1,0:T(8,128)(2,1)} %copy-done.20) | copy-start | bytes 82948
  226.0 14.0 %collective-permute-start.16 = (f32[576,128]{1,0:T(8,128)S(1)}, f32[576,128]{1,0:T(8,128)S(1)}, u32[]{:S(2)}, u32[]{:S(2)}) collective-permute-start(f32[576,128]{1,0:T(8,128)S(1)} %shard_map.120.middle), channel_id=1, source_target_pairs={{0,8},{8,16},{16,24},{24,32},{32,40},{40,48},{48,56},{56,64},{64,7... | collective-permute-start | bytes 884744 | tf_op jit(solution)/shard_map/ppermute | solution.py:45
  228.0 12.5 %collective-permute-start.17 = (f32[576,128]{1,0:T(8,128)S(1)}, f32[576,128]{1,0:T(8,128)S(1)}, u32[]{:S(2)}, u32[]{:S(2)}) collective-permute-start(f32[576,128]{1,0:T(8,128)S(1)} %shard_map.120.middle), channel_id=1, source_target_pairs={{8,0},{16,8},{24,16},{32,24},{40,32},{48,40},{56,48},{64,56},{72,6... | collective-permute-start | bytes 884744 | tf_op jit(solution)/shard_map/ppermute | solution.py:46
  243.2 43.3 %copy-start.11 = (bf16[192,1536]{1,0:T(8,128)(2,1)S(1)}, bf16[192,1536]{1,0:T(8,128)(2,1)}, u32[]{:S(2)}) copy-start(bf16[192,1536]{1,0:T(8,128)(2,1)} %copy-done.10) | copy-start | bytes 1769476
  243.2 43.3 %copy-start.13 = (bf16[192,1536]{1,0:T(8,128)(2,1)S(1)}, bf16[192,1536]{1,0:T(8,128)(2,1)}, u32[]{:S(2)}) copy-start(bf16[192,1536]{1,0:T(8,128)(2,1)} %copy-done.12) | copy-start | bytes 1769476
  299.6 10.3 %collective-permute-start.18 = (bf16[72,128]{1,0:T(8,128)(2,1)S(1)}, bf16[72,128]{1,0:T(8,128)(2,1)S(1)}, u32[]{:S(2)}, u32[]{:S(2)}) collective-permute-start(bf16[72,128]{1,0:T(8,128)(2,1)S(1)} %reduce_sum.19.sol_m), channel_id=1, source_target_pairs={{0,8},{8,16},{16,24},{24,32},{32,40},{40,48},{48,56},{56,64},{64,7... | collective-permute-start | bytes 55304 | tf_op jit(solution)/shard_map/ppermute | solution.py:45
  301.6 8.4 %collective-permute-start.19 = (bf16[72,128]{1,0:T(8,128)(2,1)S(1)}, bf16[72,128]{1,0:T(8,128)(2,1)S(1)}, u32[]{:S(2)}, u32[]{:S(2)}) collective-permute-start(bf16[72,128]{1,0:T(8,128)(2,1)S(1)} %reduce_sum.19.sol_m), channel_id=1, source_target_pairs={{8,0},{16,8},{24,16},{32,24},{40,32},{48,40},{56,48},{64,56},{72,6... | collective-permute-start | bytes 55304 | tf_op jit(solution)/shard_map/ppermute | solution.py:46
  311.4 10.2 %collective-permute-start.20 = (bf16[576,128]{1,0:T(8,128)(2,1)S(1)}, bf16[576,128]{1,0:T(8,128)(2,1)S(1)}, u32[]{:S(2)}, u32[]{:S(2)}) collective-permute-start(bf16[576,128]{1,0:T(8,128)(2,1)S(1)} %get-tuple-element.68), channel_id=1, source_target_pairs={{0,8},{8,16},{16,24},{24,32},{32,40},{40,48},{48,56},{56,64},{64,7... | collective-permute-start | bytes 442376 | tf_op jit(solution)/shard_map/ppermute | solution.py:45
  313.4 9.8 %collective-permute-start.21 = (bf16[576,128]{1,0:T(8,128)(2,1)S(1)}, bf16[576,128]{1,0:T(8,128)(2,1)S(1)}, u32[]{:S(2)}, u32[]{:S(2)}) collective-permute-start(bf16[576,128]{1,0:T(8,128)(2,1)S(1)} %get-tuple-element.69), channel_id=1, source_target_pairs={{8,0},{16,8},{24,16},{32,24},{40,32},{48,40},{56,48},{64,56},{72,6... | collective-permute-start | bytes 442376 | tf_op jit(solution)/shard_map/ppermute | solution.py:46
  323.2 7.4 %collective-permute-start.22 = (f32[192,128]{1,0:T(8,128)S(1)}, f32[192,128]{1,0:T(8,128)S(1)}, u32[]{:S(2)}, u32[]{:S(2)}) collective-permute-start(f32[192,128]{1,0:T(8,128)S(1)} %get-tuple-element.85), channel_id=1, source_target_pairs={{0,1},{1,2},{2,3},{3,4},{4,5},{5,6},{6,7},{8,9},{9,10},{10,11},{11... | collective-permute-start | bytes 294920 | tf_op jit(solution)/shard_map/ppermute | solution.py:45
  326.8 8.6 %collective-permute-start.23 = (f32[192,128]{1,0:T(8,128)S(1)}, f32[192,128]{1,0:T(8,128)S(1)}, u32[]{:S(2)}, u32[]{:S(2)}) collective-permute-start(f32[192,128]{1,0:T(8,128)S(1)} %get-tuple-element.86), channel_id=1, source_target_pairs={{1,0},{2,1},{3,2},{4,3},{5,4},{6,5},{7,6},{9,8},{10,9},{11,10},{12... | collective-permute-start | bytes 294920 | tf_op jit(solution)/shard_map/ppermute | solution.py:46
  (22 other events, 234.8 us)

commit v3 on v2

--- a/solution.py
+++ b/solution.py
@@ -9,17 +9,16 @@
 LANES = 128
 F32 = jnp.float32
 BF16 = jnp.bfloat16
-RES_A, RES_M, RES_B, RES_H = BF16, F32, F32, F32
-COARSE_A, COARSE_M = BF16, F32
+RES_A, RES_M, RES_H = BF16, F32, F32
 UPD_A, UPD_M, UPD_B = BF16, F32, F32
-RHS_1, RHS_2, PART = BF16, BF16, F32
+PART = F32
 
 
 def dot(a, b):
     return jnp.dot(a, b, preferred_element_type=F32)
 
 
-def call(kernel, outs, *args, scalar=None):
+def call(kernel, outs, *args, scalar=None, scratch=()):
     specs = [pl.BlockSpec(memory_space=pltpu.VMEM)] * len(args)
     if scalar is not None:
         specs = [pl.BlockSpec(memory_space=pltpu.SMEM)] + specs
@@ -28,6 +27,7 @@
         kernel,
         out_shape=tuple(jax.ShapeDtypeStruct(s, d) for s, d in outs),
         in_specs=specs,
+        scratch_shapes=[pltpu.VMEM(*shape) for shape in scratch],
         compiler_params=pltpu.CompilerParams(vmem_limit_bytes=48 * 1024 * 1024),
     )(*args)
 
@@ -37,18 +37,32 @@
     owner = wanted // per_owner
     row_step = owner // members - lax.axis_index("row") + 1
     col_step = owner % members - lax.axis_index("col") + 1
-    return row_step, col_step, wanted % per_owner
-
-
-def pair(to_next, to_previous, axis):
+    return row_place(row_step), col_step, wanted % per_owner
+
+
+def pair(to_far, to_near, axis):
     count = lax.axis_size(axis)
-    from_previous = lax.ppermute(to_next, axis, [(i, i + 1) for i in range(count - 1)])
-    from_next = lax.ppermute(to_previous, axis, [(i + 1, i) for i in range(count - 1)])
+    near = [(i, i ^ 1) for i in range(count)]
+    far = [(i, i - 1 + 2 * (i % 2)) for i in range(1, count - 1)]
+    from_near = lax.ppermute(to_near, axis, near)
+    from_far = lax.ppermute(to_far, axis, far)
+    return from_near, from_far
+
+
+def shifts(to_next, to_previous):
+    count = lax.axis_size("col")
+    from_previous = lax.ppermute(to_next, "col", [(i, i + 1) for i in range(count - 1)])
+    from_next = lax.ppermute(to_previous, "col", [(i + 1, i) for i in range(count - 1)])
     return from_previous, from_next
 
 
-def from_everyone(copies, groups):
-    return lax.all_to_all(copies, "row", 0, 0, axis_index_groups=groups, tiled=True)
+def row_place(step):
+    odd = lax.axis_index("row") % 2
+    return jnp.where(odd == 0, 2 - step, step)
+
+
+def from_everyone(copies, axis, groups):
+    return lax.all_to_all(copies, axis, 0, 0, axis_index_groups=groups, tiled=True)
 
 
 def wide(a):
@@ -82,7 +96,7 @@
     summed = wide(middle) + wide(from_previous) + wide(from_next)
     third = summed.shape[0] // 3
     left, own, right = summed[:third], summed[third : 2 * third], summed[2 * third :]
-    from_previous, from_next = pair(right.astype(UPD_B), left.astype(UPD_B), "col")
+    from_previous, from_next = shifts(right.astype(UPD_B), left.astype(UPD_B))
     return own + wide(from_previous) + wide(from_next)
 
 
@@ -120,16 +134,22 @@
     out[2 * third :] = summed[2 * third :] + part(1, first) + part(2, first)
 
 
-def coarse_receive_kernel(column, got, middle, out):
-    members = got.shape[0]
-    c = column[0]
-    total = wide(middle[...])
-    for step in (-1, 1):
+def coarse_receive_kernel(place, got, kept, out):
+    members = got.shape[0] // 2
+    c, k = place[0], place[1]
+    block = kept.shape[0] // 2
+    total = kept[...]
+    first = jnp.zeros((block, LANES), F32)
+    for step in (-1, 0, 1):
         there = (c + step >= 0) & (c + step < members)
-        total = total + jnp.where(there, wide(got[nth(c, step, members)]), 0.0)
+        at = nth(c, step, members)
+        if step:
+            total = total + jnp.where(there, wide(got[k * members + at]), 0.0)
+        first = first + jnp.where(there, wide(got[(1 - k) * members + at, :block, :]), 0.0)
+    total = total + jnp.concatenate([first, jnp.zeros((block, LANES), F32)], axis=0)
     total = total.astype(out.dtype)
-    for k in range(out.shape[0]):
-        out[k] = total
+    for copy in range(out.shape[0]):
+        out[copy] = total
 
 
 def prepare_kernel(pos_col, pos_row, coarse_col, coarse_row, out_col, basis, g, gt, cs, og, basis_t, counts):
@@ -215,56 +235,48 @@
 OWN_OF = {}
 
 
-def primal_kernel(column, up, middle, down, g, weight, basis_t, cs, scaled, sent, kept):
+def primal_kernel(place, up, middle, down, g, weight, basis_t, cs, scaled, sent, kept):
     rows = gathered(g, up[...], middle[...], down[...])
     values = (weight[...] * rows).astype(BF16)
     scaled[...] = values
     primal = dot(basis_t[...], values)
-    third = kept.shape[0]
-    members = sent.shape[0]
-    c = column[0]
+    block = kept.shape[0] // 2
+    third = 3 * block
+    members = sent.shape[0] // 2
+    c, k = place[0], place[1]
     high = primal.astype(BF16)
     low = (primal - wide(high)).astype(BF16)
-    sent[nth(c, -1, members)] = dot(cs[:third], high).astype(sent.dtype)
-    sent[nth(c, 1, members)] = dot(cs[2 * third :], high).astype(sent.dtype)
-    rows = cs[third : 2 * third]
-    kept[...] = dot(rows, high) + dot(rows, low)
+    for step in (-1, 0, 1):
+        rows = cs[(step + 1) * third : (step + 2) * third]
+        placed = dot(rows, high)
+        at = nth(c, step, members)
+        sent[(1 - k) * members + at, :block, :] = placed[:block].astype(BF16)
+        if step:
+            sent[k * members + at] = placed[block:].astype(BF16)
+        else:
+            kept[...] = (placed + dot(rows, low))[block:]
 
 
 def local_kernel(local_inverse, scaled, out):
     out[...] = dot(local_inverse[...], scaled[...])
 
 
-def fold_kernel(blocks, out):
-    count = blocks.shape[0]
-    third = blocks.shape[1] // 3
-    for row in range(-1, count + 1):
-        total = None
-        for k in range(max(row - 1, 0), min(row + 1, count - 1) + 1):
-            part = wide(blocks[k, (row - k + 1) * third : (row - k + 2) * third, :])
-            total = part if total is None else total + part
-        total = total.astype(out.dtype)
-        for copy in range(out.shape[0]):
-            out[copy, (row + 1) * third : (row + 2) * third, :] = total
-
-
-def coarse_kernel(blocks, high, low, out, rhs):
-    groups = blocks.shape[0]
-    third = blocks.shape[1] // 10
-    for y in range(groups):
-        base = y * 8 * third
-        rhs[base : base + 8 * third, :] = blocks[y, third : 9 * third, :]
-        if y > 0:
-            first = wide(blocks[y, third : 2 * third, :]) + wide(blocks[y - 1, 9 * third :, :])
-            rhs[base : base + third, :] = first.astype(rhs.dtype)
-        if y + 1 < groups:
-            last = wide(blocks[y, 8 * third : 9 * third, :]) + wide(blocks[y + 1, :third, :])
-            rhs[base + 7 * third : base + 8 * third, :] = last.astype(rhs.dtype)
+def coarse_kernel(halves, high, low, out, rhs):
+    pairs = halves.shape[1]
+    third = halves.shape[2] // 2
+    for j in range(pairs):
+        own = wide(halves[0, j, :third, :])
+        if j > 0:
+            own = own + wide(halves[1, j - 1, third:, :])
+        rhs[2 * j * third : (2 * j + 1) * third, :] = own
+        own = wide(halves[1, j, :third, :])
+        if j + 1 < pairs:
+            own = own + wide(halves[0, j + 1, third:, :])
+        rhs[(2 * j + 1) * third : (2 * j + 2) * third, :] = own
     values = rhs[...]
     top = values.astype(BF16)
-    part = dot(high[...], top) + dot(low[...], top)
-    if rhs.dtype == F32:
-        part = part + dot(high[...], (values - wide(top)).astype(BF16))
+    rest = (values - wide(top)).astype(BF16)
+    part = dot(high[...], top) + dot(low[...], top) + dot(high[...], rest)
     part = part.astype(out.dtype)
     members = out.shape[0]
     for c in range(members):
@@ -296,12 +308,12 @@
     rows = lax.axis_size("row")
     members = lax.axis_size("col")
     window, coarse_window = 9 * own, 9 * per_coarse
-    inner = [[8 * y + k for k in range(8)] for y in range(rows // 8)]
-    outer = [[8 * y + k for y in range(rows // 8)] for k in range(8)]
-    halves = -(-own // LANES)
+    tiles = [[2 * members * j + m for m in range(2 * members)] for j in range(rows // 2)]
+    sides = [[2 * j + k for j in range(rows // 2)] for k in range(2)]
+    chips = [[2 * j, 2 * j + 1] for j in range(rows // 2)]
     OWN_OF[72] = own
 
-    column = lax.axis_index("col").astype(jnp.int32).reshape(1)
+    column = jnp.stack([lax.axis_index("col"), lax.axis_index("row") % 2]).astype(jnp.int32)
 
     active = jnp.arange(slots, dtype=jnp.int32) < sizes[0]
     row_step, col_step, inside = window_positions(dof_ids[0], own)
@@ -311,7 +323,7 @@
     coarse_out = (row_step * 3 + col_step) * per_coarse + inside
     basis = averaging_basis[0]
 
-    left, right = pair(start, start, "col")
+    left, right = shifts(start, start)
     across = jnp.concatenate([left, start, right], axis=0)
     near = spread(across.astype(BF16))
 
@@ -368,10 +380,13 @@
                 jnp.concatenate([n[k * step : k * step + own] for k in range(3)], axis=0) for n in near
             )
             (weight,) = call(weight_kernel, [((slots, LANES), F32)], shared, positions[:, None])
-        third = 3 * per_coarse
         scaled, sent, kept = call(
             primal_kernel,
-            [((slots, LANES), BF16), ((members, third, LANES), COARSE_A), ((third, LANES), F32)],
+            [
+                ((slots, LANES), BF16),
+                ((2 * members, 2 * per_coarse, LANES), BF16),
+                ((2 * per_coarse, LANES), F32),
+            ],
             *near,
             g,
             weight,
@@ -379,17 +394,20 @@
             cs,
             scalar=column,
         )
-        got = lax.all_to_all(sent, "col", 0, 0, tiled=True)
-        (first,) = call(coarse_receive_kernel, [((8, third, LANES), RHS_1)], got, kept, scalar=column)
-        first = from_everyone(first, inner)
-        (second,) = call(fold_kernel, [((rows // 8, 10 * per_coarse, LANES), RHS_2)], first)
-        second = from_everyone(second, outer)
-        parts, _ = call(
+        got = from_everyone(sent, ("row", "col"), tiles)
+        (held,) = call(
+            coarse_receive_kernel, [((rows // 2, 2 * per_coarse, LANES), BF16)], got, kept, scalar=column
+        )
+        side = from_everyone(held, "row", sides)
+        both = from_everyone(jnp.broadcast_to(side[None], (2, *side.shape)), "row", chips)
+        third = 3 * per_coarse
+        (parts,) = call(
             coarse_kernel,
-            [((members, third, LANES), PART), ((rows * per_coarse, LANES), RHS_2)],
-            second,
+            [((members, third, LANES), PART)],
+            both,
             high,
             low,
+            scratch=[((rows * per_coarse, LANES), F32)],
         )
         (local_part,) = call(local_kernel, [((slots, LANES), F32)], local_inverse[0], scaled)
         parts = lax.all_to_all(parts, "col", 0, 0, tiled=True)

time: 339 us -> 342 us (level)
  waiting for transfers between devices: 46 us -> 84.6 us
  starting transfers between devices: 108 us -> 84.6 us
  blocking collectives: 139 us -> 124 us
  Pallas kernels: 25.3 us -> 29 us
    ppermute x24, waiting for transfers between devices: 33.6 us -> 68.2 us  [the longest x10 60.7 us: pair(): from_far = lax.ppermute(to_far, axis, far)]
    ppermute x24, starting transfers between devices: 100 us -> 73.9 us  [the longest x10 42.7 us: pair(): from_far = lax.ppermute(to_far, axis, far)]
    all_to_all x5, blocking collectives: 69.9 us -> 55.5 us  [from_everyone(): lax.all_to_all(copies, axis, 0, 0, axis_index_groups=groups, tiled=True)]
    all_to_all x1, waiting for transfers between devices: 12.4 us -> 16.4 us  [from_everyone(): lax.all_to_all(copies, axis, 0, 0, axis_index_groups=groups, tiled=True)]
    pallas_call x23 -> x21, Pallas kernels: 25.3 us -> 29 us  [call(): pl.pallas_call(kernel, out_shape=tuple((jax.ShapeDtypeStruct(s, d) for s,...]
  transfers between devices with their start and end apart: 25 -> 25, of which waited for: 17 -> 13; matrix products, arithmetic and copies ran while one was open for 2% -> 2% of each run, Pallas kernels for 1% -> 1%
where the time goes in v3:
time: 342 us; the launch traced here: 340 us
  blocking collectives  124 us (36%)
  starting transfers between devices  84.6 us (25%)
  waiting for transfers between devices  84.6 us (25%)
  Pallas kernels  29 us (8%)
  local copies, waits for them, and re-layouts  8.1 us (2%)
  other arithmetic  7.38 us (2%)
    ppermute x10, waiting for transfers between devices, pair(): from_far = lax.ppermute(to_far, axis, far)  60.7 us
    all_to_all x5, blocking collectives, from_everyone(): lax.all_to_all(copies, axis, 0, 0, axis_index_groups=groups, tiled=True)  55.5 us
    all_to_all x3, blocking collectives, shared_by_columns(): got = lax.all_to_all(sent, 'col', 0, 0, tiled=True)  44.2 us
    ppermute x10, starting transfers between devices, pair(): from_far = lax.ppermute(to_far, axis, far)  42.7 us
    pallas_call x21, Pallas kernels, call(): pl.pallas_call(kernel, out_shape=tuple((jax.ShapeDtypeStruct(s, d) for s,...  29 us
    all_to_all x2, blocking collectives, body(): parts = lax.all_to_all(parts, 'col', 0, 0, tiled=True)  24.3 us
    ppermute x10, starting transfers between devices, pair(): from_near = lax.ppermute(to_near, axis, near)  19.2 us
    all_to_all x1, waiting for transfers between devices, from_everyone(): lax.all_to_all(copies, axis, 0, 0, axis_index_groups=groups, tiled=True)  16.4 us
  transfers between devices with their start and end apart: 25, of which 13 were waited for; matrix products, arithmetic and copies ran while one was open for 2% of the time, Pallas kernels for 1%

profile of v3, /device:TPU:14, one launch (start us, length us, event | category | flops | bytes accessed | tf_op | source)
XLA Modules:
  0.0 339.9 jit_solution(18178038479308618289)
XLA Ops:
  0.7 4.3 %collective-permute-start = (f32[192,128]{1,0:T(8,128)}, f32[192,128]{1,0:T(8,128)S(1)}, u32[]{:S(2)}, u32[]{:S(2)}) collective-permute-start(f32[192,128]{1,0:T(8,128)} %param.13), channel_id=1, source_target_pairs={{0,1},{1,2},{2,3},{3,4},{4,5},{5,6},{6,7},{8,9},{9,10},{10,11},{11... | collective-permute-start | bytes 294920 | tf_op jit(solution)/shard_map/ppermute | solution.py:54
  16.5 10.0 %collective-permute-start.3 = (bf16[576,128]{1,0:T(8,128)(2,1)S(1)}, bf16[576,128]{1,0:T(8,128)(2,1)S(1)}, u32[]{:S(2)}, u32[]{:S(2)}) collective-permute-start(bf16[576,128]{1,0:T(8,128)(2,1)S(1)} %convert_element_type.24.win_m), channel_id=1, source_target_pairs={{8,16},{16,8},{24,32},{32,24},{40,48},{48,40},{56,64},{64,56},{72,... | collective-permute-start | bytes 442376 | tf_op jit(solution)/shard_map/ppermute | solution.py:48
  30.6 4.4 %shard_map.105 = (bf16[576,128]{1,0:T(8,128)(2,1)S(1)}, f32[576,128]{1,0:T(8,128)S(1)}, bf16[576,128]{1,0:T(8,128)(2,1)S(1)}) custom-call(bf16[576,128]{1,0:T(8,128)(2,1)S(1)} %collective-permute-done.2.win_l, bf16[576,128]{1,0:T(8,128)(2,1)S(1)} %convert_element_type.24.win_m, bf16[576,128]{1,0:T(8,128)(2,1)S(1)} %collective-permute-done.3.win_r, ...), custom_call_target="tpu_custom_call" | custom-call | tf_op jit(solution)/shard_map/pallas_call | solution.py:26
  37.1 6.1 %collective-permute-start.5 = (bf16[600,128]{1,0:T(8,128)(2,1)S(1)}, bf16[600,128]{1,0:T(8,128)(2,1)S(1)}, u32[]{:S(2)}, u32[]{:S(2)}) collective-permute-start(bf16[600,128]{1,0:T(8,128)(2,1)S(1)} %get-tuple-element.83), channel_id=1, source_target_pairs={{8,16},{16,8},{24,32},{32,24},{40,48},{48,40},{56,64},{64,56},{72,... | collective-permute-start | bytes 460808 | tf_op jit(solution)/shard_map/ppermute | solution.py:48
  43.3 4.8 %collective-permute-done.5.from_next = bf16[600,128]{1,0:T(8,128)(2,1)S(1)} collective-permute-done((bf16[600,128]{1,0:T(8,128)(2,1)S(1)}, bf16[600,128]{1,0:T(8,128)(2,1)S(1)}, u32[]{:S(2)}, u32[]{:S(2)}) %collective-permute-start.5) | collective-permute-done | bytes 153632 | tf_op jit(solution)/shard_map/ppermute | solution.py:48
  48.7 14.5 %all_to_all.55.got = bf16[8,400,128]{2,1,0:T(8,128)(2,1)S(1)} all-to-all(bf16[8,400,128]{2,1,0:T(8,128)(2,1)S(1)} %get-tuple-element.40), channel_id=1, replica_groups=mesh['row'=64,'col'=8] {'col'}, dimensions={0} | all-to-all | bytes 1638400 | tf_op jit(solution)/shard_map/all_to_all | solution.py:89
  65.7 6.0 %collective-permute-start.7 = (f32[600,128]{1,0:T(8,128)S(1)}, f32[600,128]{1,0:T(8,128)S(1)}, u32[]{:S(2)}, u32[]{:S(2)}) collective-permute-start(f32[600,128]{1,0:T(8,128)S(1)} %shard_map.107), channel_id=1, source_target_pairs={{8,16},{16,8},{24,32},{32,24},{40,48},{48,40},{56,64},{64,56},{72,... | collective-permute-start | bytes 921608 | tf_op jit(solution)/shard_map/ppermute | solution.py:48
  71.9 7.4 %collective-permute-done.7 = f32[600,128]{1,0:T(8,128)S(1)} collective-permute-done((f32[600,128]{1,0:T(8,128)S(1)}, f32[600,128]{1,0:T(8,128)S(1)}, u32[]{:S(2)}, u32[]{:S(2)}) %collective-permute-start.7) | collective-permute-done | bytes 307232 | tf_op jit(solution)/shard_map/ppermute | solution.py:48
  83.7 11.5 %all_to_all.56.got = bf16[16,48,128]{2,1,0:T(8,128)(2,1)S(1)} all-to-all(bf16[16,48,128]{2,1,0:T(8,128)(2,1)S(1)} %get-tuple-element.44), channel_id=1, replica_groups={{0,1,2,3,4,5,6,7,8,9,10,11,12,13,14,15},{16,17,18,19,20,21,22,23,24,25,..., dimensions={0} | all-to-all | bytes 393216 | tf_op jit(solution)/shard_map/all_to_all | solution.py:65
  96.5 10.7 %all-to-all-start.2 = ((bf16[32,48,128]{2,1,0:T(8,128)(2,1)}), bf16[32,48,128]{2,1,0:T(8,128)(2,1)}, u32[]{:S(2)}, u32[]{:S(2)}) async-start(bf16[32,48,128]{2,1,0:T(8,128)(2,1)} %shard_map.110), calls=%async_computation.2 | async-start | bytes 786432 | tf_op jit(solution)/shard_map/all_to_all | solution.py:65
  107.7 16.4 %all-to-all-done.2 = bf16[32,48,128]{2,1,0:T(8,128)(2,1)} async-done(((bf16[32,48,128]{2,1,0:T(8,128)(2,1)}), bf16[32,48,128]{2,1,0:T(8,128)(2,1)}, u32[]{:S(2)}, u32[]{:S(2)}) %all-to-all-start.2) | async-done | bytes 393248 | tf_op jit(solution)/shard_map/all_to_all | solution.py:65
  125.3 4.5 %all_to_all.57.halves = bf16[2,32,48,128]{3,2,1,0:T(8,128)(2,1)S(1)} all-to-all(bf16[2,32,48,128]{3,2,1,0:T(8,128)(2,1)S(1)} %broadcast_in_dim.6), channel_id=1, replica_groups={{0,8},{16,24},{32,40},{48,56},{64,72},{80,88},{96,104},{112,120},{128,1..., dimensions={0} | all-to-all | bytes 1572864 | tf_op jit(solution)/shard_map/all_to_all | solution.py:65
  130.5 12.3 %all_to_all.58 = f32[8,72,128]{2,1,0:T(8,128)} all-to-all(f32[8,72,128]{2,1,0:T(8,128)S(1)} %shard_map.112), channel_id=1, replica_groups=mesh['row'=64,'col'=8] {'col'}, dimensions={0} | all-to-all | bytes 589824 | tf_op jit(solution)/shard_map/all_to_all | solution.py:413
  150.4 3.3 collective-permute-done.9.sol_d
  157.1 3.1 collective-permute-start.11
  160.3 7.1 %collective-permute-done.11.from_next = bf16[576,128]{1,0:T(8,128)(2,1)S(1)} collective-permute-done((bf16[576,128]{1,0:T(8,128)(2,1)S(1)}, bf16[576,128]{1,0:T(8,128)(2,1)S(1)}, u32[]{:S(2)}, u32[]{:S(2)}) %collective-permute-start.11) | collective-permute-done | bytes 147488 | tf_op jit(solution)/shard_map/ppermute | solution.py:48
  168.0 15.1 %all_to_all.59.got = bf16[8,384,128]{2,1,0:T(8,128)(2,1)S(1)} all-to-all(bf16[8,384,128]{2,1,0:T(8,128)(2,1)S(1)} %get-tuple-element.53), channel_id=1, replica_groups=mesh['row'=64,'col'=8] {'col'}, dimensions={0} | all-to-all | bytes 1572864 | tf_op jit(solution)/shard_map/all_to_all | solution.py:89
  189.4 7.7 %collective-permute-done.13.win_r = bf16[576,128]{1,0:T(8,128)(2,1)S(1)} collective-permute-done((bf16[576,128]{1,0:T(8,128)(2,1)S(1)}, bf16[576,128]{1,0:T(8,128)(2,1)S(1)}, u32[]{:S(2)}, u32[]{:S(2)}) %collective-permute-start.13) | collective-permute-done | bytes 147488 | tf_op jit(solution)/shard_map/ppermute | solution.py:48
  197.2 4.3 %shard_map.117 = (bf16[576,128]{1,0:T(8,128)(2,1)S(1)}, f32[576,128]{1,0:T(8,128)S(1)}, bf16[576,128]{1,0:T(8,128)(2,1)S(1)}) custom-call(bf16[576,128]{1,0:T(8,128)(2,1)S(1)} %collective-permute-done.12.win_l, bf16[576,128]{1,0:T(8,128)(2,1)S(1)} %get-tuple-element.66.win_m, bf16[576,128]{1,0:T(8,128)(2,1)S(1)} %collective-permute-done.13.win_r, ...), custom_call_target="tpu_custom_call" | custom-call | tf_op jit(solution)/shard_map/pallas_call | solution.py:26
  205.4 8.6 %collective-permute-done.15.from_next = bf16[576,128]{1,0:T(8,128)(2,1)S(1)} collective-permute-done((bf16[576,128]{1,0:T(8,128)(2,1)S(1)}, bf16[576,128]{1,0:T(8,128)(2,1)S(1)}, u32[]{:S(2)}, u32[]{:S(2)}) %collective-permute-start.15) | collective-permute-done | bytes 147488 | tf_op jit(solution)/shard_map/ppermute | solution.py:48
  214.6 14.6 %all_to_all.60.got = bf16[8,384,128]{2,1,0:T(8,128)(2,1)S(1)} all-to-all(bf16[8,384,128]{2,1,0:T(8,128)(2,1)S(1)} %get-tuple-element.58), channel_id=1, replica_groups=mesh['row'=64,'col'=8] {'col'}, dimensions={0} | all-to-all | bytes 1572864 | tf_op jit(solution)/shard_map/all_to_all | solution.py:89
  231.8 3.3 collective-permute-start.17
  235.1 10.5 %collective-permute-done.17.down = f32[576,128]{1,0:T(8,128)S(1)} collective-permute-done((f32[576,128]{1,0:T(8,128)S(1)}, f32[576,128]{1,0:T(8,128)S(1)}, u32[]{:S(2)}, u32[]{:S(2)}) %collective-permute-start.17) | collective-permute-done | bytes 294944 | tf_op jit(solution)/shard_map/ppermute | solution.py:48
  248.3 10.5 %all_to_all.61.got = bf16[16,48,128]{2,1,0:T(8,128)(2,1)S(1)} all-to-all(bf16[16,48,128]{2,1,0:T(8,128)(2,1)S(1)} %get-tuple-element.60), channel_id=1, replica_groups={{0,1,2,3,4,5,6,7,8,9,10,11,12,13,14,15},{16,17,18,19,20,21,22,23,24,25,..., dimensions={0} | all-to-all | bytes 393216 | tf_op jit(solution)/shard_map/all_to_all | solution.py:65
  259.3 24.5 %all_to_all.62 = bf16[32,48,128]{2,1,0:T(8,128)(2,1)S(1)} all-to-all(bf16[32,48,128]{2,1,0:T(8,128)(2,1)S(1)} %shard_map.121), channel_id=1, replica_groups={{0,16,32,48,64,80,96,112,128,144,160,176,192,208,224,240,256,272,288,30..., dimensions={0} | all-to-all | bytes 786432 | tf_op jit(solution)/shard_map/all_to_all | solution.py:65
  284.0 4.5 %all_to_all.63.halves = bf16[2,32,48,128]{3,2,1,0:T(8,128)(2,1)S(1)} all-to-all(bf16[2,32,48,128]{3,2,1,0:T(8,128)(2,1)S(1)} %broadcast_in_dim.7), channel_id=1, replica_groups={{0,8},{16,24},{32,40},{48,56},{64,72},{80,88},{96,104},{112,120},{128,1..., dimensions={0} | all-to-all | bytes 1572864 | tf_op jit(solution)/shard_map/all_to_all | solution.py:65
  289.1 12.0 %all_to_all.64 = f32[8,72,128]{2,1,0:T(8,128)} all-to-all(f32[8,72,128]{2,1,0:T(8,128)S(1)} %shard_map.122), channel_id=1, replica_groups=mesh['row'=64,'col'=8] {'col'}, dimensions={0} | all-to-all | bytes 589824 | tf_op jit(solution)/shard_map/all_to_all | solution.py:413
  308.8 3.3 collective-permute-done.19.sol_d
  315.5 3.1 collective-permute-start.21
  318.6 7.1 %collective-permute-done.21 = bf16[576,128]{1,0:T(8,128)(2,1)S(1)} collective-permute-done((bf16[576,128]{1,0:T(8,128)(2,1)S(1)}, bf16[576,128]{1,0:T(8,128)(2,1)S(1)}, u32[]{:S(2)}, u32[]{:S(2)}) %collective-permute-start.21) | collective-permute-done | bytes 147488 | tf_op jit(solution)/shard_map/ppermute | solution.py:48
  325.8 3.9 %collective-permute-start.22 = (f32[192,128]{1,0:T(8,128)S(1)}, f32[192,128]{1,0:T(8,128)S(1)}, u32[]{:S(2)}, u32[]{:S(2)}) collective-permute-start(f32[192,128]{1,0:T(8,128)S(1)} %get-tuple-element.79), channel_id=1, source_target_pairs={{0,1},{1,2},{2,3},{3,4},{4,5},{5,6},{6,7},{8,9},{9,10},{10,11},{11... | collective-permute-start | bytes 294920 | tf_op jit(solution)/shard_map/ppermute | solution.py:54
  333.2 5.1 %collective-permute-done.23 = f32[192,128]{1,0:T(8,128)S(1)} collective-permute-done((f32[192,128]{1,0:T(8,128)S(1)}, f32[192,128]{1,0:T(8,128)S(1)}, u32[]{:S(2)}, u32[]{:S(2)}) %collective-permute-start.23) | collective-permute-done | bytes 98336 | tf_op jit(solution)/shard_map/ppermute | solution.py:55
  (164 shorter events, 73.0 us)
Async XLA Ops:
  0.7 10.7 %collective-permute-start = (f32[192,128]{1,0:T(8,128)}, f32[192,128]{1,0:T(8,128)S(1)}, u32[]{:S(2)}, u32[]{:S(2)}) collective-permute-start(f32[192,128]{1,0:T(8,128)} %param.13), channel_id=1, source_target_pairs={{0,1},{1,2},{2,3},{3,4},{4,5},{5,6},{6,7},{8,9},{9,10},{10,11},{11... | collective-permute-start | bytes 294920 | tf_op jit(solution)/shard_map/ppermute | solution.py:54
  5.0 8.8 %collective-permute-start.1 = (f32[192,128]{1,0:T(8,128)}, f32[192,128]{1,0:T(8,128)S(1)}, u32[]{:S(2)}, u32[]{:S(2)}) collective-permute-start(f32[192,128]{1,0:T(8,128)} %param.13), channel_id=1, source_target_pairs={{1,0},{2,1},{3,2},{4,3},{5,4},{6,5},{7,6},{9,8},{10,9},{11,10},{12... | collective-permute-start | bytes 294920 | tf_op jit(solution)/shard_map/ppermute | solution.py:55
  14.6 15.3 %collective-permute-start.2 = (bf16[576,128]{1,0:T(8,128)(2,1)S(1)}, bf16[576,128]{1,0:T(8,128)(2,1)S(1)}, u32[]{:S(2)}, u32[]{:S(2)}) collective-permute-start(bf16[576,128]{1,0:T(8,128)(2,1)S(1)} %convert_element_type.24.win_m), channel_id=1, source_target_pairs={{0,8},{8,0},{16,24},{24,16},{32,40},{40,32},{48,56},{56,48},{64,72... | collective-permute-start | bytes 442376 | tf_op jit(solution)/shard_map/ppermute | solution.py:47
  16.5 14.1 %collective-permute-start.3 = (bf16[576,128]{1,0:T(8,128)(2,1)S(1)}, bf16[576,128]{1,0:T(8,128)(2,1)S(1)}, u32[]{:S(2)}, u32[]{:S(2)}) collective-permute-start(bf16[576,128]{1,0:T(8,128)(2,1)S(1)} %convert_element_type.24.win_m), channel_id=1, source_target_pairs={{8,16},{16,8},{24,32},{32,24},{40,48},{48,40},{56,64},{64,56},{72,... | collective-permute-start | bytes 442376 | tf_op jit(solution)/shard_map/ppermute | solution.py:48
  29.8 50.7 %copy-start.18 = (bf16[64,768]{1,0:T(8,128)(2,1)}, bf16[64,768]{1,0:T(8,128)(2,1)S(1)}, u32[]{:S(2)}) copy-start(bf16[64,768]{1,0:T(8,128)(2,1)S(1)} %get-tuple-element.42.basis_t) | copy-start | bytes 294916
  29.8 50.7 %copy-start.20 = (bf16[216,64]{1,0:T(8,128)(2,1)}, bf16[216,64]{1,0:T(8,128)(2,1)S(1)}, u32[]{:S(2)}) copy-start(bf16[216,64]{1,0:T(8,128)(2,1)S(1)} %get-tuple-element.43.cs) | copy-start | bytes 82948
  35.2 8.0 %collective-permute-start.4 = (bf16[600,128]{1,0:T(8,128)(2,1)S(1)}, bf16[600,128]{1,0:T(8,128)(2,1)S(1)}, u32[]{:S(2)}, u32[]{:S(2)}) collective-permute-start(bf16[600,128]{1,0:T(8,128)(2,1)S(1)} %get-tuple-element.84), channel_id=1, source_target_pairs={{0,8},{8,0},{16,24},{24,16},{32,40},{40,32},{48,56},{56,48},{64,72... | collective-permute-start | bytes 460808 | tf_op jit(solution)/shard_map/ppermute | solution.py:47
  37.1 10.9 %collective-permute-start.5 = (bf16[600,128]{1,0:T(8,128)(2,1)S(1)}, bf16[600,128]{1,0:T(8,128)(2,1)S(1)}, u32[]{:S(2)}, u32[]{:S(2)}) collective-permute-start(bf16[600,128]{1,0:T(8,128)(2,1)S(1)} %get-tuple-element.83), channel_id=1, source_target_pairs={{8,16},{16,8},{24,32},{32,24},{40,48},{48,40},{56,64},{64,56},{72,... | collective-permute-start | bytes 460808 | tf_op jit(solution)/shard_map/ppermute | solution.py:48
  63.8 8.0 %collective-permute-start.6 = (f32[600,128]{1,0:T(8,128)S(1)}, f32[600,128]{1,0:T(8,128)S(1)}, u32[]{:S(2)}, u32[]{:S(2)}) collective-permute-start(f32[600,128]{1,0:T(8,128)S(1)} %shard_map.107), channel_id=1, source_target_pairs={{0,8},{8,0},{16,24},{24,16},{32,40},{40,32},{48,56},{56,48},{64,72... | collective-permute-start | bytes 921608 | tf_op jit(solution)/shard_map/ppermute | solution.py:47
  65.7 13.6 %collective-permute-start.7 = (f32[600,128]{1,0:T(8,128)S(1)}, f32[600,128]{1,0:T(8,128)S(1)}, u32[]{:S(2)}, u32[]{:S(2)}) collective-permute-start(f32[600,128]{1,0:T(8,128)S(1)} %shard_map.107), channel_id=1, source_target_pairs={{8,16},{16,8},{24,32},{32,24},{40,48},{48,40},{56,64},{64,56},{72,... | collective-permute-start | bytes 921608 | tf_op jit(solution)/shard_map/ppermute | solution.py:48
  96.5 27.6 %all-to-all-start.2 = ((bf16[32,48,128]{2,1,0:T(8,128)(2,1)}), bf16[32,48,128]{2,1,0:T(8,128)(2,1)}, u32[]{:S(2)}, u32[]{:S(2)}) async-start(bf16[32,48,128]{2,1,0:T(8,128)(2,1)} %shard_map.110), calls=%async_computation.2 | async-start | bytes 786432 | tf_op jit(solution)/shard_map/all_to_all | solution.py:65
  129.8 24.0 %copy-start.9 = (bf16[1,768,64]{2,1,0:T(8,128)(2,1)S(1)}, bf16[1,768,64]{2,1,0:T(8,128)(2,1)}, u32[]{:S(2)}) copy-start(bf16[1,768,64]{2,1,0:T(8,128)(2,1)} %copy-done.8) | copy-start | bytes 294916
  129.8 24.0 %copy-start.23 = (bf16[64,216]{1,0:T(8,128)(2,1)S(1)}, bf16[64,216]{1,0:T(8,128)(2,1)}, u32[]{:S(2)}) copy-start(bf16[64,216]{1,0:T(8,128)(2,1)} %copy-done.22) | copy-start | bytes 82948
  143.8 6.7 %collective-permute-start.8 = (bf16[72,128]{1,0:T(8,128)(2,1)S(1)}, bf16[72,128]{1,0:T(8,128)(2,1)S(1)}, u32[]{:S(2)}, u32[]{:S(2)}) collective-permute-start(bf16[72,128]{1,0:T(8,128)(2,1)S(1)} %reduce_sum.18.sol_m), channel_id=1, source_target_pairs={{0,8},{8,0},{16,24},{24,16},{32,40},{40,32},{48,56},{56,48},{64,72... | collective-permute-start | bytes 55304 | tf_op jit(solution)/shard_map/ppermute | solution.py:47
  145.7 8.1 %collective-permute-start.9 = (bf16[72,128]{1,0:T(8,128)(2,1)S(1)}, bf16[72,128]{1,0:T(8,128)(2,1)S(1)}, u32[]{:S(2)}, u32[]{:S(2)}) collective-permute-start(bf16[72,128]{1,0:T(8,128)(2,1)S(1)} %reduce_sum.18.sol_m), channel_id=1, source_target_pairs={{8,16},{16,8},{24,32},{32,24},{40,48},{48,40},{56,64},{64,56},{72,... | collective-permute-start | bytes 55304 | tf_op jit(solution)/shard_map/ppermute | solution.py:48
  155.2 5.1 %collective-permute-start.10 = (bf16[576,128]{1,0:T(8,128)(2,1)S(1)}, bf16[576,128]{1,0:T(8,128)(2,1)S(1)}, u32[]{:S(2)}, u32[]{:S(2)}) collective-permute-start(bf16[576,128]{1,0:T(8,128)(2,1)S(1)} %get-tuple-element.50), channel_id=1, source_target_pairs={{0,8},{8,0},{16,24},{24,16},{32,40},{40,32},{48,56},{56,48},{64,72... | collective-permute-start | bytes 442376 | tf_op jit(solution)/shard_map/ppermute | solution.py:47
  157.1 10.2 %collective-permute-start.11 = (bf16[576,128]{1,0:T(8,128)(2,1)S(1)}, bf16[576,128]{1,0:T(8,128)(2,1)S(1)}, u32[]{:S(2)}, u32[]{:S(2)}) collective-permute-start(bf16[576,128]{1,0:T(8,128)(2,1)S(1)} %get-tuple-element.52), channel_id=1, source_target_pairs={{8,16},{16,8},{24,32},{32,24},{40,48},{48,40},{56,64},{64,56},{72,... | collective-permute-start | bytes 442376 | tf_op jit(solution)/shard_map/ppermute | solution.py:48
  184.5 4.9 %collective-permute-start.12 = (bf16[576,128]{1,0:T(8,128)(2,1)S(1)}, bf16[576,128]{1,0:T(8,128)(2,1)S(1)}, u32[]{:S(2)}, u32[]{:S(2)}) collective-permute-start(bf16[576,128]{1,0:T(8,128)(2,1)S(1)} %get-tuple-element.66.win_m), channel_id=1, source_target_pairs={{0,8},{8,0},{16,24},{24,16},{32,40},{40,32},{48,56},{56,48},{64,72... | collective-permute-start | bytes 442376 | tf_op jit(solution)/shard_map/ppermute | solution.py:47
  186.4 10.7 %collective-permute-start.13 = (bf16[576,128]{1,0:T(8,128)(2,1)S(1)}, bf16[576,128]{1,0:T(8,128)(2,1)S(1)}, u32[]{:S(2)}, u32[]{:S(2)}) collective-permute-start(bf16[576,128]{1,0:T(8,128)(2,1)S(1)} %get-tuple-element.66.win_m), channel_id=1, source_target_pairs={{8,16},{16,8},{24,32},{32,24},{40,48},{48,40},{56,64},{64,56},{72,... | collective-permute-start | bytes 442376 | tf_op jit(solution)/shard_map/ppermute | solution.py:48
  201.4 4.0 %collective-permute-start.14 = (bf16[576,128]{1,0:T(8,128)(2,1)S(1)}, bf16[576,128]{1,0:T(8,128)(2,1)S(1)}, u32[]{:S(2)}, u32[]{:S(2)}) collective-permute-start(bf16[576,128]{1,0:T(8,128)(2,1)S(1)} %get-tuple-element.55), channel_id=1, source_target_pairs={{0,8},{8,0},{16,24},{24,16},{32,40},{40,32},{48,56},{56,48},{64,72... | collective-permute-start | bytes 442376 | tf_op jit(solution)/shard_map/ppermute | solution.py:47
  203.4 10.7 %collective-permute-start.15 = (bf16[576,128]{1,0:T(8,128)(2,1)S(1)}, bf16[576,128]{1,0:T(8,128)(2,1)S(1)}, u32[]{:S(2)}, u32[]{:S(2)}) collective-permute-start(bf16[576,128]{1,0:T(8,128)(2,1)S(1)} %get-tuple-element.57), channel_id=1, source_target_pairs={{8,16},{16,8},{24,32},{32,24},{40,48},{48,40},{56,64},{64,56},{72,... | collective-permute-start | bytes 442376 | tf_op jit(solution)/shard_map/ppermute | solution.py:48
  214.6 31.0 %copy-start.1 = (bf16[768,1728]{1,0:T(8,128)(2,1)S(1)}, bf16[768,1728]{1,0:T(8,128)(2,1)}, u32[]{:S(2)}) copy-start(bf16[768,1728]{1,0:T(8,128)(2,1)} %get-tuple-element.34.g) | copy-start | bytes 7962628
  214.6 31.0 %copy-start.19 = (bf16[64,768]{1,0:T(8,128)(2,1)S(1)}, bf16[64,768]{1,0:T(8,128)(2,1)}, u32[]{:S(2)}) copy-start(bf16[64,768]{1,0:T(8,128)(2,1)} %copy-done.18) | copy-start | bytes 294916
  214.6 31.0 %copy-start.21 = (bf16[216,64]{1,0:T(8,128)(2,1)S(1)}, bf16[216,64]{1,0:T(8,128)(2,1)}, u32[]{:S(2)}) copy-start(bf16[216,64]{1,0:T(8,128)(2,1)} %copy-done.20) | copy-start | bytes 82948
  229.9 5.2 %collective-permute-start.16 = (f32[576,128]{1,0:T(8,128)S(1)}, f32[576,128]{1,0:T(8,128)S(1)}, u32[]{:S(2)}, u32[]{:S(2)}) collective-permute-start(f32[576,128]{1,0:T(8,128)S(1)} %shard_map.119.middle), channel_id=1, source_target_pairs={{0,8},{8,0},{16,24},{24,16},{32,40},{40,32},{48,56},{56,48},{64,72... | collective-permute-start | bytes 884744 | tf_op jit(solution)/shard_map/ppermute | solution.py:47
  231.8 13.8 %collective-permute-start.17 = (f32[576,128]{1,0:T(8,128)S(1)}, f32[576,128]{1,0:T(8,128)S(1)}, u32[]{:S(2)}, u32[]{:S(2)}) collective-permute-start(f32[576,128]{1,0:T(8,128)S(1)} %shard_map.119.middle), channel_id=1, source_target_pairs={{8,16},{16,8},{24,32},{32,24},{40,48},{48,40},{56,64},{64,56},{72,... | collective-permute-start | bytes 884744 | tf_op jit(solution)/shard_map/ppermute | solution.py:48
  302.1 6.7 %collective-permute-start.18 = (bf16[72,128]{1,0:T(8,128)(2,1)S(1)}, bf16[72,128]{1,0:T(8,128)(2,1)S(1)}, u32[]{:S(2)}, u32[]{:S(2)}) collective-permute-start(bf16[72,128]{1,0:T(8,128)(2,1)S(1)} %reduce_sum.19.sol_m), channel_id=1, source_target_pairs={{0,8},{8,0},{16,24},{24,16},{32,40},{40,32},{48,56},{56,48},{64,72... | collective-permute-start | bytes 55304 | tf_op jit(solution)/shard_map/ppermute | solution.py:47
  304.0 8.1 %collective-permute-start.19 = (bf16[72,128]{1,0:T(8,128)(2,1)S(1)}, bf16[72,128]{1,0:T(8,128)(2,1)S(1)}, u32[]{:S(2)}, u32[]{:S(2)}) collective-permute-start(bf16[72,128]{1,0:T(8,128)(2,1)S(1)} %reduce_sum.19.sol_m), channel_id=1, source_target_pairs={{8,16},{16,8},{24,32},{32,24},{40,48},{48,40},{56,64},{64,56},{72,... | collective-permute-start | bytes 55304 | tf_op jit(solution)/shard_map/ppermute | solution.py:48
  313.6 5.0 %collective-permute-start.20 = (bf16[576,128]{1,0:T(8,128)(2,1)S(1)}, bf16[576,128]{1,0:T(8,128)(2,1)S(1)}, u32[]{:S(2)}, u32[]{:S(2)}) collective-permute-start(bf16[576,128]{1,0:T(8,128)(2,1)S(1)} %get-tuple-element.64), channel_id=1, source_target_pairs={{0,8},{8,0},{16,24},{24,16},{32,40},{40,32},{48,56},{56,48},{64,72... | collective-permute-start | bytes 442376 | tf_op jit(solution)/shard_map/ppermute | solution.py:47
  315.5 10.2 %collective-permute-start.21 = (bf16[576,128]{1,0:T(8,128)(2,1)S(1)}, bf16[576,128]{1,0:T(8,128)(2,1)S(1)}, u32[]{:S(2)}, u32[]{:S(2)}) collective-permute-start(bf16[576,128]{1,0:T(8,128)(2,1)S(1)} %get-tuple-element.65), channel_id=1, source_target_pairs={{8,16},{16,8},{24,32},{32,24},{40,48},{48,40},{56,64},{64,56},{72,... | collective-permute-start | bytes 442376 | tf_op jit(solution)/shard_map/ppermute | solution.py:48
  325.8 7.4 %collective-permute-start.22 = (f32[192,128]{1,0:T(8,128)S(1)}, f32[192,128]{1,0:T(8,128)S(1)}, u32[]{:S(2)}, u32[]{:S(2)}) collective-permute-start(f32[192,128]{1,0:T(8,128)S(1)} %get-tuple-element.79), channel_id=1, source_target_pairs={{0,1},{1,2},{2,3},{3,4},{4,5},{5,6},{6,7},{8,9},{9,10},{10,11},{11... | collective-permute-start | bytes 294920 | tf_op jit(solution)/shard_map/ppermute | solution.py:54
  329.7 8.6 %collective-permute-start.23 = (f32[192,128]{1,0:T(8,128)S(1)}, f32[192,128]{1,0:T(8,128)S(1)}, u32[]{:S(2)}, u32[]{:S(2)}) collective-permute-start(f32[192,128]{1,0:T(8,128)S(1)} %get-tuple-element.80), channel_id=1, source_target_pairs={{1,0},{2,1},{3,2},{4,3},{5,4},{6,5},{7,6},{9,8},{10,9},{11,10},{12... | collective-permute-start | bytes 294920 | tf_op jit(solution)/shard_map/ppermute | solution.py:55
  (22 other events, 265.4 us)

commit v4 on v3

--- a/solution.py
+++ b/solution.py
@@ -9,8 +9,8 @@
 LANES = 128
 F32 = jnp.float32
 BF16 = jnp.bfloat16
-RES_A, RES_M, RES_H = BF16, F32, F32
-UPD_A, UPD_M, UPD_B = BF16, F32, F32
+RES_A, RES_M = BF16, F32
+UPD_A, UPD_M = BF16, F32
 PART = F32
 
 
@@ -37,7 +37,7 @@
     owner = wanted // per_owner
     row_step = owner // members - lax.axis_index("row") + 1
     col_step = owner % members - lax.axis_index("col") + 1
-    return row_place(row_step), col_step, wanted % per_owner
+    return row_step, col_step, wanted % per_owner
 
 
 def pair(to_far, to_near, axis):
@@ -49,10 +49,10 @@
     return from_near, from_far
 
 
-def shifts(to_next, to_previous):
-    count = lax.axis_size("col")
-    from_previous = lax.ppermute(to_next, "col", [(i, i + 1) for i in range(count - 1)])
-    from_next = lax.ppermute(to_previous, "col", [(i + 1, i) for i in range(count - 1)])
+def shifts(to_next, to_previous, axis):
+    count = lax.axis_size(axis)
+    from_previous = lax.ppermute(to_next, axis, [(i, i + 1) for i in range(count - 1)])
+    from_next = lax.ppermute(to_previous, axis, [(i + 1, i) for i in range(count - 1)])
     return from_previous, from_next
 
 
@@ -70,12 +70,12 @@
 
 
 def spread(column):
-    from_previous, from_next = pair(column, column, "row")
+    from_previous, from_next = shifts(column.astype(BF16), column.astype(BF16), "row")
     return from_previous, column, from_next
 
 
 def shared_by_columns(column, up, middle, down):
-    from_previous, from_next = pair(down, up, "row")
+    from_previous, from_next = shifts(down, up, "row")
     members = lax.axis_size("col")
     third = middle.shape[0] // 3
     summed, sent = call(
@@ -91,13 +91,13 @@
     return assembled
 
 
-def owned_sum(up, middle, down):
-    from_previous, from_next = pair(down, up, "row")
-    summed = wide(middle) + wide(from_previous) + wide(from_next)
-    third = summed.shape[0] // 3
-    left, own, right = summed[:third], summed[third : 2 * third], summed[2 * third :]
-    from_previous, from_next = shifts(right.astype(UPD_B), left.astype(UPD_B))
-    return own + wide(from_previous) + wide(from_next)
+def owned_field(across, up, middle, down):
+    from_previous, from_next = shifts(down, up, "row")
+    third = middle.shape[0] // 3
+    left, own, right = call(sum_kernel, [((third, LANES), F32)] * 3, from_previous, middle, from_next)
+    from_previous, from_next = shifts(right, left, "col")
+    (field,) = call(field_kernel, [((third, LANES), F32)], across, own, from_previous, from_next)
+    return field
 
 
 def nth(c, step, members):
@@ -117,6 +117,17 @@
     sent[nth(c, -1, members), :third, :] = own
     sent[nth(c, -1, members), third:, :] = left
     sent[nth(c, -2, members), :third, :] = left
+
+
+def sum_kernel(from_previous, middle, from_next, left, own, right):
+    third = own.shape[0]
+    total = wide(from_previous[...]) + middle[...] + wide(from_next[...])
+    left[...], own[...], right[...] = total[:third], total[third : 2 * third], total[2 * third :]
+
+
+def field_kernel(across, own, from_previous, from_next, field):
+    third = own.shape[0]
+    field[...] = across[third : 2 * third] + own[...] + from_previous[...] + from_next[...]
 
 
 def receive_kernel(column, got, summed, out):
@@ -319,11 +330,12 @@
     row_step, col_step, inside = window_positions(dof_ids[0], own)
     positions = jnp.where(active, (row_step * 3 + col_step) * own + inside, -1)
     row_step, col_step, inside = window_positions(coarse_ids[0], per_coarse)
+    row_step = row_place(row_step)
     coarse_in = (col_step * 3 + row_step) * per_coarse + inside
     coarse_out = (row_step * 3 + col_step) * per_coarse + inside
     basis = averaging_basis[0]
 
-    left, right = shifts(start, start)
+    left, right = shifts(start, start, "col")
     across = jnp.concatenate([left, start, right], axis=0)
     near = spread(across.astype(BF16))
 
@@ -372,7 +384,7 @@
         owned = shared_by_columns(column, *parts)
         step = owned.shape[0] // 3
         residual = owned[step : step + own]
-        near = spread(owned.astype(RES_H))
+        near = spread(owned)
         if weight is None:
             blocks = [n[k * step + own : (k + 1) * step] for n in near for k in range(3)]
             shared = jnp.concatenate([wide(b) for b in blocks], axis=0)
@@ -430,7 +442,7 @@
             across = across + shared_by_columns(column, *parts)
             near = spread(across.astype(BF16))
         else:
-            field = across[own : 2 * own] + owned_sum(*parts)
+            field = owned_field(across, *parts)
     return field, residual
 
 

time: 342 us -> 333 us (0.974)
  waiting for transfers between devices: 84.6 us -> 50.4 us
  starting transfers between devices: 84.6 us -> 107 us
    ppermute x4 -> x20, starting transfers between devices: 12.1 us -> 83.3 us  [the longest x10 58.4 us: shifts(): lax.ppermute(to_previous, axis, [(i + 1, i) for i in range(count - 1)])]
    ppermute x10 -> x2, waiting for transfers between devices: 60.7 us -> 5.73 us  [pair(): from_far = lax.ppermute(to_far, axis, far)]
    ppermute x10 -> x2, starting transfers between devices: 42.7 us -> 5.98 us  [pair(): from_far = lax.ppermute(to_far, axis, far)]
    ppermute x4 -> x20, waiting for transfers between devices: 7.49 us -> 28.2 us  [the longest x10 14.4 us: shifts(): lax.ppermute(to_next, axis, [(i, i + 1) for i in range(count - 1)])]
    ppermute x10 -> x2, starting transfers between devices: 19.2 us -> 3.84 us  [pair(): from_near = lax.ppermute(to_near, axis, near)]
    pallas_call x21 -> x23, Pallas kernels: 29 us -> 29.4 us  [call(): pl.pallas_call(kernel, out_shape=tuple((jax.ShapeDtypeStruct(s, d) for s,...]
  transfers between devices with their start and end apart: 25 -> 25, of which waited for: 13 -> 19; matrix products, arithmetic and copies ran while one was open for 2% -> 1% of each run, Pallas kernels for 1% -> 1%
where the time goes in v4:
time: 333 us; the launch traced here: 331 us
  blocking collectives  127 us (38%)
  starting transfers between devices  107 us (32%)
  waiting for transfers between devices  50.4 us (15%)
  Pallas kernels  29.4 us (9%)
  local copies, waits for them, and re-layouts  8.94 us (3%)
  other arithmetic  5.79 us (2%)
    ppermute x10, starting transfers between devices, shifts(): lax.ppermute(to_previous, axis, [(i + 1, i) for i in range(count - 1)])  58.4 us
    all_to_all x5, blocking collectives, from_everyone(): lax.all_to_all(copies, axis, 0, 0, axis_index_groups=groups, tiled=True)  56.7 us
    all_to_all x3, blocking collectives, shared_by_columns(): got = lax.all_to_all(sent, 'col', 0, 0, tiled=True)  46.2 us
    pallas_call x23, Pallas kernels, call(): pl.pallas_call(kernel, out_shape=tuple((jax.ShapeDtypeStruct(s, d) for s,...  29.4 us
    ppermute x10, starting transfers between devices, shifts(): lax.ppermute(to_next, axis, [(i, i + 1) for i in range(count - 1)])  24.9 us
    all_to_all x2, blocking collectives, body(): parts = lax.all_to_all(parts, 'col', 0, 0, tiled=True)  24.3 us
    all_to_all x1, waiting for transfers between devices, from_everyone(): lax.all_to_all(copies, axis, 0, 0, axis_index_groups=groups, tiled=True)  16.4 us
    ppermute x10, waiting for transfers between devices, shifts(): lax.ppermute(to_next, axis, [(i, i + 1) for i in range(count - 1)])  14.4 us
  transfers between devices with their start and end apart: 25, of which 19 were waited for; matrix products, arithmetic and copies ran while one was open for 1% of the time, Pallas kernels for 1%

profile of v4, /device:TPU:14, one launch (start us, length us, event | category | flops | bytes accessed | tf_op | source)
XLA Modules:
  0.0 331.0 jit_solution(14340653581873366636)
XLA Ops:
  0.7 4.3 %collective-permute-start = (f32[192,128]{1,0:T(8,128)}, f32[192,128]{1,0:T(8,128)S(1)}, u32[]{:S(2)}, u32[]{:S(2)}) collective-permute-start(f32[192,128]{1,0:T(8,128)} %param.13), channel_id=1, source_target_pairs={{0,1},{1,2},{2,3},{3,4},{4,5},{5,6},{6,7},{8,9},{9,10},{10,11},{11... | collective-permute-start | bytes 294920 | tf_op jit(solution)/shard_map/ppermute | solution.py:54
  11.4 2.4 collective-permute-done.1
  16.5 7.9 %collective-permute-start.3 = (bf16[576,128]{1,0:T(8,128)(2,1)S(1)}, bf16[576,128]{1,0:T(8,128)(2,1)S(1)}, u32[]{:S(2)}, u32[]{:S(2)}) collective-permute-start(bf16[576,128]{1,0:T(8,128)(2,1)S(1)} %convert_element_type.44.win_m), channel_id=1, source_target_pairs={{8,0},{16,8},{24,16},{32,24},{40,32},{48,40},{56,48},{64,56},{72,6... | collective-permute-start | bytes 442376 | tf_op jit(solution)/shard_map/ppermute | solution.py:55
  24.7 2.9 shard_map.104
  28.3 5.2 %shard_map.105 = (bf16[576,128]{1,0:T(8,128)(2,1)S(1)}, f32[576,128]{1,0:T(8,128)S(1)}, bf16[576,128]{1,0:T(8,128)(2,1)S(1)}) custom-call(bf16[576,128]{1,0:T(8,128)(2,1)S(1)} %collective-permute-done.2.win_l, bf16[576,128]{1,0:T(8,128)(2,1)S(1)} %convert_element_type.44.win_m, bf16[576,128]{1,0:T(8,128)(2,1)S(1)} %collective-permute-done.3.win_r, ...), custom_call_target="tpu_custom_call" | custom-call | tf_op jit(solution)/shard_map/pallas_call | solution.py:26
  33.6 3.0 collective-permute-start.4
  36.8 5.5 %collective-permute-start.5 = (bf16[600,128]{1,0:T(8,128)(2,1)S(1)}, bf16[600,128]{1,0:T(8,128)(2,1)S(1)}, u32[]{:S(2)}, u32[]{:S(2)}) collective-permute-start(bf16[600,128]{1,0:T(8,128)(2,1)S(1)} %get-tuple-element.87), channel_id=1, source_target_pairs={{8,0},{16,8},{24,16},{32,24},{40,32},{48,40},{56,48},{64,56},{72,6... | collective-permute-start | bytes 460808 | tf_op jit(solution)/shard_map/ppermute | solution.py:55
  46.0 17.0 %all_to_all.55.got = bf16[8,400,128]{2,1,0:T(8,128)(2,1)S(1)} all-to-all(bf16[8,400,128]{2,1,0:T(8,128)(2,1)S(1)} %get-tuple-element.43), channel_id=1, replica_groups=mesh['row'=64,'col'=8] {'col'}, dimensions={0} | all-to-all | bytes 1638400 | tf_op jit(solution)/shard_map/all_to_all | solution.py:89
  63.6 2.4 collective-permute-start.6
  66.1 6.4 %collective-permute-start.7 = (bf16[600,128]{1,0:T(8,128)(2,1)S(1)}, bf16[600,128]{1,0:T(8,128)(2,1)S(1)}, u32[]{:S(2)}, u32[]{:S(2)}) collective-permute-start(bf16[600,128]{1,0:T(8,128)(2,1)S(1)} %convert_element_type.45), channel_id=1, source_target_pairs={{8,0},{16,8},{24,16},{32,24},{40,32},{48,40},{56,48},{64,56},{72,6... | collective-permute-start | bytes 460808 | tf_op jit(solution)/shard_map/ppermute | solution.py:55
  78.7 10.1 %all_to_all.56.got = bf16[16,48,128]{2,1,0:T(8,128)(2,1)S(1)} all-to-all(bf16[16,48,128]{2,1,0:T(8,128)(2,1)S(1)} %get-tuple-element.47), channel_id=1, replica_groups={{0,1,2,3,4,5,6,7,8,9,10,11,12,13,14,15},{16,17,18,19,20,21,22,23,24,25,..., dimensions={0} | all-to-all | bytes 393216 | tf_op jit(solution)/shard_map/all_to_all | solution.py:65
  90.2 14.0 %all-to-all-start.2 = ((bf16[32,48,128]{2,1,0:T(8,128)(2,1)}), bf16[32,48,128]{2,1,0:T(8,128)(2,1)}, u32[]{:S(2)}, u32[]{:S(2)}) async-start(bf16[32,48,128]{2,1,0:T(8,128)(2,1)} %shard_map.110), calls=%async_computation.2 | async-start | bytes 786432 | tf_op jit(solution)/shard_map/all_to_all | solution.py:65
  104.7 16.4 %all-to-all-done.2 = bf16[32,48,128]{2,1,0:T(8,128)(2,1)} async-done(((bf16[32,48,128]{2,1,0:T(8,128)(2,1)}), bf16[32,48,128]{2,1,0:T(8,128)(2,1)}, u32[]{:S(2)}, u32[]{:S(2)}) %all-to-all-start.2) | async-done | bytes 393248 | tf_op jit(solution)/shard_map/all_to_all | solution.py:65
  122.2 4.4 %all_to_all.57.halves = bf16[2,32,48,128]{3,2,1,0:T(8,128)(2,1)S(1)} all-to-all(bf16[2,32,48,128]{3,2,1,0:T(8,128)(2,1)S(1)} %broadcast_in_dim.6), channel_id=1, replica_groups={{0,8},{16,24},{32,40},{48,56},{64,72},{80,88},{96,104},{112,120},{128,1..., dimensions={0} | all-to-all | bytes 1572864 | tf_op jit(solution)/shard_map/all_to_all | solution.py:65
  127.3 12.3 %all_to_all.58 = f32[8,72,128]{2,1,0:T(8,128)} all-to-all(f32[8,72,128]{2,1,0:T(8,128)S(1)} %shard_map.112), channel_id=1, replica_groups=mesh['row'=64,'col'=8] {'col'}, dimensions={0} | all-to-all | bytes 589824 | tf_op jit(solution)/shard_map/all_to_all | solution.py:425
  142.5 3.0 collective-permute-start.9
  147.3 3.3 %collective-permute-done.9.sol_d = bf16[72,128]{1,0:T(8,128)(2,1)S(1)} collective-permute-done((bf16[72,128]{1,0:T(8,128)(2,1)S(1)}, bf16[72,128]{1,0:T(8,128)(2,1)S(1)}, u32[]{:S(2)}, u32[]{:S(2)}) %collective-permute-start.9) | collective-permute-done | bytes 18464 | tf_op jit(solution)/shard_map/ppermute | solution.py:48
  154.0 6.7 %collective-permute-start.11 = (bf16[576,128]{1,0:T(8,128)(2,1)S(1)}, bf16[576,128]{1,0:T(8,128)(2,1)S(1)}, u32[]{:S(2)}, u32[]{:S(2)}) collective-permute-start(bf16[576,128]{1,0:T(8,128)(2,1)S(1)} %get-tuple-element.55), channel_id=1, source_target_pairs={{8,0},{16,8},{24,16},{32,24},{40,32},{48,40},{56,48},{64,56},{72,6... | collective-permute-start | bytes 442376 | tf_op jit(solution)/shard_map/ppermute | solution.py:55
  164.4 13.5 %all_to_all.59.got = bf16[8,384,128]{2,1,0:T(8,128)(2,1)S(1)} all-to-all(bf16[8,384,128]{2,1,0:T(8,128)(2,1)S(1)} %get-tuple-element.56), channel_id=1, replica_groups=mesh['row'=64,'col'=8] {'col'}, dimensions={0} | all-to-all | bytes 1572864 | tf_op jit(solution)/shard_map/all_to_all | solution.py:89
  181.2 6.7 %collective-permute-start.13 = (bf16[576,128]{1,0:T(8,128)(2,1)S(1)}, bf16[576,128]{1,0:T(8,128)(2,1)S(1)}, u32[]{:S(2)}, u32[]{:S(2)}) collective-permute-start(bf16[576,128]{1,0:T(8,128)(2,1)S(1)} %get-tuple-element.72.win_m), channel_id=1, source_target_pairs={{8,0},{16,8},{24,16},{32,24},{40,32},{48,40},{56,48},{64,56},{72,6... | collective-permute-start | bytes 442376 | tf_op jit(solution)/shard_map/ppermute | solution.py:55
  190.5 4.3 %shard_map.117 = (bf16[576,128]{1,0:T(8,128)(2,1)S(1)}, f32[576,128]{1,0:T(8,128)S(1)}, bf16[576,128]{1,0:T(8,128)(2,1)S(1)}) custom-call(bf16[576,128]{1,0:T(8,128)(2,1)S(1)} %collective-permute-done.12.win_l, bf16[576,128]{1,0:T(8,128)(2,1)S(1)} %get-tuple-element.72.win_m, bf16[576,128]{1,0:T(8,128)(2,1)S(1)} %collective-permute-done.13.win_r, ...), custom_call_target="tpu_custom_call" | custom-call | tf_op jit(solution)/shard_map/pallas_call | solution.py:26
  196.7 7.7 %collective-permute-start.15 = (bf16[576,128]{1,0:T(8,128)(2,1)S(1)}, bf16[576,128]{1,0:T(8,128)(2,1)S(1)}, u32[]{:S(2)}, u32[]{:S(2)}) collective-permute-start(bf16[576,128]{1,0:T(8,128)(2,1)S(1)} %get-tuple-element.60), channel_id=1, source_target_pairs={{8,0},{16,8},{24,16},{32,24},{40,32},{48,40},{56,48},{64,56},{72,6... | collective-permute-start | bytes 442376 | tf_op jit(solution)/shard_map/ppermute | solution.py:55
  207.7 15.7 %all_to_all.60.got = bf16[8,384,128]{2,1,0:T(8,128)(2,1)S(1)} all-to-all(bf16[8,384,128]{2,1,0:T(8,128)(2,1)S(1)} %get-tuple-element.61), channel_id=1, replica_groups=mesh['row'=64,'col'=8] {'col'}, dimensions={0} | all-to-all | bytes 1572864 | tf_op jit(solution)/shard_map/all_to_all | solution.py:89
  226.0 6.7 %collective-permute-start.17 = (bf16[576,128]{1,0:T(8,128)(2,1)S(1)}, bf16[576,128]{1,0:T(8,128)(2,1)S(1)}, u32[]{:S(2)}, u32[]{:S(2)}) collective-permute-start(bf16[576,128]{1,0:T(8,128)(2,1)S(1)} %convert_element_type.54), channel_id=1, source_target_pairs={{8,0},{16,8},{24,16},{32,24},{40,32},{48,40},{56,48},{64,56},{72,6... | collective-permute-start | bytes 442376 | tf_op jit(solution)/shard_map/ppermute | solution.py:55
  237.5 10.5 %all_to_all.61.got = bf16[16,48,128]{2,1,0:T(8,128)(2,1)S(1)} all-to-all(bf16[16,48,128]{2,1,0:T(8,128)(2,1)S(1)} %get-tuple-element.63), channel_id=1, replica_groups={{0,1,2,3,4,5,6,7,8,9,10,11,12,13,14,15},{16,17,18,19,20,21,22,23,24,25,..., dimensions={0} | all-to-all | bytes 393216 | tf_op jit(solution)/shard_map/all_to_all | solution.py:65
  248.6 27.2 %all_to_all.62 = bf16[32,48,128]{2,1,0:T(8,128)(2,1)S(1)} all-to-all(bf16[32,48,128]{2,1,0:T(8,128)(2,1)S(1)} %shard_map.121), channel_id=1, replica_groups={{0,16,32,48,64,80,96,112,128,144,160,176,192,208,224,240,256,272,288,30..., dimensions={0} | all-to-all | bytes 786432 | tf_op jit(solution)/shard_map/all_to_all | solution.py:65
  275.9 4.5 %all_to_all.63.halves = bf16[2,32,48,128]{3,2,1,0:T(8,128)(2,1)S(1)} all-to-all(bf16[2,32,48,128]{3,2,1,0:T(8,128)(2,1)S(1)} %broadcast_in_dim.7), channel_id=1, replica_groups={{0,8},{16,24},{32,40},{48,56},{64,72},{80,88},{96,104},{112,120},{128,1..., dimensions={0} | all-to-all | bytes 1572864 | tf_op jit(solution)/shard_map/all_to_all | solution.py:65
  281.0 12.0 %all_to_all.64 = f32[8,72,128]{2,1,0:T(8,128)} all-to-all(f32[8,72,128]{2,1,0:T(8,128)S(1)} %shard_map.122), channel_id=1, replica_groups=mesh['row'=64,'col'=8] {'col'}, dimensions={0} | all-to-all | bytes 589824 | tf_op jit(solution)/shard_map/all_to_all | solution.py:425
  295.9 3.0 collective-permute-start.19
  308.3 6.7 %collective-permute-start.21 = (bf16[576,128]{1,0:T(8,128)(2,1)S(1)}, bf16[576,128]{1,0:T(8,128)(2,1)S(1)}, u32[]{:S(2)}, u32[]{:S(2)}) collective-permute-start(bf16[576,128]{1,0:T(8,128)(2,1)S(1)} %get-tuple-element.68), channel_id=1, source_target_pairs={{8,0},{16,8},{24,16},{32,24},{40,32},{48,40},{56,48},{64,56},{72,6... | collective-permute-start | bytes 442376 | tf_op jit(solution)/shard_map/ppermute | solution.py:55
  318.2 3.5 %collective-permute-start.22 = (f32[192,128]{1,0:T(8,128)S(1)}, f32[192,128]{1,0:T(8,128)S(1)}, u32[]{:S(2)}, u32[]{:S(2)}) collective-permute-start(f32[192,128]{1,0:T(8,128)S(1)} %get-tuple-element.70), channel_id=1, source_target_pairs={{0,1},{1,2},{2,3},{3,4},{4,5},{5,6},{6,7},{8,9},{9,10},{10,11},{11... | collective-permute-start | bytes 294920 | tf_op jit(solution)/shard_map/ppermute | solution.py:54
  324.7 5.7 %collective-permute-done.23.from_next = f32[192,128]{1,0:T(8,128)S(1)} collective-permute-done((f32[192,128]{1,0:T(8,128)S(1)}, f32[192,128]{1,0:T(8,128)S(1)}, u32[]{:S(2)}, u32[]{:S(2)}) %collective-permute-start.23) | collective-permute-done | bytes 98336 | tf_op jit(solution)/shard_map/ppermute | solution.py:55
  (171 shorter events, 74.0 us)
Async XLA Ops:
  0.7 10.7 %collective-permute-start = (f32[192,128]{1,0:T(8,128)}, f32[192,128]{1,0:T(8,128)S(1)}, u32[]{:S(2)}, u32[]{:S(2)}) collective-permute-start(f32[192,128]{1,0:T(8,128)} %param.13), channel_id=1, source_target_pairs={{0,1},{1,2},{2,3},{3,4},{4,5},{5,6},{6,7},{8,9},{9,10},{10,11},{11... | collective-permute-start | bytes 294920 | tf_op jit(solution)/shard_map/ppermute | solution.py:54
  5.0 8.8 %collective-permute-start.1 = (f32[192,128]{1,0:T(8,128)}, f32[192,128]{1,0:T(8,128)S(1)}, u32[]{:S(2)}, u32[]{:S(2)}) collective-permute-start(f32[192,128]{1,0:T(8,128)} %param.13), channel_id=1, source_target_pairs={{1,0},{2,1},{3,2},{4,3},{5,4},{6,5},{7,6},{9,8},{10,9},{11,10},{12... | collective-permute-start | bytes 294920 | tf_op jit(solution)/shard_map/ppermute | solution.py:55
  14.6 13.7 %collective-permute-start.2 = (bf16[576,128]{1,0:T(8,128)(2,1)S(1)}, bf16[576,128]{1,0:T(8,128)(2,1)S(1)}, u32[]{:S(2)}, u32[]{:S(2)}) collective-permute-start(bf16[576,128]{1,0:T(8,128)(2,1)S(1)} %convert_element_type.44.win_m), channel_id=1, source_target_pairs={{0,8},{8,16},{16,24},{24,32},{32,40},{40,48},{48,56},{56,64},{64,7... | collective-permute-start | bytes 442376 | tf_op jit(solution)/shard_map/ppermute | solution.py:54
  16.5 11.8 %collective-permute-start.3 = (bf16[576,128]{1,0:T(8,128)(2,1)S(1)}, bf16[576,128]{1,0:T(8,128)(2,1)S(1)}, u32[]{:S(2)}, u32[]{:S(2)}) collective-permute-start(bf16[576,128]{1,0:T(8,128)(2,1)S(1)} %convert_element_type.44.win_m), channel_id=1, source_target_pairs={{8,0},{16,8},{24,16},{32,24},{40,32},{48,40},{56,48},{64,56},{72,6... | collective-permute-start | bytes 442376 | tf_op jit(solution)/shard_map/ppermute | solution.py:55
  28.2 48.4 %copy-start.19 = (bf16[64,768]{1,0:T(8,128)(2,1)}, bf16[64,768]{1,0:T(8,128)(2,1)S(1)}, u32[]{:S(2)}) copy-start(bf16[64,768]{1,0:T(8,128)(2,1)S(1)} %get-tuple-element.45.basis_t) | copy-start | bytes 294916
  28.2 48.4 %copy-start.21 = (bf16[216,64]{1,0:T(8,128)(2,1)}, bf16[216,64]{1,0:T(8,128)(2,1)S(1)}, u32[]{:S(2)}) copy-start(bf16[216,64]{1,0:T(8,128)(2,1)S(1)} %get-tuple-element.46.cs) | copy-start | bytes 82948
  33.6 10.9 %collective-permute-start.4 = (bf16[600,128]{1,0:T(8,128)(2,1)S(1)}, bf16[600,128]{1,0:T(8,128)(2,1)S(1)}, u32[]{:S(2)}, u32[]{:S(2)}) collective-permute-start(bf16[600,128]{1,0:T(8,128)(2,1)S(1)} %get-tuple-element.88), channel_id=1, source_target_pairs={{0,8},{8,16},{16,24},{24,32},{32,40},{40,48},{48,56},{56,64},{64,7... | collective-permute-start | bytes 460808 | tf_op jit(solution)/shard_map/ppermute | solution.py:54
  36.8 8.6 %collective-permute-start.5 = (bf16[600,128]{1,0:T(8,128)(2,1)S(1)}, bf16[600,128]{1,0:T(8,128)(2,1)S(1)}, u32[]{:S(2)}, u32[]{:S(2)}) collective-permute-start(bf16[600,128]{1,0:T(8,128)(2,1)S(1)} %get-tuple-element.87), channel_id=1, source_target_pairs={{8,0},{16,8},{24,16},{32,24},{40,32},{48,40},{56,48},{64,56},{72,6... | collective-permute-start | bytes 460808 | tf_op jit(solution)/shard_map/ppermute | solution.py:55
  63.6 11.1 %collective-permute-start.6 = (bf16[600,128]{1,0:T(8,128)(2,1)S(1)}, bf16[600,128]{1,0:T(8,128)(2,1)S(1)}, u32[]{:S(2)}, u32[]{:S(2)}) collective-permute-start(bf16[600,128]{1,0:T(8,128)(2,1)S(1)} %convert_element_type.45), channel_id=1, source_target_pairs={{0,8},{8,16},{16,24},{24,32},{32,40},{40,48},{48,56},{56,64},{64,7... | collective-permute-start | bytes 460808 | tf_op jit(solution)/shard_map/ppermute | solution.py:54
  66.1 9.4 %collective-permute-start.7 = (bf16[600,128]{1,0:T(8,128)(2,1)S(1)}, bf16[600,128]{1,0:T(8,128)(2,1)S(1)}, u32[]{:S(2)}, u32[]{:S(2)}) collective-permute-start(bf16[600,128]{1,0:T(8,128)(2,1)S(1)} %convert_element_type.45), channel_id=1, source_target_pairs={{8,0},{16,8},{24,16},{32,24},{40,32},{48,40},{56,48},{64,56},{72,6... | collective-permute-start | bytes 460808 | tf_op jit(solution)/shard_map/ppermute | solution.py:55
  90.2 30.9 %all-to-all-start.2 = ((bf16[32,48,128]{2,1,0:T(8,128)(2,1)}), bf16[32,48,128]{2,1,0:T(8,128)(2,1)}, u32[]{:S(2)}, u32[]{:S(2)}) async-start(bf16[32,48,128]{2,1,0:T(8,128)(2,1)} %shard_map.110), calls=%async_computation.2 | async-start | bytes 786432 | tf_op jit(solution)/shard_map/all_to_all | solution.py:65
  140.6 6.7 %collective-permute-start.8 = (bf16[72,128]{1,0:T(8,128)(2,1)S(1)}, bf16[72,128]{1,0:T(8,128)(2,1)S(1)}, u32[]{:S(2)}, u32[]{:S(2)}) collective-permute-start(bf16[72,128]{1,0:T(8,128)(2,1)S(1)} %reduce_sum.18.sol_m), channel_id=1, source_target_pairs={{0,8},{8,0},{16,24},{24,16},{32,40},{40,32},{48,56},{56,48},{64,72... | collective-permute-start | bytes 55304 | tf_op jit(solution)/shard_map/ppermute | solution.py:47
  142.5 8.1 %collective-permute-start.9 = (bf16[72,128]{1,0:T(8,128)(2,1)S(1)}, bf16[72,128]{1,0:T(8,128)(2,1)S(1)}, u32[]{:S(2)}, u32[]{:S(2)}) collective-permute-start(bf16[72,128]{1,0:T(8,128)(2,1)S(1)} %reduce_sum.18.sol_m), channel_id=1, source_target_pairs={{8,16},{16,8},{24,32},{32,24},{40,48},{48,40},{56,64},{64,56},{72,... | collective-permute-start | bytes 55304 | tf_op jit(solution)/shard_map/ppermute | solution.py:48
  152.0 10.2 %collective-permute-start.10 = (bf16[576,128]{1,0:T(8,128)(2,1)S(1)}, bf16[576,128]{1,0:T(8,128)(2,1)S(1)}, u32[]{:S(2)}, u32[]{:S(2)}) collective-permute-start(bf16[576,128]{1,0:T(8,128)(2,1)S(1)} %get-tuple-element.53), channel_id=1, source_target_pairs={{0,8},{8,16},{16,24},{24,32},{32,40},{40,48},{48,56},{56,64},{64,7... | collective-permute-start | bytes 442376 | tf_op jit(solution)/shard_map/ppermute | solution.py:54
  154.0 9.8 %collective-permute-start.11 = (bf16[576,128]{1,0:T(8,128)(2,1)S(1)}, bf16[576,128]{1,0:T(8,128)(2,1)S(1)}, u32[]{:S(2)}, u32[]{:S(2)}) collective-permute-start(bf16[576,128]{1,0:T(8,128)(2,1)S(1)} %get-tuple-element.55), channel_id=1, source_target_pairs={{8,0},{16,8},{24,16},{32,24},{40,32},{48,40},{56,48},{64,56},{72,6... | collective-permute-start | bytes 442376 | tf_op jit(solution)/shard_map/ppermute | solution.py:55
  179.3 10.8 %collective-permute-start.12 = (bf16[576,128]{1,0:T(8,128)(2,1)S(1)}, bf16[576,128]{1,0:T(8,128)(2,1)S(1)}, u32[]{:S(2)}, u32[]{:S(2)}) collective-permute-start(bf16[576,128]{1,0:T(8,128)(2,1)S(1)} %get-tuple-element.72.win_m), channel_id=1, source_target_pairs={{0,8},{8,16},{16,24},{24,32},{32,40},{40,48},{48,56},{56,64},{64,7... | collective-permute-start | bytes 442376 | tf_op jit(solution)/shard_map/ppermute | solution.py:54
  181.2 9.3 %collective-permute-start.13 = (bf16[576,128]{1,0:T(8,128)(2,1)S(1)}, bf16[576,128]{1,0:T(8,128)(2,1)S(1)}, u32[]{:S(2)}, u32[]{:S(2)}) collective-permute-start(bf16[576,128]{1,0:T(8,128)(2,1)S(1)} %get-tuple-element.72.win_m), channel_id=1, source_target_pairs={{8,0},{16,8},{24,16},{32,24},{40,32},{48,40},{56,48},{64,56},{72,6... | collective-permute-start | bytes 442376 | tf_op jit(solution)/shard_map/ppermute | solution.py:55
  194.8 11.9 %collective-permute-start.14 = (bf16[576,128]{1,0:T(8,128)(2,1)S(1)}, bf16[576,128]{1,0:T(8,128)(2,1)S(1)}, u32[]{:S(2)}, u32[]{:S(2)}) collective-permute-start(bf16[576,128]{1,0:T(8,128)(2,1)S(1)} %get-tuple-element.58), channel_id=1, source_target_pairs={{0,8},{8,16},{16,24},{24,32},{32,40},{40,48},{48,56},{56,64},{64,7... | collective-permute-start | bytes 442376 | tf_op jit(solution)/shard_map/ppermute | solution.py:54
  196.7 10.4 %collective-permute-start.15 = (bf16[576,128]{1,0:T(8,128)(2,1)S(1)}, bf16[576,128]{1,0:T(8,128)(2,1)S(1)}, u32[]{:S(2)}, u32[]{:S(2)}) collective-permute-start(bf16[576,128]{1,0:T(8,128)(2,1)S(1)} %get-tuple-element.60), channel_id=1, source_target_pairs={{8,0},{16,8},{24,16},{32,24},{40,32},{48,40},{56,48},{64,56},{72,6... | collective-permute-start | bytes 442376 | tf_op jit(solution)/shard_map/ppermute | solution.py:55
  207.7 27.6 %copy-start.1 = (bf16[768,1728]{1,0:T(8,128)(2,1)S(1)}, bf16[768,1728]{1,0:T(8,128)(2,1)}, u32[]{:S(2)}) copy-start(bf16[768,1728]{1,0:T(8,128)(2,1)} %get-tuple-element.37.g) | copy-start | bytes 7962628
  207.7 27.6 %copy-start.20 = (bf16[64,768]{1,0:T(8,128)(2,1)S(1)}, bf16[64,768]{1,0:T(8,128)(2,1)}, u32[]{:S(2)}) copy-start(bf16[64,768]{1,0:T(8,128)(2,1)} %copy-done.19) | copy-start | bytes 294916
  207.7 27.6 %copy-start.22 = (bf16[216,64]{1,0:T(8,128)(2,1)S(1)}, bf16[216,64]{1,0:T(8,128)(2,1)}, u32[]{:S(2)}) copy-start(bf16[216,64]{1,0:T(8,128)(2,1)} %copy-done.21) | copy-start | bytes 82948
  224.1 10.9 %collective-permute-start.16 = (bf16[576,128]{1,0:T(8,128)(2,1)S(1)}, bf16[576,128]{1,0:T(8,128)(2,1)S(1)}, u32[]{:S(2)}, u32[]{:S(2)}) collective-permute-start(bf16[576,128]{1,0:T(8,128)(2,1)S(1)} %convert_element_type.54), channel_id=1, source_target_pairs={{0,8},{8,16},{16,24},{24,32},{32,40},{40,48},{48,56},{56,64},{64,7... | collective-permute-start | bytes 442376 | tf_op jit(solution)/shard_map/ppermute | solution.py:54
  226.0 9.3 %collective-permute-start.17 = (bf16[576,128]{1,0:T(8,128)(2,1)S(1)}, bf16[576,128]{1,0:T(8,128)(2,1)S(1)}, u32[]{:S(2)}, u32[]{:S(2)}) collective-permute-start(bf16[576,128]{1,0:T(8,128)(2,1)S(1)} %convert_element_type.54), channel_id=1, source_target_pairs={{8,0},{16,8},{24,16},{32,24},{40,32},{48,40},{56,48},{64,56},{72,6... | collective-permute-start | bytes 442376 | tf_op jit(solution)/shard_map/ppermute | solution.py:55
  237.5 42.9 %copy-start.23 = (bf16[768,128]{1,0:T(8,128)(2,1)}, bf16[768,128]{1,0:T(8,128)(2,1)S(1)}, u32[]{:S(2)}) copy-start(bf16[768,128]{1,0:T(8,128)(2,1)S(1)} %get-tuple-element.65.scaled) | copy-start | bytes 589828
  294.0 7.6 %collective-permute-start.18 = (bf16[72,128]{1,0:T(8,128)(2,1)S(1)}, bf16[72,128]{1,0:T(8,128)(2,1)S(1)}, u32[]{:S(2)}, u32[]{:S(2)}) collective-permute-start(bf16[72,128]{1,0:T(8,128)(2,1)S(1)} %reduce_sum.19.sol_m), channel_id=1, source_target_pairs={{0,8},{8,0},{16,24},{24,16},{32,40},{40,32},{48,56},{56,48},{64,72... | collective-permute-start | bytes 55304 | tf_op jit(solution)/shard_map/ppermute | solution.py:47
  295.9 8.1 %collective-permute-start.19 = (bf16[72,128]{1,0:T(8,128)(2,1)S(1)}, bf16[72,128]{1,0:T(8,128)(2,1)S(1)}, u32[]{:S(2)}, u32[]{:S(2)}) collective-permute-start(bf16[72,128]{1,0:T(8,128)(2,1)S(1)} %reduce_sum.19.sol_m), channel_id=1, source_target_pairs={{8,16},{16,8},{24,32},{32,24},{40,48},{48,40},{56,64},{64,56},{72,... | collective-permute-start | bytes 55304 | tf_op jit(solution)/shard_map/ppermute | solution.py:48
  301.1 29.2 %copy-start.16 = (f32[576,128]{1,0:T(8,128)S(1)}, f32[576,128]{1,0:T(8,128)}, u32[]{:S(2)}) copy-start(f32[576,128]{1,0:T(8,128)} %get-tuple-element.73.across) | copy-start | bytes 884740
  306.4 10.2 %collective-permute-start.20 = (bf16[576,128]{1,0:T(8,128)(2,1)S(1)}, bf16[576,128]{1,0:T(8,128)(2,1)S(1)}, u32[]{:S(2)}, u32[]{:S(2)}) collective-permute-start(bf16[576,128]{1,0:T(8,128)(2,1)S(1)} %get-tuple-element.66), channel_id=1, source_target_pairs={{0,8},{8,16},{16,24},{24,32},{32,40},{40,48},{48,56},{56,64},{64,7... | collective-permute-start | bytes 442376 | tf_op jit(solution)/shard_map/ppermute | solution.py:54
  308.3 9.8 %collective-permute-start.21 = (bf16[576,128]{1,0:T(8,128)(2,1)S(1)}, bf16[576,128]{1,0:T(8,128)(2,1)S(1)}, u32[]{:S(2)}, u32[]{:S(2)}) collective-permute-start(bf16[576,128]{1,0:T(8,128)(2,1)S(1)} %get-tuple-element.68), channel_id=1, source_target_pairs={{8,0},{16,8},{24,16},{32,24},{40,32},{48,40},{56,48},{64,56},{72,6... | collective-permute-start | bytes 442376 | tf_op jit(solution)/shard_map/ppermute | solution.py:55
  318.2 6.5 %collective-permute-start.22 = (f32[192,128]{1,0:T(8,128)S(1)}, f32[192,128]{1,0:T(8,128)S(1)}, u32[]{:S(2)}, u32[]{:S(2)}) collective-permute-start(f32[192,128]{1,0:T(8,128)S(1)} %get-tuple-element.70), channel_id=1, source_target_pairs={{0,1},{1,2},{2,3},{3,4},{4,5},{5,6},{6,7},{8,9},{9,10},{10,11},{11... | collective-permute-start | bytes 294920 | tf_op jit(solution)/shard_map/ppermute | solution.py:54
  321.7 8.6 %collective-permute-start.23 = (f32[192,128]{1,0:T(8,128)S(1)}, f32[192,128]{1,0:T(8,128)S(1)}, u32[]{:S(2)}, u32[]{:S(2)}) collective-permute-start(f32[192,128]{1,0:T(8,128)S(1)} %get-tuple-element.71), channel_id=1, source_target_pairs={{1,0},{2,1},{3,2},{4,3},{5,4},{6,5},{7,6},{9,8},{10,9},{11,10},{12... | collective-permute-start | bytes 294920 | tf_op jit(solution)/shard_map/ppermute | solution.py:55
  (25 other events, 294.4 us)

commit v5 on v4

--- a/solution.py
+++ b/solution.py
@@ -40,12 +40,15 @@
     return row_step, col_step, wanted % per_owner
 
 
+def far_swaps(count):
+    return [(i, i - 1 + 2 * (i % 2)) for i in range(1, count - 1)]
+
+
 def pair(to_far, to_near, axis):
     count = lax.axis_size(axis)
     near = [(i, i ^ 1) for i in range(count)]
-    far = [(i, i - 1 + 2 * (i % 2)) for i in range(1, count - 1)]
     from_near = lax.ppermute(to_near, axis, near)
-    from_far = lax.ppermute(to_far, axis, far)
+    from_far = lax.ppermute(to_far, axis, far_swaps(count))
     return from_near, from_far
 
 
@@ -145,7 +148,7 @@
     out[2 * third :] = summed[2 * third :] + part(1, first) + part(2, first)
 
 
-def coarse_receive_kernel(place, got, kept, out):
+def coarse_receive_kernel(place, got, kept, own, far):
     members = got.shape[0] // 2
     c, k = place[0], place[1]
     block = kept.shape[0] // 2
@@ -157,8 +160,12 @@
         if step:
             total = total + jnp.where(there, wide(got[k * members + at]), 0.0)
         first = first + jnp.where(there, wide(got[(1 - k) * members + at, :block, :]), 0.0)
-    total = total + jnp.concatenate([first, jnp.zeros((block, LANES), F32)], axis=0)
-    total = total.astype(out.dtype)
+    own[...] = total[:block] + first
+    far[...] = total[block:].astype(far.dtype)
+
+
+def coarse_copies_kernel(own, from_far, out):
+    total = (own[...] + wide(from_far[...])).astype(out.dtype)
     for copy in range(out.shape[0]):
         out[copy] = total
 
@@ -274,20 +281,13 @@
 
 def coarse_kernel(halves, high, low, out, rhs):
     pairs = halves.shape[1]
-    third = halves.shape[2] // 2
+    third = halves.shape[2]
     for j in range(pairs):
-        own = wide(halves[0, j, :third, :])
-        if j > 0:
-            own = own + wide(halves[1, j - 1, third:, :])
-        rhs[2 * j * third : (2 * j + 1) * third, :] = own
-        own = wide(halves[1, j, :third, :])
-        if j + 1 < pairs:
-            own = own + wide(halves[0, j + 1, third:, :])
-        rhs[(2 * j + 1) * third : (2 * j + 2) * third, :] = own
+        for k in range(2):
+            row = 2 * j + k
+            rhs[row * third : (row + 1) * third, :] = halves[k, j]
     values = rhs[...]
-    top = values.astype(BF16)
-    rest = (values - wide(top)).astype(BF16)
-    part = dot(high[...], top) + dot(low[...], top) + dot(high[...], rest)
+    part = dot(high[...], values) + dot(low[...], values)
     part = part.astype(out.dtype)
     members = out.shape[0]
     for c in range(members):
@@ -407,9 +407,15 @@
             scalar=column,
         )
         got = from_everyone(sent, ("row", "col"), tiles)
-        (held,) = call(
-            coarse_receive_kernel, [((rows // 2, 2 * per_coarse, LANES), BF16)], got, kept, scalar=column
+        mine, far = call(
+            coarse_receive_kernel,
+            [((per_coarse, LANES), F32), ((per_coarse, LANES), BF16)],
+            got,
+            kept,
+            scalar=column,
         )
+        from_far = lax.ppermute(far, "row", far_swaps(rows))
+        (held,) = call(coarse_copies_kernel, [((rows // 2, per_coarse, LANES), BF16)], mine, from_far)
         side = from_everyone(held, "row", sides)
         both = from_everyone(jnp.broadcast_to(side[None], (2, *side.shape)), "row", chips)
         third = 3 * per_coarse
@@ -419,7 +425,7 @@
             both,
             high,
             low,
-            scratch=[((rows * per_coarse, LANES), F32)],
+            scratch=[((rows * per_coarse, LANES), BF16)],
         )
         (local_part,) = call(local_kernel, [((slots, LANES), F32)], local_inverse[0], scaled)
         parts = lax.all_to_all(parts, "col", 0, 0, tiled=True)

time: 333 us -> 335 us (level)
  starting transfers between devices: 107 us -> 119 us
  blocking collectives: 127 us -> 122 us
  waiting for transfers between devices: 50.4 us -> 46.6 us
    ppermute x2 -> x4, starting transfers between devices: 5.98 us -> 20.4 us  [the longest x2 13.6 us: body(): from_far = lax.ppermute(far, 'row', far_swaps(rows))]
    all_to_all x1, waiting for transfers between devices: 16.4 us -> 10.7 us  [from_everyone(): lax.all_to_all(copies, axis, 0, 0, axis_index_groups=groups, tiled=True)]
    all_to_all x5, blocking collectives: 56.7 us -> 52.5 us  [from_everyone(): lax.all_to_all(copies, axis, 0, 0, axis_index_groups=groups, tiled=True)]
    ppermute x2 -> x4, waiting for transfers between devices: 5.73 us -> 7.54 us  [the longest x2 4.89 us: pair(): from_far = lax.ppermute(to_far, axis, far_swaps(count))]
    pallas_call x23 -> x25, Pallas kernels: 29.4 us -> 29.1 us  [call(): pl.pallas_call(kernel, out_shape=tuple((jax.ShapeDtypeStruct(s, d) for s,...]
  transfers between devices with their start and end apart: 25 -> 27, of which waited for: 19 -> 21; matrix products, arithmetic and copies ran while one was open for 1% -> 1% of each run, Pallas kernels for 1% -> 1%
where the time goes in v5:
time: 335 us; the launch traced here: 334 us
  blocking collectives  122 us (36%)
  starting transfers between devices  119 us (36%)
  waiting for transfers between devices  46.6 us (14%)
  Pallas kernels  29.1 us (9%)
  local copies, waits for them, and re-layouts  9.23 us (3%)
  other arithmetic  5.75 us (2%)
    ppermute x10, starting transfers between devices, shifts(): lax.ppermute(to_previous, axis, [(i + 1, i) for i in range(count - 1)])  58.4 us
    all_to_all x5, blocking collectives, from_everyone(): lax.all_to_all(copies, axis, 0, 0, axis_index_groups=groups, tiled=True)  52.5 us
    all_to_all x3, blocking collectives, shared_by_columns(): got = lax.all_to_all(sent, 'col', 0, 0, tiled=True)  45.6 us
    pallas_call x25, Pallas kernels, call(): pl.pallas_call(kernel, out_shape=tuple((jax.ShapeDtypeStruct(s, d) for s,...  29.1 us
    ppermute x10, starting transfers between devices, shifts(): lax.ppermute(to_next, axis, [(i, i + 1) for i in range(count - 1)])  24.9 us
    all_to_all x2, blocking collectives, body(): parts = lax.all_to_all(parts, 'col', 0, 0, tiled=True)  23.8 us
    ppermute x10, waiting for transfers between devices, shifts(): lax.ppermute(to_next, axis, [(i, i + 1) for i in range(count - 1)])  14.3 us
    ppermute x10, waiting for transfers between devices, shifts(): lax.ppermute(to_previous, axis, [(i + 1, i) for i in range(count - 1)])  14 us
  transfers between devices with their start and end apart: 27, of which 21 were waited for; matrix products, arithmetic and copies ran while one was open for 1% of the time, Pallas kernels for 1%

profile of v5, /device:TPU:14, one launch (start us, length us, event | category | flops | bytes accessed | tf_op | source)
XLA Modules:
  0.0 333.8 jit_solution(2452418559726331523)
XLA Ops:
  0.7 4.3 %collective-permute-start = (f32[192,128]{1,0:T(8,128)}, f32[192,128]{1,0:T(8,128)S(1)}, u32[]{:S(2)}, u32[]{:S(2)}) collective-permute-start(f32[192,128]{1,0:T(8,128)} %param.13), channel_id=1, source_target_pairs={{0,1},{1,2},{2,3},{3,4},{4,5},{5,6},{6,7},{8,9},{9,10},{10,11},{11... | collective-permute-start | bytes 294920 | tf_op jit(solution)/shard_map/ppermute | solution.py:57
  16.5 7.9 %collective-permute-start.3 = (bf16[576,128]{1,0:T(8,128)(2,1)S(1)}, bf16[576,128]{1,0:T(8,128)(2,1)S(1)}, u32[]{:S(2)}, u32[]{:S(2)}) collective-permute-start(bf16[576,128]{1,0:T(8,128)(2,1)S(1)} %convert_element_type.44.win_m), channel_id=1, source_target_pairs={{8,0},{16,8},{24,16},{32,24},{40,32},{48,40},{56,48},{64,56},{72,6... | collective-permute-start | bytes 442376 | tf_op jit(solution)/shard_map/ppermute | solution.py:58
  24.7 2.9 shard_map.104
  28.3 5.2 %shard_map.105 = (bf16[576,128]{1,0:T(8,128)(2,1)S(1)}, f32[576,128]{1,0:T(8,128)S(1)}, bf16[576,128]{1,0:T(8,128)(2,1)S(1)}) custom-call(bf16[576,128]{1,0:T(8,128)(2,1)S(1)} %collective-permute-done.2.win_l, bf16[576,128]{1,0:T(8,128)(2,1)S(1)} %convert_element_type.44.win_m, bf16[576,128]{1,0:T(8,128)(2,1)S(1)} %collective-permute-done.3.win_r, ...), custom_call_target="tpu_custom_call" | custom-call | tf_op jit(solution)/shard_map/pallas_call | solution.py:26
  33.6 3.0 collective-permute-start.4
  36.8 5.5 %collective-permute-start.5 = (bf16[600,128]{1,0:T(8,128)(2,1)S(1)}, bf16[600,128]{1,0:T(8,128)(2,1)S(1)}, u32[]{:S(2)}, u32[]{:S(2)}) collective-permute-start(bf16[600,128]{1,0:T(8,128)(2,1)S(1)} %get-tuple-element.95), channel_id=1, source_target_pairs={{8,0},{16,8},{24,16},{32,24},{40,32},{48,40},{56,48},{64,56},{72,6... | collective-permute-start | bytes 460808 | tf_op jit(solution)/shard_map/ppermute | solution.py:58
  46.0 17.0 %all_to_all.55.got = bf16[8,400,128]{2,1,0:T(8,128)(2,1)S(1)} all-to-all(bf16[8,400,128]{2,1,0:T(8,128)(2,1)S(1)} %get-tuple-element.47), channel_id=1, replica_groups=mesh['row'=64,'col'=8] {'col'}, dimensions={0} | all-to-all | bytes 1638400 | tf_op jit(solution)/shard_map/all_to_all | solution.py:92
  66.1 6.4 %collective-permute-start.7 = (bf16[600,128]{1,0:T(8,128)(2,1)S(1)}, bf16[600,128]{1,0:T(8,128)(2,1)S(1)}, u32[]{:S(2)}, u32[]{:S(2)}) collective-permute-start(bf16[600,128]{1,0:T(8,128)(2,1)S(1)} %convert_element_type.45), channel_id=1, source_target_pairs={{8,0},{16,8},{24,16},{32,24},{40,32},{48,40},{56,48},{64,56},{72,6... | collective-permute-start | bytes 460808 | tf_op jit(solution)/shard_map/ppermute | solution.py:58
  78.8 10.0 %all_to_all.56.got = bf16[16,48,128]{2,1,0:T(8,128)(2,1)S(1)} all-to-all(bf16[16,48,128]{2,1,0:T(8,128)(2,1)S(1)} %get-tuple-element.51), channel_id=1, replica_groups={{0,1,2,3,4,5,6,7,8,9,10,11,12,13,14,15},{16,17,18,19,20,21,22,23,24,25,..., dimensions={0} | all-to-all | bytes 393216 | tf_op jit(solution)/shard_map/all_to_all | solution.py:68
  89.3 6.9 %collective-permute-start.8 = (bf16[24,128]{1,0:T(8,128)(2,1)S(1)}, bf16[24,128]{1,0:T(8,128)(2,1)S(1)}, u32[]{:S(2)}, u32[]{:S(2)}) collective-permute-start(bf16[24,128]{1,0:T(8,128)(2,1)S(1)} %get-tuple-element.54), channel_id=1, source_target_pairs={{8,16},{16,8},{24,32},{32,24},{40,48},{48,40},{56,64},{64,56},{72,... | collective-permute-start | bytes 18440 | tf_op jit(solution)/shard_map/ppermute | solution.py:417
  98.3 11.5 %all-to-all-start.2 = ((bf16[32,24,128]{2,1,0:T(8,128)(2,1)}), bf16[32,24,128]{2,1,0:T(8,128)(2,1)S(1)}, u32[]{:S(2)}, u32[]{:S(2)}) async-start(bf16[32,24,128]{2,1,0:T(8,128)(2,1)} %shard_map.111), calls=%async_computation.2 | async-start | bytes 393216 | tf_op jit(solution)/shard_map/all_to_all | solution.py:68
  111.7 10.7 %all-to-all-done.2 = bf16[32,24,128]{2,1,0:T(8,128)(2,1)S(1)} async-done(((bf16[32,24,128]{2,1,0:T(8,128)(2,1)}), bf16[32,24,128]{2,1,0:T(8,128)(2,1)S(1)}, u32[]{:S(2)}, u32[]{:S(2)}) %all-to-all-start.2) | async-done | bytes 196640 | tf_op jit(solution)/shard_map/all_to_all | solution.py:68
  122.5 5.5 %all_to_all.57.halves = bf16[2,32,24,128]{3,2,1,0:T(8,128)(2,1)S(1)} all-to-all(bf16[2,32,24,128]{3,2,1,0:T(8,128)(2,1)S(1)} %broadcast_in_dim.6), channel_id=1, replica_groups={{0,8},{16,24},{32,40},{48,56},{64,72},{80,88},{96,104},{112,120},{128,1..., dimensions={0} | all-to-all | bytes 786432 | tf_op jit(solution)/shard_map/all_to_all | solution.py:68
  128.5 12.1 %all_to_all.58 = f32[8,72,128]{2,1,0:T(8,128)} all-to-all(f32[8,72,128]{2,1,0:T(8,128)S(1)} %shard_map.113), channel_id=1, replica_groups=mesh['row'=64,'col'=8] {'col'}, dimensions={0} | all-to-all | bytes 589824 | tf_op jit(solution)/shard_map/all_to_all | solution.py:431
  143.5 3.4 %collective-permute-start.10 = (bf16[72,128]{1,0:T(8,128)(2,1)S(1)}, bf16[72,128]{1,0:T(8,128)(2,1)S(1)}, u32[]{:S(2)}, u32[]{:S(2)}) collective-permute-start(bf16[72,128]{1,0:T(8,128)(2,1)S(1)} %reduce_sum.18.sol_m), channel_id=1, source_target_pairs={{8,16},{16,8},{24,32},{32,24},{40,48},{48,40},{56,64},{64,56},{72,... | collective-permute-start | bytes 55304 | tf_op jit(solution)/shard_map/ppermute | solution.py:51
  148.6 2.9 collective-permute-done.10.sol_d
  154.9 6.7 %collective-permute-start.12 = (bf16[576,128]{1,0:T(8,128)(2,1)S(1)}, bf16[576,128]{1,0:T(8,128)(2,1)S(1)}, u32[]{:S(2)}, u32[]{:S(2)}) collective-permute-start(bf16[576,128]{1,0:T(8,128)(2,1)S(1)} %get-tuple-element.61), channel_id=1, source_target_pairs={{8,0},{16,8},{24,16},{32,24},{40,32},{48,40},{56,48},{64,56},{72,6... | collective-permute-start | bytes 442376 | tf_op jit(solution)/shard_map/ppermute | solution.py:58
  165.3 13.4 %all_to_all.59.got = bf16[8,384,128]{2,1,0:T(8,128)(2,1)S(1)} all-to-all(bf16[8,384,128]{2,1,0:T(8,128)(2,1)S(1)} %get-tuple-element.62), channel_id=1, replica_groups=mesh['row'=64,'col'=8] {'col'}, dimensions={0} | all-to-all | bytes 1572864 | tf_op jit(solution)/shard_map/all_to_all | solution.py:92
  182.0 6.7 %collective-permute-start.14 = (bf16[576,128]{1,0:T(8,128)(2,1)S(1)}, bf16[576,128]{1,0:T(8,128)(2,1)S(1)}, u32[]{:S(2)}, u32[]{:S(2)}) collective-permute-start(bf16[576,128]{1,0:T(8,128)(2,1)S(1)} %get-tuple-element.80.win_m), channel_id=1, source_target_pairs={{8,0},{16,8},{24,16},{32,24},{40,32},{48,40},{56,48},{64,56},{72,6... | collective-permute-start | bytes 442376 | tf_op jit(solution)/shard_map/ppermute | solution.py:58
  191.4 4.3 %shard_map.118 = (bf16[576,128]{1,0:T(8,128)(2,1)S(1)}, f32[576,128]{1,0:T(8,128)S(1)}, bf16[576,128]{1,0:T(8,128)(2,1)S(1)}) custom-call(bf16[576,128]{1,0:T(8,128)(2,1)S(1)} %collective-permute-done.13.win_l, bf16[576,128]{1,0:T(8,128)(2,1)S(1)} %get-tuple-element.80.win_m, bf16[576,128]{1,0:T(8,128)(2,1)S(1)} %collective-permute-done.14.win_r, ...), custom_call_target="tpu_custom_call" | custom-call | tf_op jit(solution)/shard_map/pallas_call | solution.py:26
  197.6 7.7 %collective-permute-start.16 = (bf16[576,128]{1,0:T(8,128)(2,1)S(1)}, bf16[576,128]{1,0:T(8,128)(2,1)S(1)}, u32[]{:S(2)}, u32[]{:S(2)}) collective-permute-start(bf16[576,128]{1,0:T(8,128)(2,1)S(1)} %get-tuple-element.66), channel_id=1, source_target_pairs={{8,0},{16,8},{24,16},{32,24},{40,32},{48,40},{56,48},{64,56},{72,6... | collective-permute-start | bytes 442376 | tf_op jit(solution)/shard_map/ppermute | solution.py:58
  208.6 15.2 %all_to_all.60.got = bf16[8,384,128]{2,1,0:T(8,128)(2,1)S(1)} all-to-all(bf16[8,384,128]{2,1,0:T(8,128)(2,1)S(1)} %get-tuple-element.67), channel_id=1, replica_groups=mesh['row'=64,'col'=8] {'col'}, dimensions={0} | all-to-all | bytes 1572864 | tf_op jit(solution)/shard_map/all_to_all | solution.py:92
  226.4 6.7 %collective-permute-start.18 = (bf16[576,128]{1,0:T(8,128)(2,1)S(1)}, bf16[576,128]{1,0:T(8,128)(2,1)S(1)}, u32[]{:S(2)}, u32[]{:S(2)}) collective-permute-start(bf16[576,128]{1,0:T(8,128)(2,1)S(1)} %convert_element_type.54), channel_id=1, source_target_pairs={{8,0},{16,8},{24,16},{32,24},{40,32},{48,40},{56,48},{64,56},{72,6... | collective-permute-start | bytes 442376 | tf_op jit(solution)/shard_map/ppermute | solution.py:58
  237.8 10.7 %all_to_all.61.got = bf16[16,48,128]{2,1,0:T(8,128)(2,1)S(1)} all-to-all(bf16[16,48,128]{2,1,0:T(8,128)(2,1)S(1)} %get-tuple-element.69), channel_id=1, replica_groups={{0,1,2,3,4,5,6,7,8,9,10,11,12,13,14,15},{16,17,18,19,20,21,22,23,24,25,..., dimensions={0} | all-to-all | bytes 393216 | tf_op jit(solution)/shard_map/all_to_all | solution.py:68
  249.1 6.6 %collective-permute-start.19 = (bf16[24,128]{1,0:T(8,128)(2,1)S(1)}, bf16[24,128]{1,0:T(8,128)(2,1)S(1)}, u32[]{:S(2)}, u32[]{:S(2)}) collective-permute-start(bf16[24,128]{1,0:T(8,128)(2,1)S(1)} %get-tuple-element.72), channel_id=1, source_target_pairs={{8,16},{16,8},{24,32},{32,24},{40,48},{48,40},{56,64},{64,56},{72,... | collective-permute-start | bytes 18440 | tf_op jit(solution)/shard_map/ppermute | solution.py:417
  257.1 21.0 %all_to_all.62 = bf16[32,24,128]{2,1,0:T(8,128)(2,1)S(1)} all-to-all(bf16[32,24,128]{2,1,0:T(8,128)(2,1)S(1)} %shard_map.123), channel_id=1, replica_groups={{0,16,32,48,64,80,96,112,128,144,160,176,192,208,224,240,256,272,288,30..., dimensions={0} | all-to-all | bytes 393216 | tf_op jit(solution)/shard_map/all_to_all | solution.py:68
  278.1 5.5 %all_to_all.63.halves = bf16[2,32,24,128]{3,2,1,0:T(8,128)(2,1)S(1)} all-to-all(bf16[2,32,24,128]{3,2,1,0:T(8,128)(2,1)S(1)} %broadcast_in_dim.7), channel_id=1, replica_groups={{0,8},{16,24},{32,40},{48,56},{64,72},{80,88},{96,104},{112,120},{128,1..., dimensions={0} | all-to-all | bytes 786432 | tf_op jit(solution)/shard_map/all_to_all | solution.py:68
  284.1 11.7 %all_to_all.64 = f32[8,72,128]{2,1,0:T(8,128)} all-to-all(f32[8,72,128]{2,1,0:T(8,128)S(1)} %shard_map.124), channel_id=1, replica_groups=mesh['row'=64,'col'=8] {'col'}, dimensions={0} | all-to-all | bytes 589824 | tf_op jit(solution)/shard_map/all_to_all | solution.py:431
  298.7 3.4 %collective-permute-start.21 = (bf16[72,128]{1,0:T(8,128)(2,1)S(1)}, bf16[72,128]{1,0:T(8,128)(2,1)S(1)}, u32[]{:S(2)}, u32[]{:S(2)}) collective-permute-start(bf16[72,128]{1,0:T(8,128)(2,1)S(1)} %reduce_sum.19.sol_m), channel_id=1, source_target_pairs={{8,16},{16,8},{24,32},{32,24},{40,48},{48,40},{56,64},{64,56},{72,... | collective-permute-start | bytes 55304 | tf_op jit(solution)/shard_map/ppermute | solution.py:51
  311.1 6.7 %collective-permute-start.23 = (bf16[576,128]{1,0:T(8,128)(2,1)S(1)}, bf16[576,128]{1,0:T(8,128)(2,1)S(1)}, u32[]{:S(2)}, u32[]{:S(2)}) collective-permute-start(bf16[576,128]{1,0:T(8,128)(2,1)S(1)} %get-tuple-element.76), channel_id=1, source_target_pairs={{8,0},{16,8},{24,16},{32,24},{40,32},{48,40},{56,48},{64,56},{72,6... | collective-permute-start | bytes 442376 | tf_op jit(solution)/shard_map/ppermute | solution.py:58
  320.9 3.5 %collective-permute-start.24 = (f32[192,128]{1,0:T(8,128)S(1)}, f32[192,128]{1,0:T(8,128)S(1)}, u32[]{:S(2)}, u32[]{:S(2)}) collective-permute-start(f32[192,128]{1,0:T(8,128)S(1)} %get-tuple-element.78), channel_id=1, source_target_pairs={{0,1},{1,2},{2,3},{3,4},{4,5},{5,6},{6,7},{8,9},{9,10},{10,11},{11... | collective-permute-start | bytes 294920 | tf_op jit(solution)/shard_map/ppermute | solution.py:57
  327.4 5.7 %collective-permute-done.25.from_next = f32[192,128]{1,0:T(8,128)S(1)} collective-permute-done((f32[192,128]{1,0:T(8,128)S(1)}, f32[192,128]{1,0:T(8,128)S(1)}, u32[]{:S(2)}, u32[]{:S(2)}) %collective-permute-start.25) | collective-permute-done | bytes 98336 | tf_op jit(solution)/shard_map/ppermute | solution.py:58
  (177 shorter events, 80.9 us)
Async XLA Ops:
  0.7 10.7 %collective-permute-start = (f32[192,128]{1,0:T(8,128)}, f32[192,128]{1,0:T(8,128)S(1)}, u32[]{:S(2)}, u32[]{:S(2)}) collective-permute-start(f32[192,128]{1,0:T(8,128)} %param.13), channel_id=1, source_target_pairs={{0,1},{1,2},{2,3},{3,4},{4,5},{5,6},{6,7},{8,9},{9,10},{10,11},{11... | collective-permute-start | bytes 294920 | tf_op jit(solution)/shard_map/ppermute | solution.py:57
  5.0 8.8 %collective-permute-start.1 = (f32[192,128]{1,0:T(8,128)}, f32[192,128]{1,0:T(8,128)S(1)}, u32[]{:S(2)}, u32[]{:S(2)}) collective-permute-start(f32[192,128]{1,0:T(8,128)} %param.13), channel_id=1, source_target_pairs={{1,0},{2,1},{3,2},{4,3},{5,4},{6,5},{7,6},{9,8},{10,9},{11,10},{12... | collective-permute-start | bytes 294920 | tf_op jit(solution)/shard_map/ppermute | solution.py:58
  14.6 13.7 %collective-permute-start.2 = (bf16[576,128]{1,0:T(8,128)(2,1)S(1)}, bf16[576,128]{1,0:T(8,128)(2,1)S(1)}, u32[]{:S(2)}, u32[]{:S(2)}) collective-permute-start(bf16[576,128]{1,0:T(8,128)(2,1)S(1)} %convert_element_type.44.win_m), channel_id=1, source_target_pairs={{0,8},{8,16},{16,24},{24,32},{32,40},{40,48},{48,56},{56,64},{64,7... | collective-permute-start | bytes 442376 | tf_op jit(solution)/shard_map/ppermute | solution.py:57
  16.5 11.8 %collective-permute-start.3 = (bf16[576,128]{1,0:T(8,128)(2,1)S(1)}, bf16[576,128]{1,0:T(8,128)(2,1)S(1)}, u32[]{:S(2)}, u32[]{:S(2)}) collective-permute-start(bf16[576,128]{1,0:T(8,128)(2,1)S(1)} %convert_element_type.44.win_m), channel_id=1, source_target_pairs={{8,0},{16,8},{24,16},{32,24},{40,32},{48,40},{56,48},{64,56},{72,6... | collective-permute-start | bytes 442376 | tf_op jit(solution)/shard_map/ppermute | solution.py:58
  28.2 48.4 %copy-start.19 = (bf16[64,768]{1,0:T(8,128)(2,1)}, bf16[64,768]{1,0:T(8,128)(2,1)S(1)}, u32[]{:S(2)}) copy-start(bf16[64,768]{1,0:T(8,128)(2,1)S(1)} %get-tuple-element.49.basis_t) | copy-start | bytes 294916
  28.2 48.4 %copy-start.21 = (bf16[216,64]{1,0:T(8,128)(2,1)}, bf16[216,64]{1,0:T(8,128)(2,1)S(1)}, u32[]{:S(2)}) copy-start(bf16[216,64]{1,0:T(8,128)(2,1)S(1)} %get-tuple-element.50.cs) | copy-start | bytes 82948
  33.6 10.9 %collective-permute-start.4 = (bf16[600,128]{1,0:T(8,128)(2,1)S(1)}, bf16[600,128]{1,0:T(8,128)(2,1)S(1)}, u32[]{:S(2)}, u32[]{:S(2)}) collective-permute-start(bf16[600,128]{1,0:T(8,128)(2,1)S(1)} %get-tuple-element.96), channel_id=1, source_target_pairs={{0,8},{8,16},{16,24},{24,32},{32,40},{40,48},{48,56},{56,64},{64,7... | collective-permute-start | bytes 460808 | tf_op jit(solution)/shard_map/ppermute | solution.py:57
  36.8 8.6 %collective-permute-start.5 = (bf16[600,128]{1,0:T(8,128)(2,1)S(1)}, bf16[600,128]{1,0:T(8,128)(2,1)S(1)}, u32[]{:S(2)}, u32[]{:S(2)}) collective-permute-start(bf16[600,128]{1,0:T(8,128)(2,1)S(1)} %get-tuple-element.95), channel_id=1, source_target_pairs={{8,0},{16,8},{24,16},{32,24},{40,32},{48,40},{56,48},{64,56},{72,6... | collective-permute-start | bytes 460808 | tf_op jit(solution)/shard_map/ppermute | solution.py:58
  63.6 11.1 %collective-permute-start.6 = (bf16[600,128]{1,0:T(8,128)(2,1)S(1)}, bf16[600,128]{1,0:T(8,128)(2,1)S(1)}, u32[]{:S(2)}, u32[]{:S(2)}) collective-permute-start(bf16[600,128]{1,0:T(8,128)(2,1)S(1)} %convert_element_type.45), channel_id=1, source_target_pairs={{0,8},{8,16},{16,24},{24,32},{32,40},{40,48},{48,56},{56,64},{64,7... | collective-permute-start | bytes 460808 | tf_op jit(solution)/shard_map/ppermute | solution.py:57
  66.1 9.4 %collective-permute-start.7 = (bf16[600,128]{1,0:T(8,128)(2,1)S(1)}, bf16[600,128]{1,0:T(8,128)(2,1)S(1)}, u32[]{:S(2)}, u32[]{:S(2)}) collective-permute-start(bf16[600,128]{1,0:T(8,128)(2,1)S(1)} %convert_element_type.45), channel_id=1, source_target_pairs={{8,0},{16,8},{24,16},{32,24},{40,32},{48,40},{56,48},{64,56},{72,6... | collective-permute-start | bytes 460808 | tf_op jit(solution)/shard_map/ppermute | solution.py:58
  89.3 8.2 %collective-permute-start.8 = (bf16[24,128]{1,0:T(8,128)(2,1)S(1)}, bf16[24,128]{1,0:T(8,128)(2,1)S(1)}, u32[]{:S(2)}, u32[]{:S(2)}) collective-permute-start(bf16[24,128]{1,0:T(8,128)(2,1)S(1)} %get-tuple-element.54), channel_id=1, source_target_pairs={{8,16},{16,8},{24,32},{32,24},{40,48},{48,40},{56,64},{64,56},{72,... | collective-permute-start | bytes 18440 | tf_op jit(solution)/shard_map/ppermute | solution.py:417
  98.3 24.2 %all-to-all-start.2 = ((bf16[32,24,128]{2,1,0:T(8,128)(2,1)}), bf16[32,24,128]{2,1,0:T(8,128)(2,1)S(1)}, u32[]{:S(2)}, u32[]{:S(2)}) async-start(bf16[32,24,128]{2,1,0:T(8,128)(2,1)} %shard_map.111), calls=%async_computation.2 | async-start | bytes 393216 | tf_op jit(solution)/shard_map/all_to_all | solution.py:68
  141.5 7.1 %collective-permute-start.9 = (bf16[72,128]{1,0:T(8,128)(2,1)S(1)}, bf16[72,128]{1,0:T(8,128)(2,1)S(1)}, u32[]{:S(2)}, u32[]{:S(2)}) collective-permute-start(bf16[72,128]{1,0:T(8,128)(2,1)S(1)} %reduce_sum.18.sol_m), channel_id=1, source_target_pairs={{0,8},{8,0},{16,24},{24,16},{32,40},{40,32},{48,56},{56,48},{64,72... | collective-permute-start | bytes 55304 | tf_op jit(solution)/shard_map/ppermute | solution.py:50
  143.5 8.1 %collective-permute-start.10 = (bf16[72,128]{1,0:T(8,128)(2,1)S(1)}, bf16[72,128]{1,0:T(8,128)(2,1)S(1)}, u32[]{:S(2)}, u32[]{:S(2)}) collective-permute-start(bf16[72,128]{1,0:T(8,128)(2,1)S(1)} %reduce_sum.18.sol_m), channel_id=1, source_target_pairs={{8,16},{16,8},{24,32},{32,24},{40,48},{48,40},{56,64},{64,56},{72,... | collective-permute-start | bytes 55304 | tf_op jit(solution)/shard_map/ppermute | solution.py:51
  153.0 10.2 %collective-permute-start.11 = (bf16[576,128]{1,0:T(8,128)(2,1)S(1)}, bf16[576,128]{1,0:T(8,128)(2,1)S(1)}, u32[]{:S(2)}, u32[]{:S(2)}) collective-permute-start(bf16[576,128]{1,0:T(8,128)(2,1)S(1)} %get-tuple-element.59), channel_id=1, source_target_pairs={{0,8},{8,16},{16,24},{24,32},{32,40},{40,48},{48,56},{56,64},{64,7... | collective-permute-start | bytes 442376 | tf_op jit(solution)/shard_map/ppermute | solution.py:57
  154.9 9.8 %collective-permute-start.12 = (bf16[576,128]{1,0:T(8,128)(2,1)S(1)}, bf16[576,128]{1,0:T(8,128)(2,1)S(1)}, u32[]{:S(2)}, u32[]{:S(2)}) collective-permute-start(bf16[576,128]{1,0:T(8,128)(2,1)S(1)} %get-tuple-element.61), channel_id=1, source_target_pairs={{8,0},{16,8},{24,16},{32,24},{40,32},{48,40},{56,48},{64,56},{72,6... | collective-permute-start | bytes 442376 | tf_op jit(solution)/shard_map/ppermute | solution.py:58
  180.1 10.8 %collective-permute-start.13 = (bf16[576,128]{1,0:T(8,128)(2,1)S(1)}, bf16[576,128]{1,0:T(8,128)(2,1)S(1)}, u32[]{:S(2)}, u32[]{:S(2)}) collective-permute-start(bf16[576,128]{1,0:T(8,128)(2,1)S(1)} %get-tuple-element.80.win_m), channel_id=1, source_target_pairs={{0,8},{8,16},{16,24},{24,32},{32,40},{40,48},{48,56},{56,64},{64,7... | collective-permute-start | bytes 442376 | tf_op jit(solution)/shard_map/ppermute | solution.py:57
  182.0 9.3 %collective-permute-start.14 = (bf16[576,128]{1,0:T(8,128)(2,1)S(1)}, bf16[576,128]{1,0:T(8,128)(2,1)S(1)}, u32[]{:S(2)}, u32[]{:S(2)}) collective-permute-start(bf16[576,128]{1,0:T(8,128)(2,1)S(1)} %get-tuple-element.80.win_m), channel_id=1, source_target_pairs={{8,0},{16,8},{24,16},{32,24},{40,32},{48,40},{56,48},{64,56},{72,6... | collective-permute-start | bytes 442376 | tf_op jit(solution)/shard_map/ppermute | solution.py:58
  195.6 11.9 %collective-permute-start.15 = (bf16[576,128]{1,0:T(8,128)(2,1)S(1)}, bf16[576,128]{1,0:T(8,128)(2,1)S(1)}, u32[]{:S(2)}, u32[]{:S(2)}) collective-permute-start(bf16[576,128]{1,0:T(8,128)(2,1)S(1)} %get-tuple-element.64), channel_id=1, source_target_pairs={{0,8},{8,16},{16,24},{24,32},{32,40},{40,48},{48,56},{56,64},{64,7... | collective-permute-start | bytes 442376 | tf_op jit(solution)/shard_map/ppermute | solution.py:57
  197.6 10.4 %collective-permute-start.16 = (bf16[576,128]{1,0:T(8,128)(2,1)S(1)}, bf16[576,128]{1,0:T(8,128)(2,1)S(1)}, u32[]{:S(2)}, u32[]{:S(2)}) collective-permute-start(bf16[576,128]{1,0:T(8,128)(2,1)S(1)} %get-tuple-element.66), channel_id=1, source_target_pairs={{8,0},{16,8},{24,16},{32,24},{40,32},{48,40},{56,48},{64,56},{72,6... | collective-permute-start | bytes 442376 | tf_op jit(solution)/shard_map/ppermute | solution.py:58
  224.4 10.8 %collective-permute-start.17 = (bf16[576,128]{1,0:T(8,128)(2,1)S(1)}, bf16[576,128]{1,0:T(8,128)(2,1)S(1)}, u32[]{:S(2)}, u32[]{:S(2)}) collective-permute-start(bf16[576,128]{1,0:T(8,128)(2,1)S(1)} %convert_element_type.54), channel_id=1, source_target_pairs={{0,8},{8,16},{16,24},{24,32},{32,40},{40,48},{48,56},{56,64},{64,7... | collective-permute-start | bytes 442376 | tf_op jit(solution)/shard_map/ppermute | solution.py:57
  226.4 9.3 %collective-permute-start.18 = (bf16[576,128]{1,0:T(8,128)(2,1)S(1)}, bf16[576,128]{1,0:T(8,128)(2,1)S(1)}, u32[]{:S(2)}, u32[]{:S(2)}) collective-permute-start(bf16[576,128]{1,0:T(8,128)(2,1)S(1)} %convert_element_type.54), channel_id=1, source_target_pairs={{8,0},{16,8},{24,16},{32,24},{40,32},{48,40},{56,48},{64,56},{72,6... | collective-permute-start | bytes 442376 | tf_op jit(solution)/shard_map/ppermute | solution.py:58
  237.8 46.2 %copy-start.23 = (bf16[768,128]{1,0:T(8,128)(2,1)}, bf16[768,128]{1,0:T(8,128)(2,1)S(1)}, u32[]{:S(2)}) copy-start(bf16[768,128]{1,0:T(8,128)(2,1)S(1)} %get-tuple-element.73.scaled) | copy-start | bytes 589828
  237.8 45.7 %copy-start.12 = (bf16[192,1536]{1,0:T(8,128)(2,1)S(1)}, bf16[192,1536]{1,0:T(8,128)(2,1)}, u32[]{:S(2)}) copy-start(bf16[192,1536]{1,0:T(8,128)(2,1)} %copy-done.11) | copy-start | bytes 1769476
  237.8 45.7 %copy-start.14 = (bf16[192,1536]{1,0:T(8,128)(2,1)S(1)}, bf16[192,1536]{1,0:T(8,128)(2,1)}, u32[]{:S(2)}) copy-start(bf16[192,1536]{1,0:T(8,128)(2,1)} %copy-done.13) | copy-start | bytes 1769476
  249.1 8.0 %collective-permute-start.19 = (bf16[24,128]{1,0:T(8,128)(2,1)S(1)}, bf16[24,128]{1,0:T(8,128)(2,1)S(1)}, u32[]{:S(2)}, u32[]{:S(2)}) collective-permute-start(bf16[24,128]{1,0:T(8,128)(2,1)S(1)} %get-tuple-element.72), channel_id=1, source_target_pairs={{8,16},{16,8},{24,32},{32,24},{40,48},{48,40},{56,64},{64,56},{72,... | collective-permute-start | bytes 18440 | tf_op jit(solution)/shard_map/ppermute | solution.py:417
  296.8 8.0 %collective-permute-start.20 = (bf16[72,128]{1,0:T(8,128)(2,1)S(1)}, bf16[72,128]{1,0:T(8,128)(2,1)S(1)}, u32[]{:S(2)}, u32[]{:S(2)}) collective-permute-start(bf16[72,128]{1,0:T(8,128)(2,1)S(1)} %reduce_sum.19.sol_m), channel_id=1, source_target_pairs={{0,8},{8,0},{16,24},{24,16},{32,40},{40,32},{48,56},{56,48},{64,72... | collective-permute-start | bytes 55304 | tf_op jit(solution)/shard_map/ppermute | solution.py:50
  298.7 8.1 %collective-permute-start.21 = (bf16[72,128]{1,0:T(8,128)(2,1)S(1)}, bf16[72,128]{1,0:T(8,128)(2,1)S(1)}, u32[]{:S(2)}, u32[]{:S(2)}) collective-permute-start(bf16[72,128]{1,0:T(8,128)(2,1)S(1)} %reduce_sum.19.sol_m), channel_id=1, source_target_pairs={{8,16},{16,8},{24,32},{32,24},{40,48},{48,40},{56,64},{64,56},{72,... | collective-permute-start | bytes 55304 | tf_op jit(solution)/shard_map/ppermute | solution.py:51
  309.2 10.2 %collective-permute-start.22 = (bf16[576,128]{1,0:T(8,128)(2,1)S(1)}, bf16[576,128]{1,0:T(8,128)(2,1)S(1)}, u32[]{:S(2)}, u32[]{:S(2)}) collective-permute-start(bf16[576,128]{1,0:T(8,128)(2,1)S(1)} %get-tuple-element.74), channel_id=1, source_target_pairs={{0,8},{8,16},{16,24},{24,32},{32,40},{40,48},{48,56},{56,64},{64,7... | collective-permute-start | bytes 442376 | tf_op jit(solution)/shard_map/ppermute | solution.py:57
  311.1 9.8 %collective-permute-start.23 = (bf16[576,128]{1,0:T(8,128)(2,1)S(1)}, bf16[576,128]{1,0:T(8,128)(2,1)S(1)}, u32[]{:S(2)}, u32[]{:S(2)}) collective-permute-start(bf16[576,128]{1,0:T(8,128)(2,1)S(1)} %get-tuple-element.76), channel_id=1, source_target_pairs={{8,0},{16,8},{24,16},{32,24},{40,32},{48,40},{56,48},{64,56},{72,6... | collective-permute-start | bytes 442376 | tf_op jit(solution)/shard_map/ppermute | solution.py:58
  320.9 6.5 %collective-permute-start.24 = (f32[192,128]{1,0:T(8,128)S(1)}, f32[192,128]{1,0:T(8,128)S(1)}, u32[]{:S(2)}, u32[]{:S(2)}) collective-permute-start(f32[192,128]{1,0:T(8,128)S(1)} %get-tuple-element.78), channel_id=1, source_target_pairs={{0,1},{1,2},{2,3},{3,4},{4,5},{5,6},{6,7},{8,9},{9,10},{10,11},{11... | collective-permute-start | bytes 294920 | tf_op jit(solution)/shard_map/ppermute | solution.py:57
  324.5 8.6 %collective-permute-start.25 = (f32[192,128]{1,0:T(8,128)S(1)}, f32[192,128]{1,0:T(8,128)S(1)}, u32[]{:S(2)}, u32[]{:S(2)}) collective-permute-start(f32[192,128]{1,0:T(8,128)S(1)} %get-tuple-element.79), channel_id=1, source_target_pairs={{1,0},{2,1},{3,2},{4,3},{5,4},{6,5},{7,6},{9,8},{10,9},{11,10},{12... | collective-permute-start | bytes 294920 | tf_op jit(solution)/shard_map/ppermute | solution.py:58
  (27 other events, 358.8 us)
